TPU v7x, 128 devices: a whole 4x4x4 slice. The times are simulated.
128 devices in a mesh: mp: 2 (over core), dp: 64 (over z, y, x).
Axes of the slice: x: 4, y: 4, z: 4, core: 2. Of those that a mesh axis runs over, the one named last changes fastest.
Arguments:
- a: bfloat16 [131072, 768], P('dp')
- g: bfloat16 [131072, 2304], P('dp')
- w: float32 [2304, 6, 128], P(None, 'mp')
- a_old: float32 [768, 6, 128], P(None, 'mp')
- s_old: float32 [2304, 18, 128], P(None, 'mp')
Outputs:
- output 1: float32 [2304, 6, 128], P(None, 'mp')
- output 2: float32 [768, 6, 128], P(None, 'mp')
- output 3: float32 [2304, 18, 128], P(None, 'mp')
All inputs are finite; a program needn't handle non-finite values.
Results may differ from a plain program's by a relative error of at most 0.001.
Values sent between devices are 32-bit elements.
A program may use at most 1 GiB of HBM per device.

v0:
```python
import math
import jax
import jax.numpy as jnp
from jax import lax
from jax.sharding import PartitionSpec as P

FACTOR_DECAY = 0.95
DAMPING = 0.001
DAMP_SHIFT = math.sqrt(DAMPING)
LEARN_RATE = 1.0
PREC_HIGH = lax.Precision.HIGHEST


def own_columns(matrix, my_rank, n_mp, blk_width):
    n_rows = matrix.shape[0]
    n_local = matrix.shape[1] // (n_mp * blk_width)
    split_cols = matrix.reshape(n_rows, n_local, n_mp, blk_width)
    picked = lax.dynamic_index_in_dim(split_cols, my_rank, axis=2, keepdims=False)
    return picked.reshape(n_rows, n_local * blk_width)


def add_damping(local_mat, my_rank, n_mp, blk_width):
    dim_size = local_mat.shape[0]
    n_local = local_mat.shape[1] // blk_width
    col_ids = ((jnp.arange(n_local)[:, None] * n_mp + my_rank) * blk_width + jnp.arange(blk_width)[None, :]).reshape(-1)
    on_diag = jnp.arange(dim_size)[:, None] == col_ids[None, :]
    return local_mat + jnp.where(on_diag, DAMP_SHIFT, 0.0)


def factor_cyclic(local_mat, my_rank, n_mp, blk_width):
    dim_size = local_mat.shape[0]
    n_local = local_mat.shape[1] // blk_width
    n_panels = dim_size // blk_width
    block_ids = jnp.arange(n_local) * n_mp + my_rank
    work_mat = local_mat
    row_pieces = []
    for panel_idx in range(n_panels):
        local_blk = panel_idx // n_mp
        is_owner = my_rank == panel_idx % n_mp
        top_row = panel_idx * blk_width
        col_start = local_blk * blk_width
        n_below = dim_size - top_row - blk_width
        column = work_mat[top_row:, col_start:col_start + blk_width]
        diag_fac = jnp.linalg.cholesky(column[:blk_width])
        if n_below > 0:
            below_diag = lax.linalg.triangular_solve(diag_fac, column[blk_width:], left_side=False, lower=True, transpose_a=True)
            panel_vals = jnp.concatenate([diag_fac, below_diag], axis=0)
        else:
            panel_vals = diag_fac
        panel_vals = lax.psum(jnp.where(is_owner, panel_vals, 0.0), 'mp')
        if top_row > 0:
            full_panel = jnp.concatenate([jnp.zeros((top_row, blk_width), jnp.float32), panel_vals], axis=0)
        else:
            full_panel = panel_vals
        mine_rows = lax.dynamic_index_in_dim(full_panel.reshape(n_local, n_mp, blk_width, blk_width), my_rank, axis=1, keepdims=False)
        row_pieces.append(mine_rows.reshape(n_local * blk_width, blk_width))
        kept_col = jnp.where(is_owner, full_panel, work_mat[:, col_start:col_start + blk_width])
        work_mat = lax.dynamic_update_slice(work_mat, kept_col, (0, col_start))
        if n_below > 0:
            keep_mask = (block_ids[local_blk:] > panel_idx).astype(jnp.float32)
            coupling = mine_rows[local_blk:] * keep_mask[:, None, None]
            change = jnp.einsum('in,tjn->itj', panel_vals[blk_width:], coupling, precision=PREC_HIGH, preferred_element_type=jnp.float32)
            trail_cols = work_mat[top_row + blk_width:, col_start:] - change.reshape(n_below, (n_local - local_blk) * blk_width)
            work_mat = lax.dynamic_update_slice(work_mat, trail_cols, (top_row + blk_width, col_start))
    return work_mat, row_pieces


def solve_cyclic(rhs_mat, l_cols, row_pieces, my_rank, n_mp, blk_width):
    n_rows = rhs_mat.shape[0]
    n_local = rhs_mat.shape[1] // blk_width
    n_panels = n_local * n_mp
    block_ids = jnp.arange(n_local) * n_mp + my_rank
    current = rhs_mat
    for panel_idx in range(n_panels):
        local_blk = panel_idx // n_mp
        is_owner = my_rank == panel_idx % n_mp
        col_start = local_blk * blk_width
        diag_fac = l_cols[panel_idx * blk_width:(panel_idx + 1) * blk_width, col_start:col_start + blk_width]
        solved = lax.linalg.triangular_solve(diag_fac, current[:, col_start:col_start + blk_width], left_side=False, lower=True, transpose_a=True)
        solved = lax.psum(jnp.where(is_owner, solved, 0.0), 'mp')
        keep_mask = (block_ids[local_blk:] > panel_idx).astype(jnp.float32)
        coupling = row_pieces[panel_idx][col_start:].reshape(n_local - local_blk, blk_width, blk_width) * keep_mask[:, None, None]
        change = jnp.einsum('in,tkn->itk', solved, coupling, precision=PREC_HIGH, preferred_element_type=jnp.float32)
        trail_cols = current[:, col_start:] - change.reshape(n_rows, (n_local - local_blk) * blk_width)
        lead_block = jnp.where(is_owner, solved, trail_cols[:, :blk_width])
        trail_cols = jnp.concatenate([lead_block, trail_cols[:, blk_width:]], axis=1)
        current = lax.dynamic_update_slice(current, trail_cols, (0, col_start))
    for panel_idx in reversed(range(n_panels)):
        local_blk = panel_idx // n_mp
        is_owner = my_rank == panel_idx % n_mp
        col_start = local_blk * blk_width
        diag_fac = l_cols[panel_idx * blk_width:(panel_idx + 1) * blk_width, col_start:col_start + blk_width]
        solved = lax.linalg.triangular_solve(diag_fac, current[:, col_start:col_start + blk_width], left_side=False, lower=True)
        solved = lax.psum(jnp.where(is_owner, solved, 0.0), 'mp')
        keep_mask = (block_ids[:local_blk + 1] < panel_idx).astype(jnp.float32)
        coupling = l_cols[panel_idx * blk_width:(panel_idx + 1) * blk_width, :col_start + blk_width].reshape(blk_width, local_blk + 1, blk_width) * keep_mask[None, :, None]
        change = jnp.einsum('in,ntk->itk', solved, coupling, precision=PREC_HIGH, preferred_element_type=jnp.float32)
        head_cols = current[:, :col_start + blk_width] - change.reshape(n_rows, (local_blk + 1) * blk_width)
        last_block = jnp.where(is_owner, solved, head_cols[:, col_start:])
        head_cols = jnp.concatenate([head_cols[:, :col_start], last_block], axis=1)
        current = lax.dynamic_update_slice(current, head_cols, (0, 0))
    return current


def solution(mesh):
    n_mp = mesh.shape['mp']
    n_dp = mesh.shape['dp']

    def local_step(a_loc, g_loc, w_loc, a_old_loc, s_old_loc):
        my_rank = lax.axis_index('mp')
        blk_width = w_loc.shape[2]
        d_in = a_loc.shape[1]
        d_out = g_loc.shape[1]
        n_all = a_loc.shape[0] * n_dp
        n_in_loc = d_in // (n_mp * blk_width)
        n_out_loc = d_out // (n_mp * blk_width)
        a_mine = own_columns(a_loc, my_rank, n_mp, blk_width)
        g_mine = own_columns(g_loc, my_rank, n_mp, blk_width)
        a_part = jnp.einsum('nd,nc->dc', a_loc, a_mine, preferred_element_type=jnp.float32)
        s_part = jnp.einsum('no,nc->oc', g_loc, g_mine, preferred_element_type=jnp.float32)
        gt_part = jnp.einsum('nd,nc->dc', a_loc, g_mine, preferred_element_type=jnp.float32)
        a_sum, s_sum, gt_sum = lax.psum((a_part, s_part, gt_part), 'dp')
        a_new = FACTOR_DECAY * a_old_loc.reshape(d_in, -1) + (1.0 - FACTOR_DECAY) * (a_sum / n_all)
        s_new = FACTOR_DECAY * s_old_loc.reshape(d_out, -1) + (1.0 - FACTOR_DECAY) * (s_sum / n_all)
        la_cols, la_rows = factor_cyclic(add_damping(a_new, my_rank, n_mp, blk_width), my_rank, n_mp, blk_width)
        ls_cols, ls_rows = factor_cyclic(add_damping(s_new, my_rank, n_mp, blk_width), my_rank, n_mp, blk_width)
        half_solved = solve_cyclic(gt_sum / n_all, ls_cols, ls_rows, my_rank, n_mp, blk_width)
        outgoing = half_solved.reshape(n_in_loc, n_mp, blk_width, n_out_loc * blk_width)
        received = lax.all_to_all(outgoing, 'mp', 1, 1, tiled=True)
        swapped = received.reshape(n_in_loc, n_mp, blk_width, n_out_loc, blk_width).transpose(3, 1, 4, 0, 2).reshape(d_out, n_in_loc * blk_width)
        step_delta = solve_cyclic(swapped, la_cols, la_rows, my_rank, n_mp, blk_width)
        w_new = w_loc.reshape(d_out, -1) - LEARN_RATE * step_delta
        return (w_new.reshape(w_loc.shape), a_new.reshape(a_old_loc.shape), s_new.reshape(s_old_loc.shape))

    spec_rows = P('dp', None)
    spec_cyc = P(None, 'mp', None)
    return jax.shard_map(local_step, mesh=mesh, in_specs=(spec_rows, spec_rows, spec_cyc, spec_cyc, spec_cyc), out_specs=(spec_cyc, spec_cyc, spec_cyc), check_vma=False)
```

profile of v0, /device:TPU:0, one launch (start us, length us, event | category | flops | bytes accessed | tf_op | source)
XLA Modules:
  0.0 3253.3 jit_solution(13598581065626072162)
XLA Ops:
  27.3 17.4 convolution_bitcast_fusion
  54.4 12.7 copy.586
  75.9 12.7 copy.589
  88.7 170.5 %all-reduce.217.cloned.1.call-done = (f32[768,384]{1,0:T(8,128)}, f32[2304,1152]{1,0:T(8,128)}, f32[768,1152]{1,0:T(8,128)}) async-done(((f32[768,384]{1,0:T(8,128)}, f32[2304,1152]{1,0:T(8,128)}, f32[768,1152]{1,0:T(8,128)}), (f32[768,384]{1,0:T(8,128)}, f32[2304,1152]{1,0:T(8,128)}, f32[768,1152]{1,0:T(8,128)})) %all-reduce.217.cloned.1.call-update) | async-done | bytes 15335440 | tf_op jit(solution)/shard_map/psum | solution.py:122
  304.0 22.9 all-reduce.97.cloned.1.call-done
  381.5 17.7 all-reduce.99.cloned.1.call-done
  452.0 17.9 all-reduce.101.cloned.1.call-done
  514.2 25.5 all-reduce.103.cloned.1.call-done
  583.7 25.1 all-reduce.105.cloned.1.call-done
  650.4 25.6 all-reduce.107.cloned.1.call-done
  717.5 24.7 all-reduce.109.cloned.1.call-done
  781.8 24.9 all-reduce.111.cloned.1.call-done
  849.2 20.4 all-reduce.113.cloned.1.call-done
  910.0 20.8 all-reduce.115.cloned.1.call-done
  968.1 24.0 all-reduce.117.cloned.1.call-done
  1027.9 24.4 all-reduce.119.cloned.1.call-done
  1087.1 24.8 all-reduce.121.cloned.1.call-done
  1145.0 22.8 all-reduce.123.cloned.1.call-done
  1198.7 23.2 all-reduce.125.cloned.1.call-done
  1252.1 23.2 all-reduce.127.cloned.1.call-done
  1308.2 20.2 all-reduce.129.cloned.1.call-done
  1353.5 20.2 all-reduce.131.cloned.1.call-done
  1403.4 13.9 all-reduce.133.cloned.1.call-done
  1469.9 14.7 all-reduce.137.cloned.1.call-done
  1770.5 13.2 all-reduce.149.cloned.1.call-done
  1798.3 17.6 all-reduce.151.cloned.1.call-done
  1828.5 18.6 all-reduce.153.cloned.1.call-done
  1860.3 17.2 all-reduce.155.cloned.1.call-done
  1888.5 19.7 all-reduce.157.cloned.1.call-done
  1919.0 20.1 all-reduce.159.cloned.1.call-done
  1947.5 21.5 all-reduce.161.cloned.1.call-done
  1975.2 23.1 all-reduce.163.cloned.1.call-done
  2002.5 24.2 all-reduce.165.cloned.1.call-done
  2035.6 20.0 all-reduce.167.cloned.1.call-done
  2061.9 22.8 all-reduce.169.cloned.1.call-done
  2099.9 18.5 all-reduce.171.cloned.1.call-done
  2129.2 22.7 all-reduce.173.cloned.1.call-done
  2164.5 20.6 all-reduce.175.cloned.1.call-done
  2193.7 24.3 all-reduce.177.cloned.1.call-done
  2229.6 21.7 all-reduce.179.cloned.1.call-done
  2261.7 21.5 all-reduce.181.cloned.1.call-done
  2297.1 18.7 all-reduce.183.cloned.1.call-done
  2326.1 21.7 all-reduce.185.cloned.1.call-done
  2363.7 16.3 all-reduce.187.cloned.1.call-done
  2392.9 18.5 all-reduce.189.cloned.1.call-done
  2426.1 17.0 all-reduce.191.cloned.1.call-done
  2456.0 18.0 all-reduce.229.cloned.1.call-done
  2484.2 13.2 cholesky.385
  2524.6 18.5 all-reduce.227.cloned.1.call-done
  2581.0 20.1 all-reduce.225.cloned.1.call-done
  2635.4 21.6 all-reduce.223.cloned.1.call-done
  2690.2 23.4 all-reduce.221.cloned.1.call-done
  2733.6 24.9 all-reduce.219.cloned.1.call-done
  2853.5 15.8 all-reduce.195.cloned.1.call-done
  2925.9 19.4 all-reduce.199.cloned.1.call-done
  2953.3 24.5 all-reduce.201.cloned.1.call-done
  2985.5 25.5 all-reduce.203.cloned.1.call-done
  3017.9 25.8 all-reduce.205.cloned.1.call-done
  3055.5 25.3 all-reduce.207.cloned.1.call-done
  3091.9 24.3 all-reduce.209.cloned.1.call-done
  3130.4 19.2 all-reduce.211.cloned.1.call-done
  3159.3 22.9 all-reduce.213.cloned.1.call-done
  3202.1 12.7 copy.749
  3214.8 12.7 copy.752
  (1396 shorter events, 1771.3 us)
Async XLA Ops:
  7.2 252.0 %all-reduce.217.cloned.1.call-start = ((), (), s32[]{:S(2)}) async-start(), calls=%async_computation.61 | async-start | bytes 30670848 | tf_op jit(solution)/shard_map/psum | solution.py:122
  54.1 272.8 %all-reduce.97.cloned.1.call-start = ((), (), s32[]{:S(2)}) async-start(), calls=%async_computation.1 | async-start | bytes 2359296 | tf_op jit(solution)/shard_map/psum | solution.py:50
  302.8 96.4 %all-reduce.99.cloned.1.call-start = ((), (), s32[]{:S(2)}) async-start(), calls=%async_computation.2 | async-start | bytes 2228224 | tf_op jit(solution)/shard_map/psum | solution.py:50
  373.0 96.9 %all-reduce.101.cloned.1.call-start = ((), (), s32[]{:S(2)}) async-start(), calls=%async_computation.3 | async-start | bytes 2097152 | tf_op jit(solution)/shard_map/psum | solution.py:50
  443.7 96.0 %all-reduce.103.cloned.1.call-start = ((), (), s32[]{:S(2)}) async-start(), calls=%async_computation.4 | async-start | bytes 1966080 | tf_op jit(solution)/shard_map/psum | solution.py:50
  513.7 95.1 %all-reduce.105.cloned.1.call-start = ((), (), s32[]{:S(2)}) async-start(), calls=%async_computation.5 | async-start | bytes 1835008 | tf_op jit(solution)/shard_map/psum | solution.py:50
  582.9 93.1 %all-reduce.107.cloned.1.call-start = ((), (), s32[]{:S(2)}) async-start(), calls=%async_computation.6 | async-start | bytes 1703936 | tf_op jit(solution)/shard_map/psum | solution.py:50
  650.1 92.1 %all-reduce.109.cloned.1.call-start = ((), (), s32[]{:S(2)}) async-start(), calls=%async_computation.7 | async-start | bytes 1572864 | tf_op jit(solution)/shard_map/psum | solution.py:50
  716.5 90.2 %all-reduce.111.cloned.1.call-start = ((), (), s32[]{:S(2)}) async-start(), calls=%async_computation.8 | async-start | bytes 1441792 | tf_op jit(solution)/shard_map/psum | solution.py:50
  780.9 88.6 %all-reduce.113.cloned.1.call-start = ((), (), s32[]{:S(2)}) async-start(), calls=%async_computation.9 | async-start | bytes 1310720 | tf_op jit(solution)/shard_map/psum | solution.py:50
  843.9 86.8 %all-reduce.115.cloned.1.call-start = ((), (), s32[]{:S(2)}) async-start(), calls=%async_computation.10 | async-start | bytes 1179648 | tf_op jit(solution)/shard_map/psum | solution.py:50
  905.2 86.9 %all-reduce.117.cloned.1.call-start = ((), (), s32[]{:S(2)}) async-start(), calls=%async_computation.11 | async-start | bytes 1048576 | tf_op jit(solution)/shard_map/psum | solution.py:50
  966.5 85.8 %all-reduce.119.cloned.1.call-start = ((), (), s32[]{:S(2)}) async-start(), calls=%async_computation.12 | async-start | bytes 917504 | tf_op jit(solution)/shard_map/psum | solution.py:50
  1026.9 85.0 %all-reduce.121.cloned.1.call-start = ((), (), s32[]{:S(2)}) async-start(), calls=%async_computation.13 | async-start | bytes 786432 | tf_op jit(solution)/shard_map/psum | solution.py:50
  1086.6 81.2 %all-reduce.123.cloned.1.call-start = ((), (), s32[]{:S(2)}) async-start(), calls=%async_computation.14 | async-start | bytes 655360 | tf_op jit(solution)/shard_map/psum | solution.py:50
  1142.7 79.3 %all-reduce.125.cloned.1.call-start = ((), (), s32[]{:S(2)}) async-start(), calls=%async_computation.15 | async-start | bytes 524288 | tf_op jit(solution)/shard_map/psum | solution.py:50
  1196.8 78.5 %all-reduce.127.cloned.1.call-start = ((), (), s32[]{:S(2)}) async-start(), calls=%async_computation.16 | async-start | bytes 393216 | tf_op jit(solution)/shard_map/psum | solution.py:50
  1250.4 78.1 %all-reduce.129.cloned.1.call-start = ((), (), s32[]{:S(2)}) async-start(), calls=%async_computation.17 | async-start | bytes 262144 | tf_op jit(solution)/shard_map/psum | solution.py:50
  1303.6 70.2 %all-reduce.131.cloned.1.call-start = ((), (), s32[]{:S(2)}) async-start(), calls=%async_computation.18 | async-start | bytes 131072 | tf_op jit(solution)/shard_map/psum | solution.py:50
  1349.1 68.3 %all-reduce.133.cloned.1.call-start = ((), (), s32[]{:S(2)}) async-start(), calls=%async_computation.19 | async-start | bytes 786432 | tf_op jit(solution)/shard_map/psum | solution.py:80
  1392.0 59.1 %all-reduce.135.cloned.1.call-start = ((), (), s32[]{:S(2)}) async-start(), calls=%async_computation.20 | async-start | bytes 786432 | tf_op jit(solution)/shard_map/psum | solution.py:80
  1425.8 58.8 %all-reduce.137.cloned.1.call-start = ((), (), s32[]{:S(2)}) async-start(), calls=%async_computation.21 | async-start | bytes 786432 | tf_op jit(solution)/shard_map/psum | solution.py:80
  1459.3 58.4 %all-reduce.139.cloned.1.call-start = ((), (), s32[]{:S(2)}) async-start(), calls=%async_computation.22 | async-start | bytes 786432 | tf_op jit(solution)/shard_map/psum | solution.py:80
  1492.4 58.3 %all-reduce.141.cloned.1.call-start = ((), (), s32[]{:S(2)}) async-start(), calls=%async_computation.23 | async-start | bytes 786432 | tf_op jit(solution)/shard_map/psum | solution.py:80
  1525.3 59.5 %all-reduce.143.cloned.1.call-start = ((), (), s32[]{:S(2)}) async-start(), calls=%async_computation.24 | async-start | bytes 786432 | tf_op jit(solution)/shard_map/psum | solution.py:80
  1558.7 60.6 %all-reduce.145.cloned.1.call-start = ((), (), s32[]{:S(2)}) async-start(), calls=%async_computation.25 | async-start | bytes 786432 | tf_op jit(solution)/shard_map/psum | solution.py:80
  1591.5 160.1 %all-reduce.147.cloned.1.call-start = ((), (), s32[]{:S(2)}) async-start(), calls=%async_computation.26 | async-start | bytes 786432 | tf_op jit(solution)/shard_map/psum | solution.py:80
  1626.7 156.9 %all-reduce.149.cloned.1.call-start = ((), (), s32[]{:S(2)}) async-start(), calls=%async_computation.27 | async-start | bytes 786432 | tf_op jit(solution)/shard_map/psum | solution.py:80
  1758.4 57.5 %all-reduce.151.cloned.1.call-start = ((), (), s32[]{:S(2)}) async-start(), calls=%async_computation.28 | async-start | bytes 786432 | tf_op jit(solution)/shard_map/psum | solution.py:80
  1790.6 56.5 %all-reduce.153.cloned.1.call-start = ((), (), s32[]{:S(2)}) async-start(), calls=%async_computation.29 | async-start | bytes 786432 | tf_op jit(solution)/shard_map/psum | solution.py:80
  1821.8 55.7 %all-reduce.155.cloned.1.call-start = ((), (), s32[]{:S(2)}) async-start(), calls=%async_computation.30 | async-start | bytes 786432 | tf_op jit(solution)/shard_map/psum | solution.py:80
  1852.2 56.0 %all-reduce.157.cloned.1.call-start = ((), (), s32[]{:S(2)}) async-start(), calls=%async_computation.31 | async-start | bytes 786432 | tf_op jit(solution)/shard_map/psum | solution.py:80
  1882.9 56.2 %all-reduce.159.cloned.1.call-start = ((), (), s32[]{:S(2)}) async-start(), calls=%async_computation.32 | async-start | bytes 786432 | tf_op jit(solution)/shard_map/psum | solution.py:80
  1913.8 55.2 %all-reduce.161.cloned.1.call-start = ((), (), s32[]{:S(2)}) async-start(), calls=%async_computation.33 | async-start | bytes 786432 | tf_op jit(solution)/shard_map/psum | solution.py:80
  1943.7 54.5 %all-reduce.163.cloned.1.call-start = ((), (), s32[]{:S(2)}) async-start(), calls=%async_computation.34 | async-start | bytes 786432 | tf_op jit(solution)/shard_map/psum | solution.py:80
  2059.3 59.0 %all-reduce.171.cloned.1.call-start = ((), (), s32[]{:S(2)}) async-start(), calls=%async_computation.38 | async-start | bytes 786432 | tf_op jit(solution)/shard_map/psum | solution.py:94
  2093.1 58.8 %all-reduce.173.cloned.1.call-start = ((), (), s32[]{:S(2)}) async-start(), calls=%async_computation.39 | async-start | bytes 786432 | tf_op jit(solution)/shard_map/psum | solution.py:94
  2126.6 58.4 %all-reduce.175.cloned.1.call-start = ((), (), s32[]{:S(2)}) async-start(), calls=%async_computation.40 | async-start | bytes 786432 | tf_op jit(solution)/shard_map/psum | solution.py:94
  2159.8 58.3 %all-reduce.177.cloned.1.call-start = ((), (), s32[]{:S(2)}) async-start(), calls=%async_computation.41 | async-start | bytes 786432 | tf_op jit(solution)/shard_map/psum | solution.py:94
  2192.7 58.5 %all-reduce.179.cloned.1.call-start = ((), (), s32[]{:S(2)}) async-start(), calls=%async_computation.42 | async-start | bytes 786432 | tf_op jit(solution)/shard_map/psum | solution.py:94
  2226.0 57.1 %all-reduce.181.cloned.1.call-start = ((), (), s32[]{:S(2)}) async-start(), calls=%async_computation.43 | async-start | bytes 786432 | tf_op jit(solution)/shard_map/psum | solution.py:94
  2257.9 58.0 %all-reduce.183.cloned.1.call-start = ((), (), s32[]{:S(2)}) async-start(), calls=%async_computation.44 | async-start | bytes 786432 | tf_op jit(solution)/shard_map/psum | solution.py:94
  2290.6 57.2 %all-reduce.185.cloned.1.call-start = ((), (), s32[]{:S(2)}) async-start(), calls=%async_computation.45 | async-start | bytes 786432 | tf_op jit(solution)/shard_map/psum | solution.py:94
  2322.5 57.5 %all-reduce.187.cloned.1.call-start = ((), (), s32[]{:S(2)}) async-start(), calls=%async_computation.46 | async-start | bytes 786432 | tf_op jit(solution)/shard_map/psum | solution.py:94
  2354.8 56.7 %all-reduce.189.cloned.1.call-start = ((), (), s32[]{:S(2)}) async-start(), calls=%async_computation.47 | async-start | bytes 786432 | tf_op jit(solution)/shard_map/psum | solution.py:94
  2386.1 57.0 %all-reduce.191.cloned.1.call-start = ((), (), s32[]{:S(2)}) async-start(), calls=%async_computation.48 | async-start | bytes 786432 | tf_op jit(solution)/shard_map/psum | solution.py:94
  2417.8 56.1 %all-reduce.229.cloned.1.call-start = ((), (), s32[]{:S(2)}) async-start(), calls=%async_computation.67 | async-start | bytes 1572864 | tf_op jit(solution)/shard_map/psum | solution.py:50
  2448.0 95.0 %all-reduce.227.cloned.1.call-start = ((), (), s32[]{:S(2)}) async-start(), calls=%async_computation.66 | async-start | bytes 1441792 | tf_op jit(solution)/shard_map/psum | solution.py:50
  2516.5 84.6 %all-reduce.225.cloned.1.call-start = ((), (), s32[]{:S(2)}) async-start(), calls=%async_computation.65 | async-start | bytes 1310720 | tf_op jit(solution)/shard_map/psum | solution.py:50
  2575.4 81.6 %all-reduce.223.cloned.1.call-start = ((), (), s32[]{:S(2)}) async-start(), calls=%async_computation.64 | async-start | bytes 1179648 | tf_op jit(solution)/shard_map/psum | solution.py:50
  2631.4 82.2 %all-reduce.221.cloned.1.call-start = ((), (), s32[]{:S(2)}) async-start(), calls=%async_computation.63 | async-start | bytes 1048576 | tf_op jit(solution)/shard_map/psum | solution.py:50
  2688.0 70.5 %all-reduce.219.cloned.1.call-start = ((), (), s32[]{:S(2)}) async-start(), calls=%async_computation.62 | async-start | bytes 917504 | tf_op jit(solution)/shard_map/psum | solution.py:50
  2733.1 99.1 %all-reduce.193.cloned.1.call-start = ((), (), s32[]{:S(2)}) async-start(), calls=%async_computation.49 | async-start | bytes 2359296 | tf_op jit(solution)/shard_map/psum | solution.py:80
  2805.8 63.6 %all-reduce.195.cloned.1.call-start = ((), (), s32[]{:S(2)}) async-start(), calls=%async_computation.50 | async-start | bytes 2359296 | tf_op jit(solution)/shard_map/psum | solution.py:80
  2843.0 68.8 %all-reduce.197.cloned.1.call-start = ((), (), s32[]{:S(2)}) async-start(), calls=%async_computation.51 | async-start | bytes 2359296 | tf_op jit(solution)/shard_map/psum | solution.py:80
  2878.3 66.9 %all-reduce.199.cloned.1.call-start = ((), (), s32[]{:S(2)}) async-start(), calls=%async_computation.52 | async-start | bytes 2359296 | tf_op jit(solution)/shard_map/psum | solution.py:80
  2919.0 58.8 %all-reduce.201.cloned.1.call-start = ((), (), s32[]{:S(2)}) async-start(), calls=%async_computation.53 | async-start | bytes 2359296 | tf_op jit(solution)/shard_map/psum | solution.py:80
  2951.5 59.6 %all-reduce.203.cloned.1.call-start = ((), (), s32[]{:S(2)}) async-start(), calls=%async_computation.54 | async-start | bytes 2359296 | tf_op jit(solution)/shard_map/psum | solution.py:80
  2984.8 58.9 %all-reduce.205.cloned.1.call-start = ((), (), s32[]{:S(2)}) async-start(), calls=%async_computation.55 | async-start | bytes 2359296 | tf_op jit(solution)/shard_map/psum | solution.py:94
  3017.4 63.5 %all-reduce.207.cloned.1.call-start = ((), (), s32[]{:S(2)}) async-start(), calls=%async_computation.56 | async-start | bytes 2359296 | tf_op jit(solution)/shard_map/psum | solution.py:94
  3054.6 61.6 %all-reduce.209.cloned.1.call-start = ((), (), s32[]{:S(2)}) async-start(), calls=%async_computation.57 | async-start | bytes 2359296 | tf_op jit(solution)/shard_map/psum | solution.py:94
  3089.9 59.7 %all-reduce.211.cloned.1.call-start = ((), (), s32[]{:S(2)}) async-start(), calls=%async_computation.58 | async-start | bytes 2359296 | tf_op jit(solution)/shard_map/psum | solution.py:94
  3123.3 58.8 %all-reduce.213.cloned.1.call-start = ((), (), s32[]{:S(2)}) async-start(), calls=%async_computation.59 | async-start | bytes 2359296 | tf_op jit(solution)/shard_map/psum | solution.py:94
  3155.8 71.7 %all-reduce.215.cloned.1.call-start = ((), (), s32[]{:S(2)}) async-start(), calls=%async_computation.60 | async-start | bytes 2359296 | tf_op jit(solution)/shard_map/psum | solution.py:94
  (286 other events, 2291.8 us)
Sparse Core Ops, SparseCore 0:
  54.2 204.9 all-reduce.216
  373.1 26.0 all-reduce.98
  443.9 25.9 all-reduce.100
  513.8 25.8 all-reduce.102
  583.0 25.7 all-reduce.104
  650.2 25.7 all-reduce.106
  716.6 25.6 all-reduce.108
  781.1 25.5 all-reduce.110
  844.0 25.4 all-reduce.112
  905.3 25.3 all-reduce.114
  966.6 25.3 all-reduce.116
  1027.1 25.2 all-reduce.118
  1086.8 25.1 all-reduce.120
  1142.8 25.0 all-reduce.122
  1197.0 24.9 all-reduce.124
  1250.5 24.8 all-reduce.126
  1392.1 25.1 all-reduce.132
  1425.9 25.1 all-reduce.134
  1459.4 25.1 all-reduce.136
  1492.5 25.1 all-reduce.138
  1525.4 25.2 all-reduce.140
  1558.8 25.2 all-reduce.142
  1591.6 25.4 all-reduce.144
  1626.9 25.1 all-reduce.146
  1758.5 25.1 all-reduce.148
  1790.7 25.1 all-reduce.150
  1821.9 25.1 all-reduce.152
  1852.4 25.1 all-reduce.154
  1883.1 25.1 all-reduce.156
  1913.9 25.1 all-reduce.158
  1943.9 25.1 all-reduce.160
  1973.1 25.1 all-reduce.162
  2001.5 25.1 all-reduce.164
  2030.5 25.1 all-reduce.166
  2059.5 25.1 all-reduce.168
  2093.2 25.1 all-reduce.170
  2126.8 25.1 all-reduce.172
  2159.9 25.1 all-reduce.174
  2192.9 25.1 all-reduce.176
  2226.1 25.1 all-reduce.178
  2258.0 25.1 all-reduce.180
  2290.7 25.1 all-reduce.182
  2322.6 25.1 all-reduce.184
  2354.9 25.1 all-reduce.186
  2386.3 25.1 all-reduce.188
  2418.0 25.1 all-reduce.190
  2448.2 25.7 all-reduce.228
  2516.7 26.3 all-reduce.226
  2575.5 25.5 all-reduce.224
  2631.5 25.4 all-reduce.222
  2688.1 25.3 all-reduce.220
  2733.2 25.2 all-reduce.218
  2805.9 26.1 all-reduce.192
  2843.1 26.1 all-reduce.194
  2878.5 26.1 all-reduce.196
  2919.1 26.1 all-reduce.198
  2951.6 26.1 all-reduce.200
  2984.9 26.1 all-reduce.202
  3017.5 26.1 all-reduce.204
  3054.7 26.1 all-reduce.206
  3090.0 26.1 all-reduce.208
  3123.4 26.1 all-reduce.210
  3156.0 26.1 all-reduce.212
  3189.4 26.1 all-reduce.214
  (3 shorter events, 73.0 us)
where the time goes:
time: 3270 us; the launch traced here: 3250 us
  waiting for transfers between devices  1420 us (43%)
  other arithmetic  1040 us (32%)
  matrix products  412 us (13%)
  local copies, waits for them, and re-layouts  340 us (10%)
    psum x42, waiting for transfers between devices, solve_cyclic(): solved = lax.psum(jnp.where(is_owner, solved, 0.0), 'mp')  711 us
    psum x24, waiting for transfers between devices, factor_cyclic(): panel_vals = lax.psum(jnp.where(is_owner, panel_vals, 0.0), 'mp')  535 us
    another operation x72, other arithmetic, factor_cyclic(): diag_fac = jnp.linalg.cholesky(column[:blk_width])  301 us
    another operation x27, other arithmetic, solve_cyclic(): lax.linalg.triangular_solve(diag_fac, current[:, col_start:col_start + bl...  264 us
    another operation x44, other arithmetic, factor_cyclic(): lax.linalg.triangular_solve(diag_fac, column[blk_width:], left_side=False...  239 us
    psum x1, waiting for transfers between devices, local_step(): a_sum, s_sum, gt_sum = lax.psum((a_part, s_part, gt_part), 'dp')  171 us
    unnamed x545, local copies, waits for them, and re-layouts  158 us
    dot_general x22, matrix products, factor_cyclic(): jnp.einsum('in,tjn->itj', panel_vals[blk_width:], coupling, precision=PRE...  104 us
  transfers between devices with their start and end apart: 67, of which 62 were waited for; matrix products, arithmetic and copies ran while one was open for 17% of the time, Pallas kernels for 0%

commit v1 on v0

v1 whole, which is shorter than its diff:
```python
import functools
import math
import jax
import jax.numpy as jnp
from jax import lax
from jax.experimental import pallas as pl
from jax.experimental.pallas import tpu as pltpu
from jax.sharding import PartitionSpec as P

FACTOR_DECAY = 0.95
DAMPING = 0.001
DAMP_SHIFT = math.sqrt(DAMPING)
LEARN_RATE = 1.0
BW = 128
PW = 256
F32 = jnp.float32
BF = jnp.bfloat16
NT = (((1,), (1,)), ((), ()))
NN = (((1,), (0,)), ((), ()))


def bc(x, shape=(8, BW)):
    return jnp.broadcast_to(x, shape)

def factor_block(mat, linv, mb=16):
    lane = lax.broadcasted_iota(jnp.int32, (8, BW), 1)
    sub = lax.broadcasted_iota(jnp.int32, (8, BW), 0)
    for t in range(BW // mb):
        k = t * mb
        nr = mb // 8
        rows = [mat[k + 8 * r:k + 8 * r + 8, :] for r in range(nr)]
        cols = [[bc(rows[r][:, k + i:k + i + 1]) for r in range(nr)] for i in range(mb)]
        inside = (lane >= k) & (lane < k + mb)
        ext = [jnp.where(inside, jnp.where(lane == sub + (k + 8 * r), 1.0, 0.0), rows[r]) for r in range(nr)]
        rv = [jnp.zeros((8, BW), F32) for _ in range(nr)]
        below = list(range((k + mb) // 8, BW // 8))
        old = {r: mat[8 * r:8 * r + 8, :] for r in below}
        for j in range(mb):
            jr, js = divmod(j, 8)
            piv = bc(cols[j][jr][js:js + 1, :])
            rinv = 1.0 / piv
            prow = bc(ext[jr][js:js + 1, :])
            linv[k + j:k + j + 1, :] = (prow * lax.rsqrt(piv))[0:1, :]
            here = sub == js
            mask = [jnp.where(here, 0.0, cols[j][r]) if r == jr else cols[j][r] for r in range(nr)]
            fac = [mask[r] * rinv for r in range(nr)]
            for i in range(j + 1, mb):
                b = bc(cols[i][jr][js:js + 1, :])
                if i == j + 1:
                    cols[i] = [cols[i][r] - (mask[r] * b) * rinv for r in range(nr)]
                else:
                    cols[i] = [cols[i][r] - fac[r] * b for r in range(nr)]
            ext = [ext[r] - fac[r] * prow for r in range(nr)]
            rv[jr] = jnp.where(here, rinv, rv[jr])
        w = [ext[r] * rv[r] for r in range(nr)]
        for r in below:
            acc = jnp.where(inside, 0.0, old[r])
            for j in range(mb):
                jr, js = divmod(j, 8)
                acc = acc - bc(old[r][:, k + j:k + j + 1]) * bc(w[jr][js:js + 1, :])
            mat[8 * r:8 * r + 8, :] = acc
    ri = lax.broadcasted_iota(jnp.int32, (BW, BW), 0)
    ci = lax.broadcasted_iota(jnp.int32, (BW, BW), 1)
    linv[...] = jnp.where(ci <= ri, linv[...], 0.0)


def split3(x):
    h = x.astype(BF)
    r = x - h.astype(F32)
    m = r.astype(BF)
    return h, m, (r - m.astype(F32)).astype(BF)

def dot6(a, b, dims):
    d = lambda x, y: lax.dot_general(x, y, dims, preferred_element_type=F32)
    ah, am, al = a
    bh, bm, bl = b
    return (d(am, bm) + d(ah, bl) + d(al, bh)) + (d(ah, bm) + d(am, bh)) + d(ah, bh)

def dotf(a, b, dims):
    return dot6(split3(a), split3(b), dims)

def solve_kernel(n, damp, s_ref, b_ref, x_ref, tmat, mat, linv, inv_all, pan, pant):
    npan = n // PW
    eye = jnp.where(lax.broadcasted_iota(jnp.int32, (PW, PW), 0) == lax.broadcasted_iota(jnp.int32, (PW, PW), 1), damp, 0.0)
    def load(j, _):
        def rows(i, _):
            tmat[j, pl.ds(i * PW, PW), :] = s_ref[j, pl.ds(i * PW, PW), :]
            return 0
        lax.fori_loop(j, npan, rows, 0)
        tmat[j, pl.ds(j * PW, PW), :] = s_ref[j, pl.ds(j * PW, PW), :] + eye
        x_ref[j] = b_ref[j]
        return 0
    lax.fori_loop(0, npan, load, 0)

    def panel(q, _):
        r0 = q * PW
        mat[...] = tmat[q, pl.ds(r0, BW), 0:BW]
        factor_block(mat, linv)
        inv0 = linv[...]
        inv0s = split3(inv0)
        l10 = dot6(split3(tmat[q, pl.ds(r0 + BW, BW), 0:BW]), inv0s, NT)
        l10s = split3(l10)
        mat[...] = tmat[q, pl.ds(r0 + BW, BW), BW:PW] - dot6(l10s, l10s, NT)
        inv_all[q, 0:BW, 0:BW] = inv0
        inv_all[q, 0:BW, BW:PW] = jnp.zeros((BW, BW), F32)
        inv_all[q, BW:PW, 0:BW] = dot6(l10s, inv0s, NN)
        factor_block(mat, linv)
        inv1 = linv[...]
        inv_all[q, BW:PW, BW:PW] = inv1
        inv_all[q, BW:PW, 0:BW] = -dotf(inv1, inv_all[q, BW:PW, 0:BW], NN)
        invs = split3(inv_all[q])
        y = dot6(split3(x_ref[q]), invs, NT)
        x_ref[q] = y
        ys = split3(y)
        def below(i, _):
            r = pl.ds(i * PW, PW)
            lo = dot6(split3(tmat[q, r, :]), invs, NT)
            tmat[q, r, :] = lo
            sp = split3(lo)
            lt = lo.T
            st = split3(lt)
            for z in range(3):
                pan[z, r, :] = sp[z]
                pant[z, i] = st[z]
            return 0
        lax.fori_loop(q + 1, npan, below, 0)
        def trail(j, _):
            w = [pant[z, j] for z in range(3)]
            x_ref[j] = x_ref[j] - dot6(ys, w, NN)
            def rows(i, _):
                r = pl.ds(i * PW, PW)
                tmat[j, r, :] = tmat[j, r, :] - dot6([pan[z, r, :] for z in range(3)], w, NN)
                return 0
            lax.fori_loop(j, npan, rows, 0)
            return 0
        lax.fori_loop(q + 1, npan, trail, 0)
        return 0
    lax.fori_loop(0, npan, panel, 0)

    def back(p, _):
        q = npan - 1 - p
        def sub(i, acc):
            return acc - dotf(x_ref[i], tmat[q, pl.ds(i * PW, PW), :], NN)
        acc = lax.fori_loop(q + 1, npan, sub, x_ref[q])
        x_ref[q] = dotf(acc, inv_all[q], NN)
        return 0
    lax.fori_loop(0, npan, back, 0)

def spd_solve2(s2, b2, damp):
    npan, n, _ = s2.shape
    vm = pl.BlockSpec(memory_space=pltpu.VMEM)
    return pl.pallas_call(functools.partial(solve_kernel, n, damp), out_shape=jax.ShapeDtypeStruct(b2.shape, F32),
        in_specs=[vm, vm], out_specs=vm,
        scratch_shapes=[pltpu.VMEM((npan, n, PW), F32), pltpu.VMEM((BW, BW), F32), pltpu.VMEM((BW, BW), F32), pltpu.VMEM((npan, PW, PW), F32),
            pltpu.VMEM((3, n, PW), BF), pltpu.VMEM((3, npan, PW, PW), BF)],
        compiler_params=pltpu.CompilerParams(vmem_limit_bytes=63 * 2**20), name="spd_solve")(s2, b2)


def own_columns(matrix, my_rank, n_mp):
    n_rows, n_cols = matrix.shape
    split_cols = matrix.reshape(n_rows, n_cols // (n_mp * BW), n_mp, BW)
    return lax.dynamic_index_in_dim(split_cols, my_rank, axis=2, keepdims=False).reshape(n_rows, n_cols // n_mp)


def panels(local_mat):
    n_rows, n_cols = local_mat.shape
    both = lax.all_gather(local_mat, 'mp').reshape(2, n_rows, n_cols // BW, BW)
    return both.transpose(2, 1, 0, 3).reshape(n_cols // BW, n_rows, PW)


def solution(mesh):
    n_mp = mesh.shape['mp']
    n_dp = mesh.shape['dp']

    def local_step(a_loc, g_loc, w_loc, a_old_loc, s_old_loc):
        my_rank = lax.axis_index('mp')
        d_idx = lax.axis_index('dp')
        d_in = a_loc.shape[1]
        d_out = g_loc.shape[1]
        n_all = a_loc.shape[0] * n_dp
        a_mine = own_columns(a_loc, my_rank, n_mp)
        g_mine = own_columns(g_loc, my_rank, n_mp)
        a_part = jnp.einsum('nd,nc->dc', a_loc, a_mine, preferred_element_type=F32)
        s_part = jnp.einsum('no,nc->oc', g_loc, g_mine, preferred_element_type=F32)
        gt_part = jnp.einsum('nd,nc->dc', a_loc, g_mine, preferred_element_type=F32)
        a_sum, s_sum, gt_sum = lax.psum((a_part, s_part, gt_part), 'dp')
        a_new = FACTOR_DECAY * a_old_loc.reshape(d_in, -1) + (1.0 - FACTOR_DECAY) * (a_sum / n_all)
        s_new = FACTOR_DECAY * s_old_loc.reshape(d_out, -1) + (1.0 - FACTOR_DECAY) * (s_sum / n_all)
        n_own = d_in // (n_mp * n_dp)
        m_pad = -(-n_own // 8) * 8
        own = d_idx * n_own + jnp.arange(m_pad)
        spot = (own // BW) * PW + my_rank * BW + own % BW
        pick = jnp.where((jnp.arange(m_pad) < n_own)[:, None] & (spot[:, None] == jnp.arange(d_in)[None, :]), 1.0, 0.0)
        pick = pick.reshape(m_pad, d_in // PW, PW).transpose(1, 0, 2)
        inv_rows = spd_solve2(panels(a_new), pick, DAMP_SHIFT)
        inv_rows = inv_rows.transpose(1, 0, 2).reshape(m_pad, d_in)
        gt_both = lax.all_gather(gt_sum / n_all, 'mp')
        zt = jnp.einsum('md,pdc->pmc', inv_rows, gt_both, precision=lax.Precision.HIGHEST, preferred_element_type=F32)
        zt = zt.reshape(n_mp, m_pad, d_out // PW, BW).transpose(2, 1, 0, 3).reshape(d_out // PW, m_pad, PW)
        xt = spd_solve2(panels(s_new), zt, DAMP_SHIFT)[:, :n_own, :]
        delta = lax.all_gather(xt, 'dp').transpose(1, 3, 0, 2).reshape(w_loc.shape)
        w_new = w_loc - LEARN_RATE * delta
        return (w_new, a_new.reshape(a_old_loc.shape), s_new.reshape(s_old_loc.shape))

    spec_rows = P('dp', None)
    spec_cyc = P(None, 'mp', None)
    return jax.shard_map(local_step, mesh=mesh, in_specs=(spec_rows, spec_rows, spec_cyc, spec_cyc, spec_cyc), out_specs=(spec_cyc, spec_cyc, spec_cyc), check_vma=False)
```

time: 3270 us -> 704 us (0.22)
  waiting for transfers between devices: 1420 us -> 253 us
  other arithmetic: 1040 us -> 32.5 us
  matrix products: 412 us -> 29.5 us
  Pallas kernels: 0 us -> 191 us
  local copies, waits for them, and re-layouts: 340 us -> 180 us
    psum x66 -> x0, waiting for transfers between devices: 1250 us -> none  [the longest x42 711 us: solve_cyclic(): solved = lax.psum(jnp.where(is_owner, solved, 0.0), 'mp')]
    another operation x143 -> x0, other arithmetic: 803 us -> none  [the longest x72 301 us: factor_cyclic(): diag_fac = jnp.linalg.cholesky(column[:blk_width])]
    dot_general x73 -> x4, matrix products: 308 us -> 29.5 us  [the longest x1 13.7 us: local_step(): s_part = jnp.einsum('no,nc->oc', g_loc, g_mine, preferred_element_type=F32)]
    pallas_call x0 -> x2, Pallas kernels: none -> 191 us  [spd_solve2(): pl.pallas_call(functools.partial(solve_kernel, n, damp), out_shape=jax.Sh...]
    unnamed x545 -> x14, local copies, waits for them, and re-layouts: 158 us -> 42.9 us
    another operation x70 -> x0, matrix products: 104 us -> none  [the longest x48 75.4 us: solve_cyclic(): lax.linalg.triangular_solve(diag_fac, current[:, col_start:col_start + bl...]
    reshape x10 -> x8, local copies, waits for them, and re-layouts: 23.9 us -> 106 us  [the longest x4 68.3 us: panels(): both = lax.all_gather(local_mat, 'mp').reshape(2, n_rows, n_cols // BW, BW)]
    slice x131 -> x0, local copies, waits for them, and re-layouts: 78.3 us -> none  [the longest x24 26.4 us: solve_cyclic(): trail_cols[:, blk_width:]]
  transfers between devices with their start and end apart: 67 -> 5, of which waited for: 62 -> 2; matrix products, arithmetic and copies ran while one was open for 17% -> 12% of each run, Pallas kernels for 0% -> 4%
where the time goes in v1:
time: 704 us; the launch traced here: 700 us
  waiting for transfers between devices  253 us (36%)
  Pallas kernels  191 us (27%)
  local copies, waits for them, and re-layouts  180 us (26%)
  other arithmetic  32.5 us (5%)
  matrix products  29.5 us (4%)
  between operations  13.9 us (2%)
    psum x1, waiting for transfers between devices, local_step(): a_sum, s_sum, gt_sum = lax.psum((a_part, s_part, gt_part), 'dp')  203 us
    pallas_call x2, Pallas kernels, spd_solve2(): pl.pallas_call(functools.partial(solve_kernel, n, damp), out_shape=jax.Sh...  191 us
    reshape x4, local copies, waits for them, and re-layouts, panels(): both = lax.all_gather(local_mat, 'mp').reshape(2, n_rows, n_cols // BW, BW)  68.3 us
    all_gather x1, waiting for transfers between devices, local_step(): delta = lax.all_gather(xt, 'dp').transpose(1, 3, 0, 2).reshape(w_loc.shape)  49.6 us
    unnamed x14, local copies, waits for them, and re-layouts  42.9 us
    reshape x2, local copies, waits for them, and re-layouts, panels(): return both.transpose(2, 1, 0, 3).reshape(n_cols // BW, n_rows, PW)  31.1 us
  transfers between devices with their start and end apart: 5, of which 2 were waited for; matrix products, arithmetic and copies ran while one was open for 12% of the time, Pallas kernels for 4%

profile of v1, /device:TPU:0, one launch (start us, length us, event | category | flops | bytes accessed | tf_op | source)
XLA Modules:
  0.0 700.2 jit_solution(16982487868657909938)
XLA Ops:
  7.2 0.0 all-reduce.3.cloned.1.call-start
  7.2 12.6 %copy.41 = bf16[2048,2304]{0,1:T(8,128)(2,1)} copy(bf16[2048,2304]{1,0:T(8,128)(2,1)} %param.6) | data formatting | bytes 18874368 | tf_op args[1]
  19.8 0.0 copy-start
  19.8 2.9 constant_dynamic-slice_fusion.1
  22.7 2.2 copy-done
  24.9 0.0 copy-start.1
  24.9 13.7 %convolution_bitcast_fusion = f32[2304,1152]{0,1:T(8,128)} fusion(bf16[2048,1152]{0,1:T(8,128)(2,1)S(1)} %bitcast.60, bf16[2048,2304]{1,0:T(8,128)(2,1)S(1)} %copy-done), kind=kOutput, calls=%fused_computation | convolution fusion | flops 10871635968 | bytes 24772608 | tf_op jit(solution)/shard_map/no,nc->oc/dot_general | solution.py:184
  38.6 0.0 copy-done.1
  38.6 5.7 convolution_bitcast_fusion.1
  44.3 3.2 copy.44
  47.5 0.2 constant_dynamic-slice_fusion
  47.7 4.3 convolution_bitcast_fusion.2
  52.0 0.0 copy-start.2
  52.0 0.0 all-reduce.3.cloned.1.call-update
  52.0 0.0 all-gather.13.cloned.1.call-start
  52.1 1.2 copy-done.2
  53.3 0.1 broadcast_multiply_fusion.2
  53.4 0.4 copy.43
  53.7 203.3 %all-reduce.3.cloned.1.call-done = (f32[2304,1152]{0,1:T(8,128)}, f32[768,1152]{0,1:T(8,128)}, f32[768,384]{0,1:T(8,128)}) async-done(((f32[2304,1152]{0,1:T(8,128)}, f32[768,1152]{0,1:T(8,128)}, f32[768,384]{0,1:T(8,128)}), (f32[2304,1152]{0,1:T(8,128)}, f32[768,1152]{0,1:T(8,128)}, f32[768,384]{0,1:T(8,128)})) %all-reduce.3.cloned.1.call-update) | async-done | bytes 15335440 | tf_op jit(solution)/shard_map/psum | solution.py:186
  257.0 2.5 bitcast_add_fusion.1
  259.5 0.0 all-gather.13.cloned.1.call-update
  259.6 0.0 all-gather.11.cloned.1.call-start
  259.6 4.0 broadcast_multiply_fusion.1
  263.6 0.0 all-gather.11.cloned.1.call-update
  263.7 0.0 all-gather.9.cloned.1.call-start
  263.7 9.1 %broadcast_multiply_fusion = f32[2304,9,128]{2,0,1:T(8,128)} fusion(f32[2304,9,128]{2,0,1:T(8,128)} %param.9), kind=kLoop, calls=%fused_computation.3 | loop fusion | flops 2654208 | bytes 21233664 | tf_op jit(solution)/shard_map/mul | solution.py:188
  272.8 12.7 %copy.40 = f32[2304,9,128]{0,2,1:T(8,128)} copy(f32[2304,9,128]{2,0,1:T(8,128)} %broadcast_multiply_fusion) | data formatting | bytes 21233664 | tf_op jit(solution)/shard_map/mul | solution.py:188
  285.4 12.0 %bitcast_add_fusion = f32[2304,1152]{0,1:T(8,128)} fusion(f32[2304,9,128]{0,2,1:T(8,128)} %copy.40, f32[2304,1152]{0,1:T(8,128)} %get-tuple-element.15), kind=kLoop, calls=%fused_computation.1 | loop fusion | flops 5308416 | bytes 31850496 | tf_op jit(solution)/shard_map/add | solution.py:188
  297.4 0.0 all-gather.9.cloned.1.call-update
  297.4 0.2 all-gather.15.cloned.1.call-start
  297.7 0.7 and_select_fusion.b_ref
  298.4 0.0 all-gather.13.cloned.1.call-done
  298.4 3.0 reshape.119
  301.4 3.1 copy.45
  304.6 4.1 reshape.120.s_ref
  308.7 30.9 %spd_solve.2 = f32[3,8,256]{2,1,0:T(8,128)} custom-call(f32[3,768,256]{2,1,0:T(8,128)} %reshape.120.s_ref, f32[3,8,256]{2,1,0:T(8,128)} %and_select_fusion.b_ref), custom_call_target="tpu_custom_call" | custom-call | tf_op jit(solution)/shard_map/spd_solve/pallas_call | solution.py:152
  339.6 0.0 copy-start.3
  339.6 0.0 all-gather.11.cloned.1.call-done
  339.6 8.0 %copy.53 = f32[1536,1152]{1,0:T(8,128)} copy(f32[1536,1152]{0,1:T(8,128)} %all-gather.11.cloned.1.call-done) | data formatting | bytes 14155776 | tf_op jit(solution)/shard_map/all_gather | solution.py:197
  347.6 0.0 copy-done.3
  347.6 5.8 convolution_bitcast_fusion.3
  353.4 0.6 copy.57
  354.1 0.0 all-gather.9.cloned.1.call-done
  354.1 24.5 %reshape.115 = f32[2,2304,9,128]{1,0,3,2:T(2,128)} reshape(f32[4608,1152]{0,1:T(8,128)} %all-gather.9.cloned.1.call-done) | data formatting | bytes 42467328 | tf_op jit(solution)/shard_map/reshape | solution.py:167
  378.6 37.6 %copy.42 = f32[2,2304,9,128]{3,0,1,2:T(2,128)} copy(f32[2,2304,9,128]{1,0,3,2:T(2,128)} %reshape.115) | data formatting | bytes 42467328 | tf_op jit(solution)/shard_map/reshape | solution.py:167
  416.2 26.9 %reshape.116.s_ref = f32[9,2304,256]{2,1,0:T(8,128)} reshape(f32[9,2304,2,128]{3,2,1,0:T(2,128)} %bitcast.53) | data formatting | bytes 42467328 | tf_op jit(solution)/shard_map/reshape | solution.py:168
  443.1 160.1 %spd_solve.3 = f32[9,8,256]{2,1,0:T(8,128)} custom-call(f32[9,2304,256]{2,1,0:T(8,128)} %reshape.116.s_ref, f32[9,8,256]{2,1,0:T(8,128)} %bitcast.65), custom_call_target="tpu_custom_call" | custom-call | tf_op jit(solution)/shard_map/spd_solve/pallas_call | solution.py:152
  603.2 0.0 all-gather.15.cloned.1.call-update
  603.3 3.3 copy.49
  606.6 12.6 %copy.52 = f32[2304,9,128]{2,0,1:T(8,128)} copy(f32[2304,9,128]{0,2,1:T(8,128)} %bitcast.52) | data formatting | bytes 21233664
  619.2 2.7 copy.51
  621.9 49.6 %all-gather.15.cloned.1.call-done = f32[576,6,256]{2,1,0:T(8,128)} async-done(((f32[9,6,256]{2,1,0:T(8,128)}), f32[576,6,256]{2,1,0:T(8,128)}) %all-gather.15.cloned.1.call-update) | async-done | bytes 3538960 | tf_op jit(solution)/shard_map/all_gather | solution.py:201
  671.5 6.9 copy.56
  678.4 6.0 reshape.124
  684.4 4.2 sub.8
  688.5 5.1 copy.50
  (3 shorter events, 0.0 us)
Async XLA Ops:
  7.2 249.9 %all-reduce.3.cloned.1.call-start = ((), (), s32[]{:S(2)}) async-start(), calls=%async_computation.4 | async-start | bytes 30670848 | tf_op jit(solution)/shard_map/psum | solution.py:186
  19.8 5.1 copy-start
  24.9 13.7 %copy-start.1 = (bf16[2048,768]{1,0:T(8,128)(2,1)S(1)}, bf16[2048,768]{1,0:T(8,128)(2,1)}, u32[]{:S(2)}) copy-start(bf16[2048,768]{1,0:T(8,128)(2,1)} %param.5) | copy-start | bytes 9437188
  52.0 1.3 copy-start.2
  52.0 246.4 %all-gather.13.cloned.1.call-start = ((), (), s32[]{:S(2)}) async-start(), calls=%async_computation.2 | async-start | bytes 3538944 | tf_op jit(solution)/shard_map/all_gather | solution.py:167
  259.6 80.0 %all-gather.11.cloned.1.call-start = ((), (), s32[]{:S(2)}) async-start(), calls=%async_computation.1 | async-start | bytes 10616832 | tf_op jit(solution)/shard_map/all_gather | solution.py:197
  263.7 90.4 %all-gather.9.cloned.1.call-start = ((), (), s32[]{:S(2)}) async-start(), calls=%async_computation | async-start | bytes 31850496 | tf_op jit(solution)/shard_map/all_gather | solution.py:167
  297.4 374.1 %all-gather.15.cloned.1.call-start = ((), (), s32[]{:S(2)}) async-start(), calls=%async_computation.3 | async-start | bytes 4792320 | tf_op jit(solution)/shard_map/all_gather | solution.py:201
  339.6 8.0 %copy-start.3 = (f32[3,8,256]{2,1,0:T(8,128)S(1)}, f32[3,8,256]{2,1,0:T(8,128)}, u32[]{:S(2)}) copy-start(f32[3,8,256]{2,1,0:T(8,128)} %spd_solve.2) | copy-start | bytes 73732
Sparse Core Ops, SparseCore 0:
  52.1 204.8 all-reduce.2
  259.7 12.8 all-gather.12
  274.8 22.7 all-gather.10
  299.1 40.3 all-gather.8
  603.4 68.0 all-gather.14

commit v2 on v1

v2 whole, which is shorter than its diff:
```python
import functools
import math
import numpy as np
import jax
import jax.numpy as jnp
from jax import lax
from jax.experimental import pallas as pl
from jax.experimental.pallas import tpu as pltpu
from jax.sharding import PartitionSpec as P

FACTOR_DECAY = 0.95
DAMPING = 0.001
DAMP_SHIFT = math.sqrt(DAMPING)
LEARN_RATE = 1.0
BW = 128
PW = 256
RING = 4
F32 = jnp.float32
BF = jnp.bfloat16
NT = (((1,), (1,)), ((), ()))
NN = (((1,), (0,)), ((), ()))


def bc(x, shape=(8, BW)):
    return jnp.broadcast_to(x, shape)

def factor_block(mat, linv, mb=16):
    lane = lax.broadcasted_iota(jnp.int32, (8, BW), 1)
    sub = lax.broadcasted_iota(jnp.int32, (8, BW), 0)
    for t in range(BW // mb):
        k = t * mb
        nr = mb // 8
        rows = [mat[k + 8 * r:k + 8 * r + 8, :] for r in range(nr)]
        cols = [[bc(rows[r][:, k + i:k + i + 1]) for r in range(nr)] for i in range(mb)]
        inside = (lane >= k) & (lane < k + mb)
        ext = [jnp.where(inside, jnp.where(lane == sub + (k + 8 * r), 1.0, 0.0), rows[r]) for r in range(nr)]
        rv = [jnp.zeros((8, BW), F32) for _ in range(nr)]
        below = list(range((k + mb) // 8, BW // 8))
        old = {r: mat[8 * r:8 * r + 8, :] for r in below}
        for j in range(mb):
            jr, js = divmod(j, 8)
            piv = bc(cols[j][jr][js:js + 1, :])
            rinv = 1.0 / piv
            prow = bc(ext[jr][js:js + 1, :])
            linv[k + j:k + j + 1, :] = (prow * lax.rsqrt(piv))[0:1, :]
            here = sub == js
            mask = [jnp.where(here, 0.0, cols[j][r]) if r == jr else cols[j][r] for r in range(nr)]
            fac = [mask[r] * rinv for r in range(nr)]
            for i in range(j + 1, mb):
                b = bc(cols[i][jr][js:js + 1, :])
                if i == j + 1:
                    cols[i] = [cols[i][r] - (mask[r] * b) * rinv for r in range(nr)]
                else:
                    cols[i] = [cols[i][r] - fac[r] * b for r in range(nr)]
            ext = [ext[r] - fac[r] * prow for r in range(nr)]
            rv[jr] = jnp.where(here, rinv, rv[jr])
        w = [ext[r] * rv[r] for r in range(nr)]
        for r in below:
            acc = jnp.where(inside, 0.0, old[r])
            for j in range(mb):
                jr, js = divmod(j, 8)
                acc = acc - bc(old[r][:, k + j:k + j + 1]) * bc(w[jr][js:js + 1, :])
            mat[8 * r:8 * r + 8, :] = acc
    ri = lax.broadcasted_iota(jnp.int32, (BW, BW), 0)
    ci = lax.broadcasted_iota(jnp.int32, (BW, BW), 1)
    linv[...] = jnp.where(ci <= ri, linv[...], 0.0)


def split3(x):
    h = x.astype(BF)
    r = x - h.astype(F32)
    m = r.astype(BF)
    return h, m, (r - m.astype(F32)).astype(BF)

def dot6(a, b, dims):
    d = lambda x, y: lax.dot_general(x, y, dims, preferred_element_type=F32)
    ah, am, al = a
    bh, bm, bl = b
    return (d(am, bm) + d(ah, bl) + d(al, bh)) + (d(ah, bm) + d(am, bh)) + d(ah, bh)

def dotf(a, b, dims):
    return dot6(split3(a), split3(b), dims)


def coords():
    d = lax.axis_index('dp')
    x = lax.rem(d, RING)
    y = lax.rem(lax.div(d, RING), RING)
    z = lax.div(d, RING * RING)
    return d, (x, y, z)

def neighbour(d, pos, axis, step):
    stride = (1, RING, RING * RING)[axis]
    return d + (lax.rem(pos[axis] + step, RING) - pos[axis]) * stride

def axis_of(part, phase):
    return (part + phase) % 3

def entry_barrier(d, pos, partner):
    sem = pltpu.get_barrier_semaphore()
    count = 0
    for axis in range(3):
        for step in (1, 3):
            pl.semaphore_signal(sem, inc=1, device_id={'dp': neighbour(d, pos, axis, step)}, device_id_type=pl.DeviceIdType.MESH)
            count += 1
    if partner is not None:
        pl.semaphore_signal(sem, inc=1, device_id={'mp': partner}, device_id_type=pl.DeviceIdType.MESH)
        count += 1
    pl.semaphore_wait(sem, count)

def remote(src, dst, ssem, rsem, dev):
    return pltpu.make_async_remote_copy(src_ref=src, dst_ref=dst, send_sem=ssem, recv_sem=rsem, device_id={'dp': dev}, device_id_type=pl.DeviceIdType.MESH)

def each(lo, hi, fn):
    def body(i, c):
        fn(i)
        return c
    lax.fori_loop(lo, hi, body, 0)

def decode(b, np_in, np_out):
    n_in, n_out = 2 * np_in, 2 * np_out
    starts, at = [], 0
    for q0, base_row, base_col, n in [(0, n_in, np_in, n_out)] + [(q, 0, 0, n_in) for q in range(np_in)] + [(q, n_in, np_in, n_out) for q in range(1, np_out)]:
        starts.append((at, base_row + 2 * q0 - at, base_col + q0))
        at += n - 2 * q0
    row, col, was = b, 0, (0, 0)
    for z, (first, d_row, d_col) in enumerate(starts):
        hit = 1 if z == 0 else (b >= first).astype(jnp.int32)
        row = row + hit * (d_row - was[0])
        col = col + hit * (d_col - was[1])
        was = (d_row, d_col)
    is_g = (b >= at).astype(jnp.int32)
    g_row, g_col = lax.rem(b - at * is_g, n_in), np_in + lax.div(b - at * is_g, n_in)
    row = row + is_g * (g_row - row)
    col = col + is_g * (g_col - col)
    in_s = (col >= np_in).astype(jnp.int32)
    old = in_s * ((col - np_in) * n_out + row - n_in) + (1 - in_s) * (np_out * n_out + col * n_in + row)
    return row, col, (1 - is_g) * old, is_g

def stats_kernel(nm, ns, c_in, c_out, a_hbm, g_hbm, s_hbm, ao_hbm, share, ag, agt, old, acc, ra1, rb1, rc1, rd1, ra2, rb2, rc2, rd2, ra3, rb3, rc3, rd3, lsem, ssem, rsem):
    p = lax.axis_index('mp')
    d, pos = coords()
    n_in, n_out = c_in // BW, c_out // BW
    n_all = ns * RING**3
    nso = s_hbm.shape[0]
    loads = [pltpu.make_async_copy(a_hbm, ag.at[:, 0:c_in], lsem.at[0]), pltpu.make_async_copy(g_hbm, ag.at[:, c_in:c_in + c_out], lsem.at[1]),
        pltpu.make_async_copy(s_hbm, old.at[0:nso], lsem.at[2]), pltpu.make_async_copy(ao_hbm, old.at[nso:nso + ao_hbm.shape[0]], lsem.at[3])]
    for c in loads:
        c.start()
    entry_barrier(d, pos, None)
    ck = min(512, ns)
    for z, (base, cnt) in enumerate(((0, n_in), (n_in, n_out))):
        loads[z].wait()
        def flip(c):
            for r in range(ns // ck):
                agt[base + c, :, r * ck:(r + 1) * ck] = ag[r * ck:(r + 1) * ck, pl.ds(pl.multiple_of((base + c) * BW, BW), BW)].T
        each(0, cnt, flip)
    loads[2].wait()
    loads[3].wait()

    def quarter(rel):
        def body(m):
            for part in range(3):
                c1 = lax.rem(pos[axis_of(part, 0)] + rel, RING)
                b = (m * 3 + part) * RING + c1
                row, col, at, is_g = decode(b, n_in // 2, n_out // 2)
                w_new = jnp.where(is_g == 1, 1.0 / n_all, (1.0 - FACTOR_DECAY) / n_all)
                w_old = jnp.where(is_g == 1, 0.0, FACTOR_DECAY / RING**3)
                rhs = ag[:, pl.ds(pl.multiple_of((2 * col + p) * BW, BW), BW)]
                prod = lax.dot_general(agt[row], rhs, NN, preferred_element_type=F32)
                acc[part, m, c1] = prod * w_new + old[at] * w_old
        each(0, nm, body)

    def hop(part, phase, step):
        return neighbour(d, pos, axis_of(part, phase), step)

    def both(k, part, phase, pairs):
        out = []
        for z, (step, src, dst) in enumerate(pairs):
            s = (k * 3 + part) * 2 + z
            c = remote(src, dst, ssem.at[s], rsem.at[s], hop(part, phase, step))
            c.start()
            out.append(c)
        return out

    cs = [[pos[axis_of(part, ph)] for ph in range(3)] for part in range(3)]
    rel = lambda part, ph, k: lax.rem(cs[part][ph] + k, RING)
    copies = []
    quarter(2)
    s1 = []
    for part in range(3):
        o = rel(part, 0, 2)
        s1.append(both(0, part, 0, [(1, acc.at[part, :, o, 0:64], ra1.at[part]), (3, acc.at[part, :, o, 64:128], rb1.at[part])]))
    quarter(1)
    s2 = []
    for z, k in enumerate((1, 3)):
        if z == 1:
            quarter(3)
        for part in range(3):
            u = rel(part, 0, k)
            s1[part][z].wait_recv()
            src = (ra1, rb1)[z]
            lo = 64 * z
            def body(m):
                acc[part, m, u, lo:lo + 64] = acc[part, m, u, lo:lo + 64] + src[part, m]
            each(0, nm, body)
            n = (3 + part) * 2 + z
            c = remote(acc.at[part, :, u], (rc1, rd1)[z].at[part], ssem.at[n], rsem.at[n], hop(part, 0, k))
            c.start()
            s2.append(c)
    quarter(0)
    for part in range(3):
        c1 = cs[part][0]
        s2[part].wait_recv()
        s2[3 + part].wait_recv()
        def body(m):
            acc[part, m, c1] = acc[part, m, c1] + (rc1[part, m] + rd1[part, m])
        each(0, nm, body)
        o = pl.multiple_of(rel(part, 1, 2) * 32, 32)
        copies.append(both(2, part, 1, [(1, acc.at[part, :, c1, pl.ds(o, 16)], ra2.at[part]), (3, acc.at[part, :, c1, pl.ds(o + 16, 16)], rb2.at[part])]))
    p2 = []
    for part in range(3):
        c1 = cs[part][0]
        lst = []
        for z, k in enumerate((1, 3)):
            u = pl.multiple_of(rel(part, 1, k) * 32, 32)
            copies[part][z].wait_recv()
            src = (ra2, rb2)[z]
            def body(m):
                r = pl.ds(pl.multiple_of(u + 16 * z, 16), 16)
                acc[part, m, c1, r] = acc[part, m, c1, r] + src[part, m]
            each(0, nm, body)
            n = (9 + part) * 2 + z
            c = remote(acc.at[part, :, c1, pl.ds(u, 32)], (rc2, rd2)[z].at[part], ssem.at[n], rsem.at[n], hop(part, 1, k))
            c.start()
            lst.append(c)
        p2.append(lst)
    h = (nm + 1) // 2
    p3 = []
    for part in range(3):
        c1 = cs[part][0]
        e = pl.multiple_of(cs[part][1] * 32, 32)
        for c in p2[part]:
            c.wait_recv()
        def body(m):
            acc[part, m, c1, pl.ds(e, 32)] = acc[part, m, c1, pl.ds(e, 32)] + (rc2[part, m] + rd2[part, m])
        each(0, nm, body)
        o = pl.multiple_of(e + rel(part, 2, 2) * 8, 8)
        p3.append(both(4, part, 2, [(1, acc.at[part, 0:h, c1, pl.ds(o, 8)], ra3.at[part]), (3, acc.at[part, h:nm, c1, pl.ds(o, 8)], rb3.at[part])]))
    p4 = []
    for part in range(3):
        c1 = cs[part][0]
        e = pl.multiple_of(cs[part][1] * 32, 32)
        lst = []
        for z, k in enumerate((1, 3)):
            u = pl.multiple_of(e + rel(part, 2, k) * 8, 8)
            p3[part][z].wait_recv()
            for m in range(h if z == 0 else nm - h):
                mm = m + h * z
                acc[part, mm, c1, pl.ds(u, 8)] = acc[part, mm, c1, pl.ds(u, 8)] + (ra3, rb3)[z][part, m]
            n = (15 + part) * 2 + z
            c = remote(acc.at[part, :, c1, pl.ds(u, 8)], (rc3, rd3)[z].at[part], ssem.at[n], rsem.at[n], hop(part, 2, k))
            c.start()
            lst.append(c)
        p4.append(lst)
    for part in range(3):
        c1 = cs[part][0]
        f = pl.multiple_of(cs[part][1] * 32 + cs[part][2] * 8, 8)
        for c in p4[part]:
            c.wait_recv()
        for m in range(nm):
            share[part, m] = acc[part, m, c1, pl.ds(f, 8)] + (rc3[part, m] + rd3[part, m])
    for group in (s1, copies, p2, p3, p4):
        for lst in group:
            for c in lst:
                c.wait_send()
    for c in s2:
        c.wait_send()

def stats(a_loc, g_loc, a_old3, s_old3):
    ns, c_in = a_loc.shape
    c_out = g_loc.shape[1]
    np_in, np_out = c_in // 256, c_out // 256
    nb = (np_in + np_out) * (np_in + np_out + 1)
    nm = nb // 12
    assert nm * 12 == nb
    h = (nm + 1) // 2
    hb = pl.BlockSpec(memory_space=pl.ANY)
    V = pltpu.VMEM
    s_blk = s_old3.reshape(-1, BW, BW)
    a_blk = a_old3.reshape(-1, BW, BW)
    return pl.pallas_call(functools.partial(stats_kernel, nm, ns, c_in, c_out),
        out_shape=jax.ShapeDtypeStruct((3, nm, 8, BW), F32),
        in_specs=[hb, hb, hb, hb], out_specs=pl.BlockSpec(memory_space=V),
        scratch_shapes=[V((ns, c_in + c_out), BF), V(((c_in + c_out) // BW, BW, ns), BF), V((s_blk.shape[0] + a_blk.shape[0], BW, BW), F32), V((3, nm, 4, BW, BW), F32),
            V((3, nm, 64, BW), F32), V((3, nm, 64, BW), F32), V((3, nm, 128, BW), F32), V((3, nm, 128, BW), F32),
            V((3, nm, 16, BW), F32), V((3, nm, 16, BW), F32), V((3, nm, 32, BW), F32), V((3, nm, 32, BW), F32),
            V((3, h, 8, BW), F32), V((3, nm - h, 8, BW), F32), V((3, nm, 8, BW), F32), V((3, nm, 8, BW), F32),
            pltpu.SemaphoreType.DMA((4,)), pltpu.SemaphoreType.DMA((36,)), pltpu.SemaphoreType.DMA((36,))],
        compiler_params=pltpu.CompilerParams(collective_id=0, has_side_effects=True, vmem_limit_bytes=63 * 2**20), name="stats_rs")(a_loc, g_loc, s_blk, a_blk)


def stack_dot(x, w, dims):
    xh, xm, xl = split3(x)
    wh, wm, wl = split3(w)
    k = x.shape[0]
    d = lambda u, v: lax.dot_general(u, v, dims, preferred_element_type=F32)
    p1 = d(jnp.concatenate([xh, xm, xl], 0), wh)
    p2 = d(jnp.concatenate([xh, xm], 0), wm)
    p3 = d(xh, wl)
    return (p1[2 * k:3 * k] + p2[k:2 * k] + p3) + (p1[k:2 * k] + p2[0:k]) + p1[0:k]

def solve_all_kernel(nm, np_in, np_out, n_dp, damp, share, x_out, a_out, s_out, full, tmat, mat, linv, inv_all, pan, pant, xw, zin, stage, ssem, rsem, psem, osem):
    p = lax.axis_index('mp')
    q_partner = 1 - p
    d, pos = coords()
    n_own = np_in * BW // n_dp
    cs = [[pos[axis_of(part, ph)] for ph in range(3)] for part in range(3)]
    own_rows = [pl.ds(pl.multiple_of(cs[part][1] * 32 + cs[part][2] * 8, 8), 8) for part in range(3)]
    for part in range(3):
        def put(m):
            full[p, m, part, cs[part][0], own_rows[part]] = share[part, m]
        each(0, nm, put)
    entry_barrier(d, pos, q_partner)
    pend = []

    def ag_round(k, m0, m1):
        ms = pl.ds(m0, m1 - m0)
        mh = m0 + (m1 - m0 + 1) // 2
        ma, mb = pl.ds(m0, mh - m0), pl.ds(mh, m1 - mh)
        def go(n, part, phase, step, ref):
            s = k * 36 + n
            c = remote(ref, ref, ssem.at[s], rsem.at[s], neighbour(d, pos, axis_of(part, phase), step))
            c.start()
            pend.append(c)
            return c
        for phase in (2, 1, 0):
            def piece(part, coord, half):
                c1, e = cs[part][0], cs[part][1]
                if phase == 2:
                    r = pl.ds(pl.multiple_of(e * 32 + coord * 8, 8), 8)
                    return full.at[p, (ms, ma, mb)[0 if half is None else half + 1], part, c1, r]
                if phase == 1:
                    r = pl.ds(pl.multiple_of(coord * 32 + (16 if half == 1 else 0), 16), 32 if half is None else 16)
                    return full.at[p, ms, part, c1, r]
                if half is None:
                    return full.at[p, ms, part, coord]
                return full.at[p, ms, part, coord, pl.ds(64 * half, 64)]
            first = []
            for part in range(3):
                c = cs[part][phase]
                n = (phase * 3 + part) * 4
                first.append([go(n, part, phase, 1, piece(part, c, None)), go(n + 1, part, phase, 3, piece(part, c, None))])
            second = []
            for part in range(3):
                c = cs[part][phase]
                n = (phase * 3 + part) * 4
                up, dn = lax.rem(c + 1, RING), lax.rem(c + 3, RING)
                first[part][0].wait_recv()
                second.append(go(n + 2, part, phase, 1, piece(part, dn, 0)))
                first[part][1].wait_recv()
                second.append(go(n + 3, part, phase, 3, piece(part, up, 1)))
            for c in second:
                c.wait_recv()
        ref = full.at[p, ms]
        c = pltpu.make_async_remote_copy(src_ref=ref, dst_ref=ref, send_sem=psem.at[0, k], recv_sem=psem.at[1, k], device_id={'mp': q_partner}, device_id_type=pl.DeviceIdType.MESH)
        c.start()
        pend.append(c)
        return c

    x1 = ag_round(0, 0, nm)
    x1.wait_recv()

    def block(par, b):
        return full[par, lax.div(b, 12), lax.div(lax.rem(b, 12), 4), lax.rem(b, 4)]

    n_in, n_out = 2 * np_in, 2 * np_out
    base_a = n_out
    base_s1 = n_out + np_in * (np_in + 1)
    base_g = base_s1 + np_out * (np_out + 1) - n_out
    def s_base(q):
        return q * n_out - q * (q - 1) + (base_s1 - n_out) * jnp.minimum(q, 1)
    def a_base(q):
        return base_a + q * n_in - q * (q - 1)
    is_a = p
    npan = np_out - (np_out - np_in) * p

    eye = jnp.where(lax.broadcasted_iota(jnp.int32, (BW, BW), 0) == lax.broadcasted_iota(jnp.int32, (BW, BW), 1), damp, 0.0)
    def load(q):
        base = is_a * a_base(q) + (1 - is_a) * s_base(q)
        for par in range(2):
            def rows(i):
                tmat[q, pl.ds(pl.multiple_of(i * BW, BW), BW), par * BW:(par + 1) * BW] = block(par, base + i - 2 * q)
            each(2 * q, 2 * npan, rows)
            r = pl.ds(pl.multiple_of((2 * q + par) * BW, BW), BW)
            tmat[q, r, par * BW:(par + 1) * BW] = tmat[q, r, par * BW:(par + 1) * BW] + eye
    each(0, npan, load)

    def panel(k):
        q = lax.div(k, 2)
        h = lax.rem(k, 2)
        r0 = pl.multiple_of(q * PW, PW)
        @pl.when(h == 0)
        def _():
            mat[...] = tmat[q, pl.ds(r0, BW), 0:BW]
        factor_block(mat, linv)
        @pl.when(h == 0)
        def _():
            inv0 = linv[...]
            inv0s = split3(inv0)
            l10 = dot6(split3(tmat[q, pl.ds(r0 + BW, BW), 0:BW]), inv0s, NT)
            l10s = split3(l10)
            mat[...] = tmat[q, pl.ds(r0 + BW, BW), BW:PW] - dot6(l10s, l10s, NT)
            inv_all[q, 0:BW, 0:BW] = inv0
            inv_all[q, 0:BW, BW:PW] = jnp.zeros((BW, BW), F32)
            inv_all[q, BW:PW, 0:BW] = dot6(l10s, inv0s, NN)
        @pl.when(h == 1)
        def _():
            inv1 = linv[...]
            inv_all[q, BW:PW, BW:PW] = inv1
            inv_all[q, BW:PW, 0:BW] = -dotf(inv1, inv_all[q, BW:PW, 0:BW], NN)
            invs = split3(inv_all[q])
            def below(i):
                r = pl.ds(pl.multiple_of(i * PW, PW), PW)
                lo = dot6(split3(tmat[q, r, :]), invs, NT)
                tmat[q, r, :] = lo
                sp = split3(lo)
                st = split3(lo.T)
                for z in range(3):
                    pan[z, r, :] = sp[z]
                    pant[z, i] = st[z]
            each(q + 1, npan, below)
            def trail(j):
                w = [pant[z, j] for z in range(3)]
                def rows(i):
                    r = pl.ds(pl.multiple_of(i * PW, PW), PW)
                    tmat[j, r, :] = tmat[j, r, :] - dot6([pan[z, r, :] for z in range(3)], w, NN)
                each(j, npan, rows)
            each(q + 1, npan, trail)
    each(0, 2 * npan, panel)

    zcopy = pltpu.make_async_remote_copy(src_ref=zin.at[0], dst_ref=zin.at[1], send_sem=psem.at[0, 2], recv_sem=psem.at[1, 2], device_id={'mp': q_partner}, device_id_type=pl.DeviceIdType.MESH)

    @pl.when(p == 1)
    def _():
        row = lax.broadcasted_iota(jnp.int32, (16, PW), 0)
        lane = lax.broadcasted_iota(jnp.int32, (16, PW), 1)
        par = lax.div(row, 8)
        idx = lax.rem(row, 8)
        col = d * n_own + idx
        for q in range(np_in):
            hit = (idx < n_own) & (lax.div(col, BW) == q) & (lane == par * BW + lax.rem(col, BW))
            xw[q] = jnp.where(hit, 1.0, 0.0)
    @pl.when(p == 0)
    def _():
        zcopy.wait_recv()
        def cp(q):
            xw[q] = zin[1, q]
        each(0, np_out, cp)

    def fwd(q):
        y = stack_dot(xw[q], inv_all[q], NT)
        xw[q] = y
        def sub(j):
            xw[j] = xw[j] - stack_dot(y, tmat[q, pl.ds(pl.multiple_of(j * PW, PW), PW), :], NT)
        each(q + 1, npan, sub)
    each(0, npan, fwd)
    def back(s):
        q = npan - 1 - s
        def sub(i, acc):
            return acc - stack_dot(xw[i], tmat[q, pl.ds(pl.multiple_of(i * PW, PW), PW), :], NN)
        xw[q] = stack_dot(lax.fori_loop(q + 1, npan, sub, xw[q]), inv_all[q], NN)
    each(0, npan, back)

    @pl.when(p == 1)
    def _():
        def zq(q):
            for par in range(2):
                acc = jnp.zeros((16, BW), F32)
                for i in range(n_in):
                    acc = acc + stack_dot(xw[i // 2, :, (i % 2) * BW:(i % 2 + 1) * BW], block(par, base_g + q * n_in + i), NN)
                zin[0, q, :, par * BW:(par + 1) * BW] = acc
        each(0, np_out, zq)
        zcopy.start()

    def column(out, slot, n_blk, par, q, base_fn):
        def lower(i):
            stage[slot, pl.ds(pl.multiple_of(i * BW, BW), BW), :] = block(par, base_fn(q) + i - 2 * q)
        each(2 * q, n_blk, lower)
        def upper(q2):
            for par2 in range(2):
                i = 2 * q2 + par2
                stage[slot, pl.ds(pl.multiple_of(i * BW, BW), BW), :] = block(par2, base_fn(q2) + (2 * q + par) - 2 * q2).T
        each(0, q, upper)

    def remote_out(slot, rows, out, q, s):
        return pltpu.make_async_remote_copy(src_ref=stage.at[slot, pl.ds(0, rows)], dst_ref=out.at[q], send_sem=osem.at[0, s], recv_sem=osem.at[1, s], device_id={'mp': 0}, device_id_type=pl.DeviceIdType.MESH)
    jobs = [(s_out, n_out, q, s_base) for q in range(np_out)] + [(a_out, n_in, q, a_base) for q in range(np_in)]
    @pl.when(p == 1)
    def _():
        live = {}
        for z, (out, n_blk, q, fn) in enumerate(jobs):
            for par in range(2):
                slot = (2 * z + par) % 4
                if slot in live:
                    live[slot]()
                column(out, slot, n_blk, par, q, fn)
                if par == 0:
                    c = remote_out(slot, n_blk * BW, out, q, z)
                    c.start()
                    live[slot] = c.wait_send
                else:
                    c = pltpu.make_async_copy(stage.at[slot, pl.ds(0, n_blk * BW)], out.at[q], osem.at[0, len(jobs) + z])
                    c.start()
                    live[slot] = c.wait
        for fn in live.values():
            fn()
        zcopy.wait_send()

    xcopy = pltpu.make_async_remote_copy(src_ref=zin.at[0, :, pl.ds(8, 8)], dst_ref=x_out, send_sem=psem.at[0, 3], recv_sem=psem.at[1, 3], device_id={'mp': q_partner}, device_id_type=pl.DeviceIdType.MESH)
    @pl.when(p == 0)
    def _():
        def cp(q):
            zin[0, q] = xw[q]
            x_out[q] = xw[q, 0:8]
        each(0, np_out, cp)
        xcopy.start()
        for z, (out, n_blk, q, fn) in enumerate(jobs):
            remote_out(0, n_blk * BW, out, q, z).wait_recv()
        xcopy.wait_send()
    @pl.when(p == 1)
    def _():
        xcopy.wait_recv()
    for c in pend:
        c.wait_send()

def solve_all(share, np_in, np_out, n_dp, damp):
    nm = share.shape[1]
    n_in, n_out = 2 * np_in, 2 * np_out
    hb = pl.BlockSpec(memory_space=pl.ANY)
    V = pltpu.VMEM
    vb = pl.BlockSpec(memory_space=V)
    njob = np_in + np_out
    return pl.pallas_call(functools.partial(solve_all_kernel, nm, np_in, np_out, n_dp, damp),
        out_shape=(jax.ShapeDtypeStruct((np_out, 8, PW), F32), jax.ShapeDtypeStruct((np_in, n_in * BW, BW), F32), jax.ShapeDtypeStruct((np_out, n_out * BW, BW), F32)),
        in_specs=[vb], out_specs=(vb, hb, hb),
        scratch_shapes=[V((2, nm, 3, 4, BW, BW), F32), V((np_out, n_out * BW, PW), F32), V((BW, BW), F32), V((BW, BW), F32), V((np_out, PW, PW), F32),
            V((3, n_out * BW, PW), BF), V((3, np_out, PW, PW), BF), V((np_out, 16, PW), F32), V((2, np_out, 16, PW), F32), V((4, n_out * BW, BW), F32),
            pltpu.SemaphoreType.DMA((36,)), pltpu.SemaphoreType.DMA((36,)), pltpu.SemaphoreType.DMA((2, 4)), pltpu.SemaphoreType.DMA((2, 2 * njob))],
        compiler_params=pltpu.CompilerParams(collective_id=1, has_side_effects=True, vmem_limit_bytes=63 * 2**20), name="factor_solve")(share)


def solution(mesh):
    n_dp = mesh.shape['dp']

    def local_step(a_loc, g_loc, w_loc, a_old_loc, s_old_loc):
        np_in = a_loc.shape[1] // PW
        np_out = g_loc.shape[1] // PW
        share = stats(a_loc, g_loc, a_old_loc.transpose(1, 0, 2), s_old_loc.transpose(1, 0, 2))
        xt, a3, s3 = solve_all(share, np_in, np_out, n_dp, DAMP_SHIFT)
        n_own = np_in * BW // n_dp
        delta = lax.all_gather(xt[:, :n_own, :], 'dp').transpose(1, 3, 0, 2).reshape(w_loc.shape)
        return (w_loc - LEARN_RATE * delta, a3.transpose(1, 0, 2), s3.transpose(1, 0, 2))

    spec_rows = P('dp', None)
    spec_cyc = P(None, 'mp', None)
    return jax.shard_map(local_step, mesh=mesh, in_specs=(spec_rows, spec_rows, spec_cyc, spec_cyc, spec_cyc), out_specs=(spec_cyc, spec_cyc, spec_cyc), check_vma=False)
```

time: 704 us -> 410 us (0.58)
  waiting for transfers between devices: 253 us -> 63.3 us
  local copies, waits for them, and re-layouts: 180 us -> 31.3 us
  Pallas kernels: 191 us -> 297 us
  matrix products: 29.5 us -> 0 us
  other arithmetic: 32.5 us -> 4.19 us
    psum x1 -> x0, waiting for transfers between devices: 203 us -> none  [local_step(): a_sum, s_sum, gt_sum = lax.psum((a_part, s_part, gt_part), 'dp')]
    pallas_call x2, Pallas kernels: 191 us -> 297 us  [the longest x1 214 us: solve_all(): pl.pallas_call(functools.partial(solve_all_kernel, nm, np_in, np_out, n_d...]
    reshape x8 -> x1, local copies, waits for them, and re-layouts: 106 us -> 5.98 us  [local_step(): lax.all_gather(xt[:, :n_own, :], 'dp').transpose(1, 3, 0, 2)]
    dot_general x4 -> x0, matrix products: 29.5 us -> none  [the longest x1 13.7 us: local_step(): s_part = jnp.einsum('no,nc->oc', g_loc, g_mine, preferred_element_type=F32)]
    unnamed x14 -> x6, local copies, waits for them, and re-layouts: 42.9 us -> 18.4 us
    add x3 -> x0, other arithmetic: 14.5 us -> none  [the longest x1 12 us: local_step(): FACTOR_DECAY * s_old_loc.reshape(d_out, -1)]
    all_gather x4 -> x1, waiting for transfers between devices: 49.6 us -> 63.3 us  [local_step(): lax.all_gather(xt[:, :n_own, :], 'dp').transpose(1, 3, 0, 2)]
    mul x2 -> x0, local copies, waits for them, and re-layouts: 13 us -> none  [the longest x1 12.7 us: local_step(): FACTOR_DECAY * s_old_loc.reshape(d_out, -1)]
  transfers between devices with their start and end apart: 5 -> 1, of which waited for: 2 -> 1; matrix products, arithmetic and copies ran while one was open for 12% -> 1% of each run, Pallas kernels for 4% -> 0%
where the time goes in v2:
time: 410 us
  Pallas kernels  297 us (72%)
  waiting for transfers between devices  63.3 us (15%)
  local copies, waits for them, and re-layouts  31.3 us (8%)
  between operations  14.1 us (3%)
  other arithmetic  4.19 us (1%)
    pallas_call x1, Pallas kernels, solve_all(): pl.pallas_call(functools.partial(solve_all_kernel, nm, np_in, np_out, n_d...  214 us
    pallas_call x1, Pallas kernels, stats(): pl.pallas_call(functools.partial(stats_kernel, nm, ns, c_in, c_out), out_...  82.8 us
    all_gather x1, waiting for transfers between devices, local_step(): lax.all_gather(xt[:, :n_own, :], 'dp').transpose(1, 3, 0, 2)  63.3 us
    unnamed x6, local copies, waits for them, and re-layouts  18.4 us
  transfers between devices with their start and end apart: 1, of which 1 were waited for; matrix products, arithmetic and copies ran while one was open for 1% of the time, Pallas kernels for 0%

profile of v2, /device:TPU:0, one launch (start us, length us, event | category | flops | bytes accessed | tf_op | source)
XLA Modules:
  0.0 409.7 jit_solution(3947678334670299717)
XLA Ops:
  7.2 0.0 all-gather.3.cloned.1.call-start
  7.2 82.8 %stats_rs.1.share = f32[3,13,8,128]{3,2,1,0:T(8,128)} custom-call(bf16[2048,768]{1,0:T(8,128)(2,1)} %a_hbm.1, bf16[2048,2304]{1,0:T(8,128)(2,1)} %g_hbm.1, f32[162,128,128]{2,1,0:T(8,128)} %bitcast.17, f32[18,128,128]{2,1,0:T(8,128)} %bitcast.20), custom_call_target="tpu_custom_call" | custom-call | tf_op jit(solution)/shard_map/stats_rs/pallas_call | solution.py:292
  90.0 214.0 %factor_solve.1 = (f32[9,8,256]{2,1,0:T(8,128)}, f32[3,768,128]{2,1,0:T(8,128)}, f32[9,2304,128]{2,1,0:T(8,128)}) custom-call(f32[3,13,8,128]{3,2,1,0:T(8,128)} %stats_rs.1.share), custom_call_target="tpu_custom_call" | custom-call | tf_op jit(solution)/shard_map/factor_solve/pallas_call | solution.py:544
  304.0 0.0 all-gather.3.cloned.1.call-update
  304.0 3.3 copy.12
  307.3 63.3 %all-gather.3.cloned.1.call-done = f32[576,6,256]{2,1,0:T(8,128)} async-done(((f32[9,6,256]{2,1,0:T(8,128)}), f32[576,6,256]{2,1,0:T(8,128)}) %all-gather.3.cloned.1.call-update) | async-done | bytes 3538960 | tf_op jit(solution)/shard_map/all_gather | solution.py:562
  370.6 7.0 %copy.15 = f32[64,9,6,256]{3,1,2,0:T(8,128)} copy(f32[64,9,6,256]{3,2,1,0:T(8,128)} %bitcast.18) | data formatting | bytes 7077888 | tf_op jit(solution)/shard_map/all_gather | solution.py:562
  377.6 6.0 %reshape.17 = f32[2304,3,128]{0,2,1:T(8,128)} reshape(f32[9,256,64,6]{1,0,3,2:T(8,128)} %bitcast.15) | data formatting | bytes 7077888 | tf_op jit(solution)/shard_map/reshape | solution.py:562
  383.5 4.2 %sub.3 = f32[2304,3,128]{0,2,1:T(8,128)} subtract(f32[2304,3,128]{0,2,1:T(8,128)S(1)} %copy.12, f32[2304,3,128]{0,2,1:T(8,128)} %reshape.17) | non-fusion elementwise | flops 884736 | bytes 10616832 | tf_op jit(solution)/shard_map/sub | solution.py:563
  387.7 0.0 copy-start
  387.7 5.2 %copy.13 = f32[2304,3,128]{2,0,1:T(8,128)} copy(f32[2304,3,128]{0,2,1:T(8,128)} %sub.3) | data formatting | bytes 7077888
  393.0 0.0 copy-done
  393.0 1.0 copy.18
  394.0 8.8 %copy.19 = f32[2304,9,128]{2,0,1:T(8,128)} copy(f32[2304,9,128]{2,0,1:T(8,128)} %bitcast.16) | data formatting | bytes 21233664
Async XLA Ops:
  7.2 363.4 %all-gather.3.cloned.1.call-start = ((), (), s32[]{:S(2)}) async-start(), calls=%async_computation | async-start | bytes 4792320 | tf_op jit(solution)/shard_map/all_gather | solution.py:562
  387.7 5.2 %copy-start = (f32[3,768,128]{2,1,0:T(8,128)S(1)}, f32[3,768,128]{2,1,0:T(8,128)}, u32[]{:S(2)}) copy-start(f32[3,768,128]{2,1,0:T(8,128)} %get-tuple-element.7) | copy-start | bytes 3538948
Sparse Core Ops, SparseCore 0:
  304.1 66.4 all-gather.2

commit v3 on v2

v3 whole, which is shorter than its diff:
```python
import functools
import math
import numpy as np
import jax
import jax.numpy as jnp
from jax import lax
from jax.experimental import pallas as pl
from jax.experimental.pallas import tpu as pltpu
from jax.sharding import PartitionSpec as P

FACTOR_DECAY = 0.95
DAMPING = 0.001
DAMP_SHIFT = math.sqrt(DAMPING)
LEARN_RATE = 1.0
BW = 128
PW = 256
RING = 4
SUBL = 8
HALVES = (0, 1)
PARTS = (0, 1, 2)
UPDOWN = (1, 3)
HALF = 64
GROUP = 12
F32 = jnp.float32
BF = jnp.bfloat16
NT = (((1,), (1,)), ((), ()))
NN = (((1,), (0,)), ((), ()))


MB = 16

def split3(x):
    h = x.astype(BF)
    r = x - h.astype(F32)
    m = r.astype(BF)
    return h, m, (r - m.astype(F32)).astype(BF)

def lane_bc(x, i, zero):
    return bc(x[:, i:i + 1]) + zero

def bc(x):
    return jnp.broadcast_to(x, (SUBL, BW))

def factor_block(mat, linv, beside=None):
    lane = lax.broadcasted_iota(jnp.int32, (SUBL, BW), 1)
    sub = lax.broadcasted_iota(jnp.int32, (SUBL, BW), 0)
    zero = lane.astype(F32) * 0.0
    nxt = None
    for t in range(BW // MB):
        k = t * MB
        if beside is not None:
            beside(t)
        rows = [mat[k + SUBL * r:k + SUBL * r + SUBL, :] for r in HALVES] if nxt is None else nxt
        cols = [[lane_bc(rows[r], k + i, zero) for r in HALVES] for i in range(MB)]
        inside = (lane >= k) & (lane < k + MB)
        ext = [jnp.where(inside, jnp.where(lane == sub + (k + SUBL * r), 1.0, 0.0), rows[r]) for r in HALVES]
        more = k + MB < BW
        far = k + MB + MB < BW
        if more:
            near = [mat[k + MB + SUBL * r:k + MB + SUBL * r + SUBL, :] for r in HALVES]
            mult = [[lane_bc(near[r], k + i, zero) for r in HALVES] for i in range(MB)]
        if far:
            rh, rm, rl = split3(jnp.concatenate(rows, 0))
            left = jnp.concatenate([rh, rh, rm, rh, rl, rm], 0).T[k + MB + MB:, :]
        rv = [None, None]
        for j in range(0, MB, 2):
            jr, js = divmod(j, SUBL)
            u, v = cols[j], cols[j + 1]
            a, b, c = bc(u[jr][js:js + 1]), bc(u[jr][js + 1:js + 2]), bc(v[jr][js + 1:js + 2])
            det = a * c - b * b
            rdet = 1.0 / det
            ra = 1.0 / a
            e0, e1 = bc(ext[jr][js:js + 1]), bc(ext[jr][js + 1:js + 2])
            linv[k + j:k + j + 1, :] = (e0 * lax.rsqrt(a))[:1]
            linv[k + j + 1:k + j + 2, :] = ((e1 - (b * ra) * e0) * lax.rsqrt(det * ra))[:1]
            pair = (sub == js) | (sub == js + 1)
            um, vm = ([jnp.where(pair, 0.0, x[r]) if r == jr else x[r] for r in HALVES] for x in (u, v))
            n0 = [c * um[r] - b * vm[r] for r in HALVES]
            n1 = [a * vm[r] - b * um[r] for r in HALVES]
            f0 = [n0[r] * rdet for r in HALVES]
            f1 = [n1[r] * rdet for r in HALVES]
            for i in range(j + 2, MB):
                b0, b1 = bc(cols[i][jr][js:js + 1]), bc(cols[i][jr][js + 1:js + 2])
                if i < j + 4:
                    cols[i] = [cols[i][r] - (n0[r] * b0 + n1[r] * b1) * rdet for r in HALVES]
                else:
                    cols[i] = [cols[i][r] - (f0[r] * b0 + f1[r] * b1) for r in HALVES]
            ext = [ext[r] - (f0[r] * e0 + f1[r] * e1) for r in HALVES]
            w0, w1 = (c * e0 - b * e1) * rdet, (a * e1 - b * e0) * rdet
            own = (a * rdet, b * rdet, c * rdet)
            rv[jr] = [(js, own)] if js == 0 else rv[jr] + [(js, own)]
        w = []
        for r in HALVES:
            cur = ext[r]
            swap = jnp.where(lax.rem(sub, 2) == 0, jnp.roll(cur, -1, 0), jnp.roll(cur, 1, 0))
            dg = of = None
            for js, (ad, bd, cd) in rv[r]:
                d_here = jnp.where(sub == js, cd, ad)
                if dg is None:
                    dg, of = d_here, bd
                else:
                    dg = jnp.where(sub >= js, d_here, dg)
                    of = jnp.where(sub >= js, bd, of)
            w.append(cur * dg - swap * of)
        if more:
            nxt = []
            for r in HALVES:
                terms = [mult[j][r] * bc(w[j // SUBL][j % SUBL:j % SUBL + 1]) for j in range(MB)]
                while len(terms) > 1:
                    terms = [x + y for x, y in zip(terms[::2], terms[1::2])]
                nxt.append(jnp.where(inside, 0.0, near[r]) - terms[0])
        if far:
            wh, wm, wl = split3(jnp.concatenate(w, 0))
            right = jnp.concatenate([wh, wm, wh, wl, wh, wm], 0)
            prod = lax.dot_general(left, right, NN, preferred_element_type=F32)
            ins = jnp.broadcast_to(inside[:1], (BW - k - 2 * MB, BW))
            mat[k + MB + MB:, :] = jnp.where(ins, 0.0, mat[k + MB + MB:, :]) - prod
    ri = lax.broadcasted_iota(jnp.int32, (BW, BW), 0)
    ci = lax.broadcasted_iota(jnp.int32, (BW, BW), 1)
    linv[...] = jnp.where(ci <= ri, linv[...], 0.0)


EARLY = 2

def coords():
    d = lax.axis_index('dp')
    x = lax.rem(d, RING)
    y = lax.rem(lax.div(d, RING), RING)
    z = lax.div(d, RING * RING)
    return d, (x, y, z)

def neighbour(d, pos, axis, step):
    stride = (1, RING, RING * RING)[axis]
    return d + (lax.rem(pos[axis] + step, RING) - pos[axis]) * stride

def axis_of(part, phase):
    return (part + phase) % 3

def entry_barrier(d, pos, partner):
    sem = pltpu.get_barrier_semaphore()
    count = 0
    for axis in PARTS:
        for step in ((1, 3, 2) if partner is not None else UPDOWN):
            pl.semaphore_signal(sem, inc=1, device_id={'dp': neighbour(d, pos, axis, step)}, device_id_type=pl.DeviceIdType.MESH)
            count += 1
    if partner is not None:
        pl.semaphore_signal(sem, inc=1, device_id={'mp': partner}, device_id_type=pl.DeviceIdType.MESH)
        count += 1
    pl.semaphore_wait(sem, count)

def remote(src, dst, ssem, rsem, dev):
    return pltpu.make_async_remote_copy(src_ref=src, dst_ref=dst, send_sem=ssem, recv_sem=rsem, device_id={'dp': dev}, device_id_type=pl.DeviceIdType.MESH)

def each(lo, hi, fn):
    def body(i, c):
        fn(i)
        return c
    lax.fori_loop(lo, hi, body, 0)

def decode(b, np_in, np_out):
    n_in, n_out = 2 * np_in, 2 * np_out
    starts, at = [], 0
    for q0, base_row, base_col, n in [(q, n_in, np_in, n_out) for q in range(EARLY)] + [(q, 0, 0, n_in) for q in range(np_in)] + [(q, n_in, np_in, n_out) for q in range(EARLY, np_out)]:
        starts.append((at, base_row + 2 * q0 - at, base_col + q0))
        at += n - 2 * q0
    row, col, was = b, 0, (0, 0)
    for z, (first, d_row, d_col) in enumerate(starts):
        hit = 1 if z == 0 else (b >= first).astype(jnp.int32)
        row = row + hit * (d_row - was[0])
        col = col + hit * (d_col - was[1])
        was = (d_row, d_col)
    is_g = (b >= at).astype(jnp.int32)
    g_row, g_col = lax.rem(b - at * is_g, n_in), np_in + lax.div(b - at * is_g, n_in)
    row = row + is_g * (g_row - row)
    col = col + is_g * (g_col - col)
    in_s = (col >= np_in).astype(jnp.int32)
    old = in_s * ((col - np_in) * n_out + row - n_in) + (1 - in_s) * (np_out * n_out + col * n_in + row)
    return row, col, (1 - is_g) * old, is_g

def stats_kernel(nm, ns, c_in, c_out, a_hbm, g_hbm, s_hbm, ao_hbm, share, ag, agt, old, acc, ra1, rb1, rc1, rd1, ra2, rb2, rc2, rd2, ra3, rb3, rc3, rd3, lsem, ssem, rsem):
    p = lax.axis_index('mp')
    d, pos = coords()
    n_in, n_out = c_in // BW, c_out // BW
    n_all = ns * RING**3
    nso = s_hbm.shape[0]
    loads = [pltpu.make_async_copy(a_hbm, ag.at[:, 0:c_in], lsem.at[0]), pltpu.make_async_copy(g_hbm, ag.at[:, c_in:c_in + c_out], lsem.at[1]),
        pltpu.make_async_copy(s_hbm, old.at[0:nso], lsem.at[2]), pltpu.make_async_copy(ao_hbm, old.at[nso:nso + ao_hbm.shape[0]], lsem.at[3])]
    for c in loads:
        c.start()
    entry_barrier(d, pos, None)
    ck = min(512, ns)
    for z, (base, cnt) in enumerate(((0, n_in), (n_in, n_out))):
        loads[z].wait()
        def flip(c):
            for r in range(ns // ck):
                agt[base + c, :, r * ck:(r + 1) * ck] = ag[r * ck:(r + 1) * ck, pl.ds(pl.multiple_of((base + c) * BW, BW), BW)].T
        each(0, cnt, flip)
    loads[2].wait()
    loads[3].wait()

    def quarter(rel):
        def body(m):
            for part in PARTS:
                c1 = lax.rem(pos[axis_of(part, 0)] + rel, RING)
                b = (m * 3 + part) * RING + c1
                row, col, at, is_g = decode(b, n_in // 2, n_out // 2)
                w_new = jnp.where(is_g == 1, 1.0 / n_all, (1.0 - FACTOR_DECAY) / n_all)
                w_old = jnp.where(is_g == 1, 0.0, FACTOR_DECAY / RING**3)
                rhs = ag[:, pl.ds(pl.multiple_of((2 * col + p) * BW, BW), BW)]
                prod = lax.dot_general(agt[row], rhs, NN, preferred_element_type=F32)
                acc[part, m, c1] = prod * w_new + old[at] * w_old
        each(0, nm, body)

    def hop(part, phase, step):
        return neighbour(d, pos, axis_of(part, phase), step)

    def both(k, part, phase, pairs):
        out = []
        for z, (step, src, dst) in enumerate(pairs):
            s = (k * 3 + part) * 2 + z
            c = remote(src, dst, ssem.at[s], rsem.at[s], hop(part, phase, step))
            c.start()
            out.append(c)
        return out

    cs = [[pos[axis_of(part, ph)] for ph in range(3)] for part in PARTS]
    rel = lambda part, ph, k: lax.rem(cs[part][ph] + k, RING)
    copies = []
    quarter(2)
    s1 = []
    for part in PARTS:
        o = rel(part, 0, 2)
        s1.append(both(0, part, 0, [(1, acc.at[part, :, o, :HALF], ra1.at[part]), (3, acc.at[part, :, o, HALF:], rb1.at[part])]))
    quarter(1)
    s2 = []
    for z, k in enumerate(UPDOWN):
        if z == 1:
            quarter(3)
        for part in PARTS:
            u = rel(part, 0, k)
            s1[part][z].wait_recv()
            src = (ra1, rb1)[z]
            lo = HALF * z
            def body(m):
                acc[part, m, u, lo:lo + HALF] = acc[part, m, u, lo:lo + HALF] + src[part, m]
            each(0, nm, body)
            n = (3 + part) * 2 + z
            c = remote(acc.at[part, :, u], (rc1, rd1)[z].at[part], ssem.at[n], rsem.at[n], hop(part, 0, k))
            c.start()
            s2.append(c)
    quarter(0)
    for part in PARTS:
        c1 = cs[part][0]
        s2[part].wait_recv()
        s2[3 + part].wait_recv()
        def body(m):
            acc[part, m, c1] = acc[part, m, c1] + (rc1[part, m] + rd1[part, m])
        each(0, nm, body)
        o = pl.multiple_of(rel(part, 1, 2) * 32, 32)
        copies.append(both(2, part, 1, [(1, acc.at[part, :, c1, pl.ds(o, 16)], ra2.at[part]), (3, acc.at[part, :, c1, pl.ds(o + 16, 16)], rb2.at[part])]))
    p2 = []
    for part in PARTS:
        c1 = cs[part][0]
        lst = []
        for z, k in enumerate(UPDOWN):
            u = pl.multiple_of(rel(part, 1, k) * 32, 32)
            copies[part][z].wait_recv()
            src = (ra2, rb2)[z]
            def body(m):
                r = pl.ds(pl.multiple_of(u + 16 * z, 16), 16)
                acc[part, m, c1, r] = acc[part, m, c1, r] + src[part, m]
            each(0, nm, body)
            n = (9 + part) * 2 + z
            c = remote(acc.at[part, :, c1, pl.ds(u, 32)], (rc2, rd2)[z].at[part], ssem.at[n], rsem.at[n], hop(part, 1, k))
            c.start()
            lst.append(c)
        p2.append(lst)
    h = (nm + 1) // 2
    p3 = []
    for part in PARTS:
        c1 = cs[part][0]
        e = pl.multiple_of(cs[part][1] * 32, 32)
        for c in p2[part]:
            c.wait_recv()
        def body(m):
            acc[part, m, c1, pl.ds(e, 32)] = acc[part, m, c1, pl.ds(e, 32)] + (rc2[part, m] + rd2[part, m])
        each(0, nm, body)
        o = pl.multiple_of(e + rel(part, 2, 2) * SUBL, SUBL)
        p3.append(both(4, part, 2, [(1, acc.at[part, 0:h, c1, pl.ds(o, SUBL)], ra3.at[part]), (3, acc.at[part, h:nm, c1, pl.ds(o, SUBL)], rb3.at[part])]))
    p4 = []
    for part in PARTS:
        c1 = cs[part][0]
        e = pl.multiple_of(cs[part][1] * 32, 32)
        lst = []
        for z, k in enumerate(UPDOWN):
            u = pl.multiple_of(e + rel(part, 2, k) * SUBL, SUBL)
            p3[part][z].wait_recv()
            for m in range(h if z == 0 else nm - h):
                mm = m + h * z
                acc[part, mm, c1, pl.ds(u, SUBL)] = acc[part, mm, c1, pl.ds(u, SUBL)] + (ra3, rb3)[z][part, m]
            n = (15 + part) * 2 + z
            c = remote(acc.at[part, :, c1, pl.ds(u, SUBL)], (rc3, rd3)[z].at[part], ssem.at[n], rsem.at[n], hop(part, 2, k))
            c.start()
            lst.append(c)
        p4.append(lst)
    for part in PARTS:
        c1 = cs[part][0]
        f = pl.multiple_of(cs[part][1] * 32 + cs[part][2] * SUBL, SUBL)
        for c in p4[part]:
            c.wait_recv()
        for m in range(nm):
            share[part, m] = acc[part, m, c1, pl.ds(f, SUBL)] + (rc3[part, m] + rd3[part, m])
    for group in (s1, copies, p2, p3, p4):
        for lst in group:
            for c in lst:
                c.wait_send()
    for c in s2:
        c.wait_send()

def stats(a_loc, g_loc, a_old3, s_old3):
    ns, c_in = a_loc.shape
    c_out = g_loc.shape[1]
    np_in, np_out = c_in // 256, c_out // 256
    nb = (np_in + np_out) * (np_in + np_out + 1)
    nm = nb // GROUP
    assert nm * GROUP == nb
    h = (nm + 1) // 2
    hb = pl.BlockSpec(memory_space=pl.ANY)
    V = pltpu.VMEM
    slab = lambda n: [V((len(PARTS), nm, n, BW), F32)] * 2
    s_blk = s_old3.reshape(-1, BW, BW)
    a_blk = a_old3.reshape(-1, BW, BW)
    return pl.pallas_call(functools.partial(stats_kernel, nm, ns, c_in, c_out),
        out_shape=jax.ShapeDtypeStruct((3, nm, SUBL, BW), F32),
        in_specs=[hb, hb, hb, hb], out_specs=pl.BlockSpec(memory_space=V),
        scratch_shapes=[V((ns, c_in + c_out), BF), V(((c_in + c_out) // BW, BW, ns), BF), V((s_blk.shape[0] + a_blk.shape[0], BW, BW), F32), V((3, nm, 4, BW, BW), F32),
            *slab(HALF), *slab(BW), *slab(16), *slab(32),
            V((3, h, SUBL, BW), F32), V((3, nm - h, SUBL, BW), F32), *slab(SUBL),
            pltpu.SemaphoreType.DMA((4,)), pltpu.SemaphoreType.DMA((36,)), pltpu.SemaphoreType.DMA((36,))],
        compiler_params=pltpu.CompilerParams(collective_id=0, has_side_effects=True, vmem_limit_bytes=63 * 2**20), name="stats_rs")(a_loc, g_loc, s_blk, a_blk)


def dot6(a, b, dims):
    d = lambda x, y: lax.dot_general(x, y, dims, preferred_element_type=F32)
    ah, am, al = a
    bh, bm, bl = b
    return (d(am, bm) + d(ah, bl) + d(al, bh)) + (d(ah, bm) + d(am, bh)) + d(ah, bh)

def stack_dot(x, w, dims):
    xh, xm, xl = x
    wh, wm, wl = w
    k = xh.shape[0]
    d = lambda u, v: lax.dot_general(u, v, dims, preferred_element_type=F32)
    p1 = d(jnp.concatenate([xh, xm, xl], 0), wh)
    p2 = d(jnp.concatenate([xh, xm], 0), wm)
    p3 = d(xh, wl)
    return (p1[k + k:] + p2[k:] + p3) + (p1[k:k + k] + p2[:k]) + p1[:k]

def pieces(ref, at):
    return [ref[z, at] for z in PARTS]

def rows_at(start, size):
    return pl.ds(pl.multiple_of(start, SUBL), size)

def to_partner(src, dst, sems, s):
    return pltpu.make_async_remote_copy(src_ref=src, dst_ref=dst, send_sem=sems.at[0, s], recv_sem=sems.at[1, s], device_id={'mp': 1 - lax.axis_index('mp')}, device_id_type=pl.DeviceIdType.MESH)

def ring_steps(spot, base, ssem, rsem):
    d, pos = coords()
    def copy(part, phase, z):
        axis = axis_of(part, phase)
        c = pos[axis]
        step, come = ((1, None), (3, None), (2, None), (1, 3), (3, 1))[z]
        ref = spot(part, phase, c, None) if come is None else spot(part, phase, lax.rem(c + come, RING), z - 3)
        s = base + (part * 3 + phase) * 4 + z - (z > 2)
        return remote(ref, ref, ssem.at[s], rsem.at[s], neighbour(d, pos, axis, step))
    def act(phase, zs, name):
        for part in PARTS:
            for z in zs:
                getattr(copy(part, phase, z), name)()
    every, near, on = PARTS, HALVES, (3, 4)
    def relay():
        for z in near:
            act(0, (z,), 'wait_recv')
            act(0, (z + 3,), 'start')
    def settle():
        act(2, every, 'wait_send')
        act(1, every, 'wait_send')
        act(0, near + on, 'wait_send')
    steps = [lambda: act(2, every, 'start'), lambda: (act(2, every, 'wait_recv'), act(1, every, 'start')), lambda: (act(1, every, 'wait_recv'), act(0, near, 'start')),
        relay, lambda: act(0, on, 'wait_recv')]
    return steps, settle

def block_at(q, np_in, np_out, of_s):
    n_in, n_out = 2 * np_in, 2 * np_out
    in_s = q * n_out - q * (q - 1) + np_in * (np_in + 1) * jnp.minimum(lax.div(q, EARLY), 1)
    in_a = EARLY * n_out - EARLY * (EARLY - 1) + q * n_in - q * (q - 1)
    return of_s * in_s + (1 - of_s) * in_a

def solve_all_kernel(nm, np_in, np_out, n_dp, damp, rounds, plan, share, blocks, fin0, fin1, fin2, full, tmat, mat, linv, inv_all, lsp, xw, zin, pack, ssem, rsem, psem, osem):
    p = lax.axis_index('mp')
    d, pos = coords()
    n_own = np_in * BW // n_dp
    n_in, n_out = 2 * np_in, 2 * np_out
    n_rounds = len(rounds) - 1
    per_round = 36
    cs = [[pos[axis_of(part, ph)] for ph in PARTS] for part in PARTS]
    for part in PARTS:
        c1, e, f = cs[part]
        def put(m):
            full[p, m, part, c1, rows_at(e * 32 + f * SUBL, SUBL)] = share[part, m]
        each(0, nm, put)
    entry_barrier(d, pos, 1 - p)

    def gather(k):
        ms = pl.ds(rounds[k], rounds[k + 1] - rounds[k])
        def spot(part, phase, coord, half):
            c1, e, f = cs[part]
            if phase == 2:
                return full.at[p, ms, part, c1, rows_at(e * 32 + coord * SUBL, SUBL)]
            if phase == 1:
                return full.at[p, ms, part, c1, rows_at(coord * 32, 32)]
            size = BW if half is None else BW // 2
            return full.at[p, ms, part, coord, pl.ds((half or 0) * size, size)]
        steps, settle = ring_steps(spot, k * per_round, ssem, rsem)
        swap = lambda: to_partner(full.at[p, ms], full.at[p, ms], psem, k)
        def keep(half):
            return pltpu.make_async_copy(full.at[half, ms], blocks.at[half, ms], osem.at[half, k])
        def close():
            swap().wait_recv()
            for half in HALVES:
                keep(half).start()
        def finish():
            settle()
            swap().wait_send()
            for half in HALVES:
                keep(half).wait()
        last = steps[-1]
        steps[-1] = lambda: (last(), swap().start())
        return steps + [close], finish

    gathers = [gather(k) for k in range(n_rounds)]
    agenda = {}
    for (steps, _), times in zip(gathers, plan):
        for fn, z in zip(steps, times):
            agenda.setdefault(z, []).append(fn)
    for z in sorted(z for z in agenda if z < 0):
        for fn in agenda[z]:
            fn()
    poll = sorted(z for z in agenda if z >= 0)
    closing = [g[0][-1] for g in gathers]
    n_a_round = n_rounds
    @pl.when(p == 1)
    def _():
        for z in poll:
            for fn in agenda[z]:
                if fn not in closing[n_a_round:]:
                    fn()

    def block(par, b):
        return full[par, lax.div(b, GROUP), lax.div(lax.rem(b, GROUP), RING), lax.rem(b, RING)]

    base_g = np_out * (np_out + 1) + np_in * (np_in + 1)
    npan = np_out - (np_out - np_in) * p
    eye = jnp.where(lax.broadcasted_iota(jnp.int32, (BW, BW), 0) == lax.broadcasted_iota(jnp.int32, (BW, BW), 1), damp, 0.0)

    def load(q):
        base = block_at(q, np_in, np_out, 1 - p)
        slot = lax.rem(q, 2)
        for par in HALVES:
            cols = pl.ds(par * BW, BW)
            def rows(i):
                for h in HALVES:
                    tmat[slot, i, h * BW:(h + 1) * BW, cols] = block(par, base + 2 * (i - q) + h)
            each(q, npan, rows)
            tmat[slot, q, cols, cols] = tmat[slot, q, cols, cols] + eye

    def ltile(i, k):
        return lax.div(i * (i - 1), 2) + k

    def update(i, k, q, ok):
        slot = lax.rem(q, 2)
        at = ok * i + (1 - ok) * np_out
        prod = stack_dot(pieces(lsp, ok * ltile(i, k)), pieces(lsp, ok * ltile(q, k)), NT)
        tmat[slot, at] = tmat[slot, at] - prod

    def task(s, q):
        left = jnp.maximum(npan - 1 - q, 1)
        turn = lax.div(s, left)
        ok = (turn <= q).astype(jnp.int32) * jnp.minimum(q, 1) * jnp.minimum(npan - 1 - q, 1)
        k = turn - 1 + q * (1 - jnp.minimum(turn, 1))
        update(q + 1 + lax.rem(s, left), k, q + jnp.minimum(turn, 1), ok)

    load(0)
    n_slot = MB

    def panel(k):
        q = lax.div(k, 2)
        h = lax.rem(k, 2)
        slot = lax.rem(q, 2)
        @pl.when(h == 0)
        def _():
            mat[...] = tmat[slot, q, :BW, :BW]
        factor_block(mat, linv, lambda t: task(h * SUBL + t, q))
        @pl.when(h == 0)
        def _():
            inv0 = linv[...]
            inv0s = split3(inv0)
            l10 = dot6(split3(tmat[slot, q, BW:, :BW]), inv0s, NT)
            l10s = split3(l10)
            mat[...] = tmat[slot, q, BW:, BW:] - dot6(l10s, l10s, NT)
            inv_all[q, :BW, :BW] = inv0
            inv_all[q, :BW, BW:] = jnp.zeros((BW, BW), F32)
            inv_all[q, BW:, :BW] = dot6(l10s, inv0s, NN)
        @pl.when((h == 1) & (q < npan - 1))
        def _():
            each(n_slot, (npan - 1 - q) * (q + 1), lambda s: task(s, q))
        @pl.when(h == 1)
        def _():
            inv1 = linv[...]
            inv_all[q, BW:, BW:] = inv1
            inv_all[q, BW:, :BW] = -dot6(split3(inv1), split3(inv_all[q, BW:, :BW]), NN)
            invs = split3(inv_all[q])
            def below(i):
                for z, v in enumerate(split3(stack_dot(split3(tmat[slot, i]), invs, NT))):
                    lsp[z, ltile(i, q)] = v
            each(q + 1, npan, below)
        for z in poll:
            @pl.when((p == 0) & (k == z))
            def _():
                for fn in agenda[z]:
                    fn()
        @pl.when((h == 1) & (q < npan - 1))
        def _():
            @pl.when(q == 0)
            def _():
                load(1)
            update(q + 1, q, q + 1, 1)
            @pl.when(q < npan - 2)
            def _():
                load(q + 2)
    each(0, 2 * npan, panel)

    zcopy = to_partner(zin.at[0], zin.at[1], psem, n_rounds)
    @pl.when(p == 1)
    def _():
        row = lax.broadcasted_iota(jnp.int32, (MB, PW), 0)
        lane = lax.broadcasted_iota(jnp.int32, (MB, PW), 1)
        par = lax.div(row, SUBL)
        idx = lax.rem(row, SUBL)
        col = d * n_own + idx
        for q in range(np_in):
            hit = (idx < n_own) & (lax.div(col, BW) == q) & (lane == par * BW + lax.rem(col, BW))
            xw[q] = jnp.where(hit, 1.0, 0.0)
    @pl.when(p == 0)
    def _():
        zcopy.wait_recv()
        def cp(q):
            xw[q] = zin[1, q]
        each(0, np_out, cp)

    def fwd(q):
        y = stack_dot(split3(xw[q]), split3(inv_all[q]), NT)
        xw[q] = y
        ys = split3(y)
        def sub(j):
            xw[j] = xw[j] - stack_dot(ys, pieces(lsp, ltile(j, q)), NT)
        each(q + 1, npan, sub)
    each(0, npan, fwd)
    def back(s):
        q = npan - 1 - s
        x = stack_dot(split3(xw[q]), split3(inv_all[q]), NN)
        xw[q] = x
        xs = split3(x)
        def sub(j):
            xw[j] = xw[j] - stack_dot(xs, pieces(lsp, ltile(q, j)), NN)
        each(0, q, sub)
    each(0, npan, back)

    xcopy = to_partner(pack.at[1], pack.at[0], psem, n_rounds + 1)
    @pl.when(p == 1)
    def _():
        for fn in closing[n_a_round:]:
            fn()
        def zq(q):
            for par in HALVES:
                acc = jnp.zeros((MB, BW), F32)
                for i in range(n_in):
                    acc = acc + stack_dot(split3(xw[i // 2, :, (i % 2) * BW:(i % 2 + 1) * BW]), split3(block(par, base_g + q * n_in + i)), NN)
                zin[0, q, :, par * BW:(par + 1) * BW] = acc
        each(0, np_out, zq)
        zcopy.start()
        xcopy.wait_recv()
        zcopy.wait_send()
    @pl.when(p == 0)
    def _():
        for par in reversed(HALVES):
            pack[par, np_out * n_own:] = jnp.zeros((pack.shape[1] - np_out * n_own, PW), F32)
            for q in range(np_out):
                pack[par, q * n_own:(q + 1) * n_own] = xw[q, par * SUBL:par * SUBL + n_own]
            if par == 1:
                xcopy.start()
    fins = (fin0, fin1, fin2)
    t = 0
    for part in PARTS:
        for z in range(fins[part].shape[3]):
            half = t % 2
            fins[part][(*cs[part], z)] = pack[0, t // 2 * SUBL:(t // 2 + 1) * SUBL, half * BW:(half + 1) * BW]
            t += 1
    def spot(part, phase, coord, half):
        at = (*cs[part][:phase], coord)
        return fins[part].at[at if half is None else (*at, pl.ds(2 * half, 2))]
    steps, settle = ring_steps(spot, n_rounds * per_round, ssem, rsem)
    for fn in steps:
        fn()
    settle()
    @pl.when(p == 0)
    def _():
        xcopy.wait_send()
    for _, finish in gathers:
        finish()

def solve_all(share, np_in, np_out, n_dp, damp):
    nm = share.shape[1]
    n_own = np_in * BW // n_dp
    n_row = -(-np_out * n_own // SUBL)
    tiles = [-(-(2 * n_row - part) // 3) for part in PARTS]
    V = pltpu.VMEM
    vb = pl.BlockSpec(memory_space=V)
    hb = pl.BlockSpec(memory_space=pl.ANY)
    gathered = (2, nm, 3, 4, BW, BW)
    rounds = (0, 2, 5, 8, nm)
    plan = [range(k - 9, k - 3) for k in range(len(rounds) - 1)]
    n_rounds = len(rounds) - 1
    n_tile = np_out * (np_out - 1) // 2
    D = pltpu.SemaphoreType.DMA
    sems = 36 * (n_rounds + 1)
    return pl.pallas_call(functools.partial(solve_all_kernel, nm, np_in, np_out, n_dp, damp, rounds, plan),
        out_shape=(jax.ShapeDtypeStruct(gathered, F32), *(jax.ShapeDtypeStruct((4, 4, 4, t, SUBL, BW), F32) for t in tiles)),
        in_specs=[vb], out_specs=(hb, vb, vb, vb),
        scratch_shapes=[V(gathered, F32), V((2, np_out + 1, PW, PW), F32), *[V((BW, BW), F32)] * 2, V((np_out, PW, PW), F32),
            V((3, n_tile, PW, PW), BF), V((np_out, MB, PW), F32), V((2, np_out, MB, PW), F32), V((2, n_row * SUBL, PW), F32),
            D((sems,)), D((sems,)), D((2, n_rounds + 2)), D((2, n_rounds))],
        compiler_params=pltpu.CompilerParams(collective_id=1, has_side_effects=True, vmem_limit_bytes=63 * 2**20), name="factor_solve")(share)

def finish_kernel(np_in, np_out, n_own, w_hbm, blocks, fin0, fin1, fin2, w_out, a_out, s_out, wbuf, gath, cols_s, cols_a, up_s, up_a, isem, lsem, usem, wsem, csem):
    p = lax.axis_index('mp')
    wload = pltpu.make_async_copy(w_hbm, wbuf, isem)
    wload.start()
    sets = [(s_out, cols_s, up_s, np_out, 1), (a_out, cols_a, up_a, np_in, 0)]
    jobs, n = [], 0
    for out, cols, up, n_pan, of_s in sets:
        for q in range(n_pan):
            base = block_at(q, np_in, np_out, of_s) // 2
            low = pltpu.make_async_copy(blocks.at[p, pl.ds(base, n_pan - q)], cols.at[q, pl.ds(q, n_pan - q)], lsem.at[n])
            ups = [pltpu.make_async_copy(blocks.at[par, pl.ds(base + 1, n_pan - 1 - q), p], up.at[par, q, pl.ds(q + 1, n_pan - 1 - q)], usem.at[par, n]) for par in HALVES] if q < n_pan - 1 else []
            send = pltpu.make_async_copy(cols.at[q], out.at[q], csem.at[n])
            jobs.append((low, ups, send, cols, up, q))
            n += 1
    for low, ups, *_ in jobs:
        for c in (*ups, low):
            c.start()
    fins = (fin0, fin1, fin2)
    rows = fins[0].shape[3]
    def tile(t, c):
        part = 0
        while t >= fins[part].shape[3]:
            t -= fins[part].shape[3]
            part += 1
        return fins[part][c[part], c[(part + 1) % 3], c[(part + 2) % 3], t]
    wload.wait()
    for q in range(np_out):
        lo, hi = q * n_own // SUBL, ((q + 1) * n_own - 1) // SUBL
        for half in HALVES:
            def fill(g):
                vals = []
                for x in range(RING):
                    c = (x, lax.rem(g, RING), lax.div(g, RING))
                    v = jnp.concatenate([tile(2 * r + half, c) for r in range(lo, hi + 1)], 0)
                    at = q * n_own - lo * SUBL
                    vals.append(v[at:at + n_own])
                gath[rows_at(g * RING * n_own, RING * n_own)] = jnp.concatenate(vals, 0)
            each(0, RING * RING, fill)
            for b in range(np_in):
                r = slice((2 * q + half) * BW, (2 * q + half + 1) * BW)
                wbuf[b, r] = wbuf[b, r] - LEARN_RATE * gath[b * BW:(b + 1) * BW].T
    wsend = pltpu.make_async_copy(wbuf, w_out, wsem)
    wsend.start()
    for low, ups, send, cols, up, q in jobs:
        low.wait()
        for c in ups:
            c.wait()
    for low, ups, send, cols, up, q in jobs:
        def mirror(q2):
            for par in HALVES:
                cols[q, q2, par] = up[par, q2, q].T
        each(0, q, mirror)
        send.start()
    for low, ups, send, *_ in jobs:
        send.wait()
    wsend.wait()

def finish(w3, blocks, fins, np_in, np_out, n_dp):
    V = pltpu.VMEM
    D = pltpu.SemaphoreType.DMA
    hb = pl.BlockSpec(memory_space=pl.ANY)
    vb = pl.BlockSpec(memory_space=V)
    n_job = np_in + np_out
    square = lambda n: (n, n, 2, BW, BW)
    w_new, a_new, s_new = pl.pallas_call(functools.partial(finish_kernel, np_in, np_out, np_in * BW // n_dp),
        out_shape=(jax.ShapeDtypeStruct(w3.shape, F32), jax.ShapeDtypeStruct(square(np_in), F32), jax.ShapeDtypeStruct(square(np_out), F32)),
        in_specs=[hb, hb, vb, vb, vb], out_specs=(hb, hb, hb),
        scratch_shapes=[V(w3.shape, F32), V((np_in * BW, BW), F32), V(square(np_out), F32), V(square(np_in), F32), V((2, np_out, np_out, BW, BW), F32), V((2, np_in, np_in, BW, BW), F32),
            D, D((n_job,)), D((2, n_job)), D, D((n_job,))],
        compiler_params=pltpu.CompilerParams(vmem_limit_bytes=63 * 2**20), name="outputs")(w3, blocks.reshape(2, -1, 2, BW, BW), *fins)
    return w_new, a_new.reshape(np_in, -1, BW), s_new.reshape(np_out, -1, BW)


def solution(mesh):
    n_dp = mesh.shape['dp']

    def local_step(a_loc, g_loc, w_loc, a_old_loc, s_old_loc):
        np_in = a_loc.shape[1] // PW
        np_out = g_loc.shape[1] // PW
        panels = lambda x: x.transpose(1, 0, 2)
        share = stats(a_loc, g_loc, panels(a_old_loc), panels(s_old_loc))
        blocks, *fins = solve_all(share, np_in, np_out, n_dp, DAMP_SHIFT)
        return tuple(panels(x) for x in finish(panels(w_loc), blocks, fins, np_in, np_out, n_dp))

    spec_rows = P('dp', None)
    spec_cyc = P(None, 'mp', None)
    return jax.shard_map(local_step, mesh=mesh, in_specs=(spec_rows, spec_rows, spec_cyc, spec_cyc, spec_cyc), out_specs=(spec_cyc, spec_cyc, spec_cyc), check_vma=False)
```

time: 410 us -> 288 us (0.70)
  waiting for transfers between devices: 63.3 us -> 0 us
  local copies, waits for them, and re-layouts: 31.3 us -> 0 us
  between operations: 14.1 us -> 0.81 us
  Pallas kernels: 297 us -> 287 us
  other arithmetic: 4.19 us -> 0 us
    all_gather x1 -> x0, waiting for transfers between devices: 63.3 us -> none  [local_step(): lax.all_gather(xt[:, :n_own, :], 'dp').transpose(1, 3, 0, 2)]
    pallas_call x1, Pallas kernels: 214 us -> 185 us  [solve_all(): pl.pallas_call(functools.partial(solve_all_kernel, nm, np_in, np_out, n_d...]
    unnamed x6 -> x0, local copies, waits for them, and re-layouts: 18.4 us -> none
    pallas_call x0 -> x1, Pallas kernels: none -> 18.4 us  [finish(): pl.pallas_call(functools.partial(finish_kernel, np_in, np_out, np_in * BW...]
    all_gather x1 -> x0, local copies, waits for them, and re-layouts: 6.97 us -> none  [local_step(): lax.all_gather(xt[:, :n_own, :], 'dp').transpose(1, 3, 0, 2)]
    reshape x1 -> x0, local copies, waits for them, and re-layouts: 5.98 us -> none  [local_step(): lax.all_gather(xt[:, :n_own, :], 'dp').transpose(1, 3, 0, 2)]
    sub x1 -> x0, other arithmetic: 4.19 us -> none  [local_step(): w_loc - LEARN_RATE * delta]
  transfers between devices with their start and end apart: 1 -> 0, of which waited for: 1 -> 0; matrix products, arithmetic and copies ran while one was open for 1% -> 0% of each run, Pallas kernels for 0% -> 0%
where the time goes in v3:
time: 288 us; the launch traced here: 287 us
  Pallas kernels  287 us (100%)
    pallas_call x1, Pallas kernels, solve_all(): pl.pallas_call(functools.partial(solve_all_kernel, nm, np_in, np_out, n_d...  185 us
    pallas_call x1, Pallas kernels, stats(): pl.pallas_call(functools.partial(stats_kernel, nm, ns, c_in, c_out), out_...  82.9 us
    pallas_call x1, Pallas kernels, finish(): pl.pallas_call(functools.partial(finish_kernel, np_in, np_out, np_in * BW...  18.4 us

profile of v3, /device:TPU:0, one launch (start us, length us, event | category | flops | bytes accessed | tf_op | source)
XLA Modules:
  0.0 287.5 jit_solution(13995676771092357666)
XLA Ops:
  0.6 82.9 %stats_rs.1.share = f32[3,13,8,128]{3,2,1,0:T(8,128)} custom-call(bf16[2048,768]{1,0:T(8,128)(2,1)} %a_hbm.1, bf16[2048,2304]{1,0:T(8,128)(2,1)} %g_hbm.1, f32[162,128,128]{2,1,0:T(8,128)} %bitcast.16, f32[18,128,128]{2,1,0:T(8,128)} %bitcast.18), custom_call_target="tpu_custom_call" | custom-call | tf_op jit(solution)/shard_map/stats_rs/pallas_call | solution.py:333
  83.5 185.4 %factor_solve.1 = (f32[2,13,3,4,128,128]{5,4,3,2,1,0:T(8,128)}, f32[4,4,4,5,8,128]{5,4,3,2,1,0:T(8,128)}, f32[4,4,4,5,8,128]{5,4,3,2,1,0:T(8,128)}, f32[4,4,4,4,8,128]{5,4,3,2,1,0:T(8,128)}) custom-call(f32[3,13,8,128]{3,2,1,0:T(8,128)} %stats_rs.1.share), custom_call_target="tpu_custom_call" | custom-call | tf_op jit(solution)/shard_map/factor_solve/pallas_call | solution.py:638
  269.0 18.4 %outputs.1 = (f32[3,2304,128]{2,1,0:T(8,128)}, f32[3,3,2,128,128]{4,3,2,1,0:T(8,128)}, f32[9,9,2,128,128]{4,3,2,1,0:T(8,128)}) custom-call(f32[3,2304,128]{2,1,0:T(8,128)} %bitcast.17, f32[2,78,2,128,128]{4,3,2,1,0:T(8,128)} %bitcast.15, f32[4,4,4,5,8,128]{5,4,3,2,1,0:T(8,128)} %get-tuple-element.11.fin0, f32[4,4,4,5,8,128]{5,4,3,2,1,0:T(8,128)} %get-tuple-element.12.fin1, ...), custom_call_target="tpu_custom_call" | custom-call | tf_op jit(solution)/shard_map/outputs/pallas_call | solution.py:710

commit v4 on v0

v4 whole, which is shorter than its diff:
```python
import functools
import math
import jax
import jax.numpy as jnp
from jax import lax
from jax.experimental import pallas as pl
from jax.experimental.pallas import tpu as pltpu
from jax.sharding import PartitionSpec as P

BW = 128
PW = 256
RING = 4
SUBL = 8
HALF = 64
ROWS = 32
GROUP = 12
EARLY = 4
PAIR = 2
HALVES = (0, 1)
UPDOWN = (1, 3)
PARTS = (0, 1, 2)
FACTOR_DECAY = 0.95
LEARN_RATE = 1.0
DAMPING = 0.001
DAMP_SHIFT = math.sqrt(DAMPING)
MB = 16
F32 = jnp.float32
BF = jnp.bfloat16
NT = (((1,), (1,)), ((), ()))
NN = (((1,), (0,)), ((), ()))


def split3(x):
    h = x.astype(BF)
    r = x - h.astype(F32)
    m = r.astype(BF)
    return h, m, (r - m.astype(F32)).astype(BF)

def bc(x):
    return jnp.broadcast_to(x, (MB, BW))

def factor_block(mat, linv, beside=None):
    lane = lax.broadcasted_iota(jnp.int32, (MB, BW), 1)
    sub = lax.broadcasted_iota(jnp.int32, (MB, BW), 0)
    odd = lax.rem(sub, PAIR)
    zero = lane.astype(F32) * 0.0
    rows = mat[:MB]
    for t in range(BW // MB):
        k = t * MB
        if beside is not None:
            beside(t)
        cols = jnp.concatenate([bc(rows[:, k + i:k + i + 1]) for i in range(MB)], 0).reshape(MB, MB, BW) + zero
        inside = (lane >= k) & (lane < k + MB)
        ext = jnp.where(inside, jnp.where(lane == sub + k, 1.0, 0.0), rows)
        more = k + MB < BW
        far = k + MB + MB < BW
        if more:
            near = mat[k + MB:k + MB + MB]
            mult = [bc(near[:, k + i:k + i + 1]) for i in range(MB)]
        if far:
            rh, rm, rl = split3(rows)
            left = jnp.concatenate([rh, rh, rm, rh, rl, rm], 0).T[k + MB + MB:]
        dg = of = None
        for j in range(0, MB, PAIR):
            u, v = cols[0], cols[1]
            a, b, c = bc(u[j:j + 1]), bc(u[j + 1:j + 2]), bc(v[j + 1:j + 2])
            det = a * c - b * b
            rdet = 1.0 / det
            ra = 1.0 / a
            e0, e1 = bc(ext[j:j + 1]), bc(ext[j + 1:j + 2])
            linv[k + j:k + j + 1] = (e0 * lax.rsqrt(a))[:1]
            linv[k + j + 1:k + j + 2] = ((e1 - (b * ra) * e0) * lax.rsqrt(det * ra))[:1]
            pair = (sub == j) | (sub == j + 1)
            u, v = jnp.where(pair, 0.0, u), jnp.where(pair, 0.0, v)
            n0, n1 = c * u - b * v, a * v - b * u
            f0, f1 = n0 * rdet, n1 * rdet
            if j + 2 < MB:
                left_cols = cols[2:]
                soon = left_cols[:2]
                soon = soon - (n0 * jnp.broadcast_to(soon[:, j:j + 1], soon.shape) + n1 * jnp.broadcast_to(soon[:, j + 1:j + 2], soon.shape)) * rdet
                if j + 4 < MB:
                    late = left_cols[2:]
                    late = late - (f0 * jnp.broadcast_to(late[:, j:j + 1], late.shape) + f1 * jnp.broadcast_to(late[:, j + 1:j + 2], late.shape))
                    cols = jnp.concatenate([soon, late], 0)
                else:
                    cols = soon
            ext = ext - (f0 * e0 + f1 * e1)
            d_here = jnp.where(odd == 0, c, a) * rdet
            dg = d_here if dg is None else jnp.where(sub >= j, d_here, dg)
            of = b * rdet if of is None else jnp.where(sub >= j, b * rdet, of)
        w = ext * dg - jnp.where(odd == 0, jnp.roll(ext, -1, 0), jnp.roll(ext, 1, 0)) * of
        if far:
            wh, wm, wl = split3(w)
            prod = lax.dot_general(left, jnp.concatenate([wh, wm, wh, wl, wh, wm], 0), NN, preferred_element_type=F32)
            ins = jnp.broadcast_to(inside[:1], prod.shape)
            mat[k + MB + MB:] = jnp.where(ins, 0.0, mat[k + MB + MB:]) - prod
        if more:
            terms = [mult[j] * bc(w[j:j + 1]) for j in range(MB)]
            while len(terms) > 1:
                terms = [x + y for x, y in zip(terms[::2], terms[1::2])]
            rows = jnp.where(inside, 0.0, near) - terms[0]
    ri = lax.broadcasted_iota(jnp.int32, (BW, BW), 0)
    ci = lax.broadcasted_iota(jnp.int32, (BW, BW), 1)
    linv[...] = jnp.where(ci <= ri, linv[...], 0.0)


def dot6(a, b, dims):
    d = lambda x, y: lax.dot_general(x, y, dims, preferred_element_type=F32)
    ah, am, al = a
    bh, bm, bl = b
    return (d(am, bm) + d(ah, bl) + d(al, bh)) + (d(ah, bm) + d(am, bh)) + d(ah, bh)

def stack_dot(x, w, dims):
    xh, xm, xl = x
    wh, wm, wl = w
    k = xh.shape[0]
    d = lambda u, v: lax.dot_general(u, v, dims, preferred_element_type=F32)
    p1 = d(jnp.concatenate([xh, xm, xl], 0), wh)
    p2 = d(jnp.concatenate([xh, xm], 0), wm)
    p3 = d(xh, wl)
    return (p1[k + k:] + p2[k:] + p3) + (p1[k:k + k] + p2[:k]) + p1[:k]

def pieces(ref, at):
    return [ref[z, at] for z in PARTS]

def each(lo, hi, fn):
    def body(i, c):
        fn(i)
        return c
    lax.fori_loop(lo, hi, body, 0)

def upto(n, fn):
    each(0, n, fn)

def rows_at(start, size):
    return pl.ds(pl.multiple_of(start, SUBL), size)

def turn(c, step):
    return lax.rem(c + step, RING)

def place(part, phase):
    stride = RING**((part + phase) % 3)
    return lax.rem(lax.div(lax.axis_index('dp'), stride), RING), stride

def remote(src, dst, ssem, rsem, where):
    return pltpu.make_async_remote_copy(src_ref=src, dst_ref=dst, send_sem=ssem, recv_sem=rsem, device_id=where, device_id_type=pl.DeviceIdType.MESH)

def along(part, phase):
    return place(part, phase)[0]

def chip(part, phase, step):
    c, stride = place(part, phase)
    return {'dp': lax.axis_index('dp') + (turn(c, step) - c) * stride}

def partner():
    return {'mp': 1 - lax.axis_index('mp')}

def entry_barrier():
    sem = pltpu.get_barrier_semaphore()
    where = [chip(part, 0, step + 1) for part in PARTS for step in PARTS] + [partner()]
    for dev in where:
        pl.semaphore_signal(sem, inc=1, device_id=dev, device_id_type=pl.DeviceIdType.MESH)
    pl.semaphore_wait(sem, len(where))

def block_at(q, np_in, np_out, of_s):
    n_in, n_out = PAIR * np_in, PAIR * np_out
    past = min(q // EARLY, 1) if isinstance(q, int) else jnp.minimum(lax.div(q, EARLY), 1)
    in_s = q * n_out - q * (q - 1) + np_in * (np_in + 1) * past
    in_a = EARLY * n_out - EARLY * (EARLY - 1) + q * n_in - q * (q - 1)
    return of_s * in_s + (1 - of_s) * in_a

def decode(b, np_in, np_out):
    n_in, n_out = PAIR * np_in, PAIR * np_out
    at, was = 0, (0, 0)
    row, col = b, 0
    for q, in_s in [(q, 1) for q in range(EARLY)] + [(q, 0) for q in range(np_in)] + [(q, 1) for q in range(EARLY, np_out)]:
        now = (in_s * n_in + PAIR * q - at, in_s * np_in + q)
        hit = (b >= at).astype(jnp.int32)
        row = row + hit * (now[0] - was[0])
        col = col + hit * (now[1] - was[1])
        was = now
        at += in_s * n_out + (1 - in_s) * n_in - PAIR * q
    is_g = (b >= at).astype(jnp.int32)
    off = (b - at) * is_g
    row = row + is_g * (lax.rem(off, n_in) - row)
    col = jnp.minimum(col + is_g * (np_in + lax.div(off, n_in) - col), np_in + np_out - 1)
    in_s = (col >= np_in).astype(jnp.int32)
    old = in_s * ((col - np_in) * n_out + row - n_in) + (1 - in_s) * (col * n_in + row)
    return (1 - is_g) * old, is_g

def front_kernel(np_in, np_out, n_dp, cuts, order, a_hbm, g_hbm, s_hbm, ao_hbm, blocks, quarter, acc, full, agt, own, flip, old, ra, rb, rc, rd, ra2, rb2, rc2, rd2, r3, lsem, ssem, rsem, psem):
    p = lax.axis_index('mp')
    ns = a_hbm.shape[0]
    n_in, n_out = PAIR * np_in, PAIR * np_out
    n_col = np_in + np_out
    n_slot = flip.shape[0]

    def column(i, par):
        src, q = (a_hbm, i) if i < np_in else (g_hbm, i - np_in)
        return src.at[:, pl.ds(pl.multiple_of((PAIR * q + par) * BW, BW), BW)]
    def pair_of(i):
        return (i // PAIR, i % PAIR) if i < np_in else ((np_in + 1) // PAIR + (i - np_in) // PAIR, (i - np_in) % PAIR)
    def mine_at(i):
        z, h = pair_of(i)
        return own.at[z, :, h * BW:(h + 1) * BW]
    mine = [pltpu.make_async_copy(column(i, p), mine_at(i), lsem.at[i]) for i in range(n_col)]
    theirs = [pltpu.make_async_copy(column(i, 1 - p), flip.at[i % n_slot], lsem.at[n_col + i]) for i in range(n_col)]
    of_a = range(block_at(0, np_in, np_out, 0), block_at(np_in, np_in, np_out, 0))
    n_old = block_at(np_out, np_in, np_out, 1)
    mine_rows = [rows_at(along(part, 1) * ROWS + along(part, 2) * SUBL, SUBL) for part in PARTS]
    olds = []
    for j in range(-(-n_old // RING)):
        m, part = divmod(j, 3)
        at, _ = decode(j * RING + along(part, 0), np_in, np_out)
        src = ao_hbm if j * RING in of_a else s_hbm
        olds.append(pltpu.make_async_copy(src.at[at, mine_rows[part]], old.at[m, part], lsem.at[PAIR * n_col + j]))
    for c in theirs[:n_slot] + mine:
        c.start()
    entry_barrier()
    def transpose(src, i, par):
        for kc in range(ns // PW):
            agt[i * (ns // PW) + kc, pl.ds(pl.multiple_of(par * BW, BW), BW), :] = src[kc * PW:(kc + 1) * PW, :].T
    for i in range(n_col):
        theirs[i].wait()
        transpose(flip.at[i % n_slot], i, 1 - p)
        if i + n_slot < n_col:
            theirs[i + n_slot].start()
    for c in olds:
        c.start()
    for i in range(n_col):
        mine[i].wait()
        transpose(mine_at(i), i, p)

    def gram(z, row0, lo, hi, starts, scale):
        n = len(starts)
        rhs = own.at[z, :, :n * BW]
        def some(i):
            lhs = jnp.concatenate([agt[(row0 + i) * (ns // PW) + kc] for kc in range(ns // PW)], 1)
            prod = lax.dot_general(lhs, rhs[...], NN, preferred_element_type=F32) * scale
            for c in reversed(range(n)):
                for h in HALVES:
                    b = starts[c] + PAIR * (i - lo) + h
                    acc[lax.div(b, GROUP), lax.div(lax.rem(b, GROUP), RING), lax.rem(b, RING)] = prod[h * BW:(h + 1) * BW, c * BW:(c + 1) * BW]
        each(lo, hi, some)
    share_of_new = (1.0 - FACTOR_DECAY) / (ns * n_dp)
    n_pair = (np_in + 1) // PAIR
    start_of = lambda q, of_s: block_at(q, np_in, np_out, of_s)
    def grams(of_s, qs):
        n_pan = np_out if of_s else np_in
        for q in qs:
            both = [x for x in (q, q + 1) if x < n_pan]
            gram(n_pair * of_s + q // PAIR, np_in * of_s, q, n_pan, [start_of(x, of_s) - PAIR * (x - q) for x in both], share_of_new)
    def grads(qs):
        base = (np_in + np_out) * (np_in + np_out + 1) - np_out * n_in
        for q in qs:
            both = [x for x in (q, q + 1) if x < np_out]
            gram(n_pair + q // PAIR, 0, 0, np_in, [base + x * n_in for x in both], 1.0 / (ns * n_dp))

    def share(buf, ms, part, phase, coord):
        c1, e = along(part, 0), along(part, 1)
        if phase == 0:
            return buf.at[ms, part, coord]
        return buf.at[ms, part, c1, rows_at(coord * ROWS, ROWS) if phase == 1 else rows_at(e * ROWS + coord * SUBL, SUBL)]
    def cut(buf, ms, part, phase, coord, half):
        if phase == 0:
            return buf.at[ms, part, coord, pl.ds(half * HALF, HALF)]
        return buf.at[ms, part, along(part, 0), rows_at(coord * ROWS + half * MB, MB)]
    firsts = ((ra, rb), (ra2, rb2))
    seconds = ((rc, rd), (rc2, rd2))
    n_copy = 21
    def round_steps(k):
        m0, m1 = cuts[k], cuts[k + 1]
        ms = pl.ds(m0, m1 - m0)
        late = k == len(cuts) - 2
        def copy(part, kind, phase, i):
            c = along(part, phase)
            step = i + 1 if kind == 2 or kind == 3 and phase else UPDOWN[i]
            if kind == 0:
                src, dst = cut(acc, ms, part, phase, turn(c, 2), i), firsts[phase][i].at[ms, part]
            elif kind == 1:
                src, dst = share(acc, ms, part, phase, turn(c, step)), seconds[phase][i].at[ms, part]
            elif kind == 2:
                src, dst = share(acc, ms, part, phase, turn(c, step)), r3.at[i, ms, part]
            else:
                src = share(full, ms, part, phase, c) if kind == 3 else cut(full, ms, part, 0, turn(c, 4 - step), i)
                dst = src
            s = (k * 3 + part) * n_copy + (0, 4, 8, 11, 19)[kind] + (PAIR * phase + i if kind < 2 else 3 * (2 - phase) + i if kind == 3 else i)
            return remote(src, dst, ssem.at[s], rsem.at[s], chip(part, phase, step))
        every, near = PARTS, HALVES
        def go(part, kind, phase, which):
            for i in which:
                copy(part, kind, phase, i).start()
        def come(part, kind, phase, which):
            for i in which:
                copy(part, kind, phase, i).wait_recv()
        def add(part, c1, rows, *srcs):
            def some(m):
                v = acc[m, part, c1, rows]
                for s in srcs:
                    v = v + s(m)
                acc[m, part, c1, rows] = v
            each(m0, m1, some)
        def fold(phase):
            for part in PARTS:
                c = along(part, phase)
                for z in HALVES:
                    come(part, 0, phase, (z,))
                    u = turn(c, UPDOWN[z])
                    buf = firsts[phase][z]
                    if phase == 0:
                        add(part, u, pl.ds(z * HALF, HALF), lambda m: buf[m, part])
                    else:
                        add(part, along(part, 0), rows_at(u * ROWS + z * MB, MB), lambda m: buf[m, part])
                    go(part, 1, phase, (z,))
        def gain(phase):
            for part in PARTS:
                come(part, 1, phase, near)
                b0, b1 = seconds[phase]
                rows = pl.ds(0, BW) if phase == 0 else rows_at(along(part, 1) * ROWS, ROWS)
                add(part, along(part, 0), rows, lambda m: b0[m, part], lambda m: b1[m, part])
                go(part, phase * 2, 1 + phase, every if phase else near)
        def done():
            for part in PARTS:
                come(part, 2, 2, every)
                c1, rows = along(part, 0), mine_rows[part]
                def some(m):
                    v = acc[m, part, c1, rows] + (r3[0, m, part] + r3[1, m, part] + r3[2, m, part])
                    if not late:
                        _, is_g = decode((m * 3 + part) * RING + c1, np_in, np_out)
                        v = v + jnp.where(is_g == 1, 0.0, old[m, part] * FACTOR_DECAY)
                    full[m, part, c1, rows] = v
                each(m0, m1, some)
                go(part, 3, 2, every)
        def widen():
            for part in PARTS:
                come(part, 3, 2, every)
                go(part, 3, 1, every)
        def near_go():
            for part in PARTS:
                come(part, 3, 1, every)
                go(part, 3, 0, near)
        def relay():
            for z in near:
                for part in PARTS:
                    come(part, 3, 0, (z,))
                    go(part, 4, 0, (z,))
        def whole():
            for part in PARTS:
                come(part, 4, 0, near)
                swap(part).start()
                keep(part).start()
        def swap(part):
            return remote(full.at[ms, part], blocks.at[p, ms, part], psem.at[0, k, part], psem.at[1, k, part], partner())
        def keep(part):
            return pltpu.make_async_copy(full.at[ms, part], blocks.at[p, ms, part], psem.at[2, k, part])
        def wide():
            for part in PARTS:
                come(part, 3, 1, every)
                swap_quarter(part).start()
                def some(m):
                    quarter[p, m - m0, part] = full[m, part, along(part, 0)]
                each(m0, m1, some)
        def swap_quarter(part):
            return remote(full.at[ms, part, along(part, 0)], quarter.at[p, :, part], psem.at[0, k, part], psem.at[1, k, part], partner())
        def start():
            for part in PARTS:
                go(part, 0, 0, near)
        kinds = [(0, 0, near), (1, 0, near), (0, 1, near), (1, 1, near), (2, 2, every), (3, 2, every), (3, 1, every), (3, 0, near), (4, 0, near)]
        def settle():
            for part in PARTS:
                for kind, phase, which in kinds[:len(kinds) - PAIR * late]:
                    for i in which:
                        copy(part, kind, phase, i).wait_send()
                c = swap_quarter(part) if late else swap(part)
                c.wait_recv()
                c.wait_send()
                if not late:
                    keep(part).wait()
        return [start, lambda: fold(0), lambda: gain(0), lambda: fold(1), lambda: gain(1), done, widen] + ([wide] if late else [near_go, relay, whole]), settle
    rounds = [round_steps(k) for k in range(len(cuts) - 1)]
    chunks = [lambda: grams(1, (0,)), lambda: (grams(1, (2,)), grams(0, range(0, np_in, PAIR))), lambda: (grams(1, range(EARLY, np_out, PAIR)), grads((0,))), lambda: grads(range(2, np_out, PAIR)),
        lambda: [c.wait() for c in olds]]
    for k, z in order:
        todo = chunks if k < 0 else rounds[k][0]
        if 0 <= z < len(todo):
            todo[z]()
    for _, settle in rounds:
        settle()

def front(a_loc, g_loc, a_old3, s_old3, n_dp, cuts):
    ns, c_in = a_loc.shape
    np_in, np_out = c_in // PW, g_loc.shape[1] // PW
    V = lambda *s: pltpu.VMEM(s, F32)
    B = lambda *s: pltpu.VMEM(s, BF)
    D = lambda *s: pltpu.SemaphoreType.DMA(s)
    hb = pl.BlockSpec(memory_space=pl.ANY)
    vb = pl.BlockSpec(memory_space=pltpu.VMEM)
    nm = cuts[-1]
    order = [(k, x - lag) for x in range(13) for k, lag in ((-1, 0), (0, 0), (1, 3), (2, 3))]
    slab = lambda n: [V(nm, 3, n, BW)] * 2
    n_col = np_in + np_out
    s_blk, a_blk = s_old3.reshape(-1, BW, BW), a_old3.reshape(-1, BW, BW)
    n_old = -(-block_at(np_out, np_in, np_out, 1) // RING)
    f32 = lambda *s: jax.ShapeDtypeStruct(s, F32)
    return pl.pallas_call(functools.partial(front_kernel, np_in, np_out, n_dp, cuts, order),
        out_shape=(f32(2, cuts[-2], 3, RING, BW, BW), f32(2, nm - cuts[-2], 3, BW, BW)),
        in_specs=[hb] * 4, out_specs=(hb, vb),
        scratch_shapes=[*[V(nm, 3, RING, BW, BW)] * 2, B(n_col * ns // PW, PW, PW), B((np_in + 1) // PAIR + (np_out + 1) // PAIR, ns, PW), B(4, ns, BW), V(cuts[-2], 3, SUBL, BW),
            *slab(HALF), *slab(BW), *slab(MB), *slab(ROWS), V(3, nm, 3, SUBL, BW), D(PAIR * n_col + n_old), *[D(63 * (len(cuts) - 1))] * 2, D(3, len(cuts) - 1, 3)],
        compiler_params=pltpu.CompilerParams(collective_id=0, has_side_effects=True, vmem_limit_bytes=67043328), name="front")(a_loc, g_loc, s_blk, a_blk)

def solve_kernel(np_in, np_out, n_dp, damp, cuts, early, quarter, fin, full, tmat, mat, linv, inv_all, lsp, xw, zin, pack, ssem, rsem, psem, osem):
    p = lax.axis_index('mp')
    d = lax.axis_index('dp')
    n_own = np_in * BW // n_dp
    n_in, n_out = PAIR * np_in, PAIR * np_out
    first = [pltpu.make_async_copy(early.at[par], full.at[par, pl.ds(0, cuts[-2])], osem.at[par]) for par in HALVES]
    for c in first:
        c.start()
    entry_barrier()
    ms = pl.ds(cuts[-2], cuts[-1] - cuts[-2])
    def last(par, part, z, on):
        c = along(part, 0)
        ref = full.at[par, ms, part, turn(c, 3 - PAIR * z), pl.ds(z * HALF, HALF)] if on else full.at[par, ms, part, c]
        s = 30 + (par * 3 + part) * 4 + PAIR * on + z
        return remote(ref, ref, ssem.at[s], rsem.at[s], chip(part, 0, UPDOWN[z]))
    every = [(z, part, par) for z in HALVES for part in PARTS for par in HALVES]
    @pl.when(p == 1)
    def _():
        for part in PARTS:
            for par in HALVES:
                def put(m):
                    full[par, m, part, along(part, 0)] = quarter[par, m - cuts[-2], part]
                each(cuts[-2], cuts[-1], put)
        for z, part, par in every:
            last(par, part, z, 0).start()
    for c in first:
        c.wait()

    def block(par, b):
        return full[par, lax.div(b, GROUP), lax.div(lax.rem(b, GROUP), RING), lax.rem(b, RING)]

    base_g = np_out * (np_out + 1) + np_in * (np_in + 1)
    npan = np_out - (np_out - np_in) * p
    eye = jnp.where(lax.broadcasted_iota(jnp.int32, (BW, BW), 0) == lax.broadcasted_iota(jnp.int32, (BW, BW), 1), damp, 0.0)

    def load(q):
        base = block_at(q, np_in, np_out, 1 - p)
        slot = lax.rem(q, PAIR)
        for par in HALVES:
            cols = pl.ds(par * BW, BW)
            def rows(i):
                for h in HALVES:
                    tmat[slot, i, h * BW:(h + 1) * BW, cols] = block(par, base + PAIR * (i - q) + h)
            each(q, npan, rows)
            tmat[slot, q, cols, cols] = tmat[slot, q, cols, cols] + eye

    lsp_spare = lsp.shape[1] - 1
    def ltile(i, k):
        return lax.div(i * (i - 1), PAIR) + k

    def update(i, k, q, ok):
        slot = lax.rem(q, PAIR)
        at = ok * i + (1 - ok) * np_out
        prod = stack_dot(pieces(lsp, ok * ltile(i, k)), pieces(lsp, ok * ltile(q, k)), NT)
        tmat[slot, at] = tmat[slot, at] - prod

    def task(s, q):
        left = jnp.maximum(npan - 1 - q, 1)
        turn = lax.div(s, left)
        ok = (turn <= q).astype(jnp.int32) * jnp.minimum(q, 1) * jnp.minimum(npan - 1 - q, 1)
        k = turn - 1 + q * (1 - jnp.minimum(turn, 1))
        update(q + 1 + lax.rem(s, left), k, q + jnp.minimum(turn, 1), ok)

    load(0)

    def panel(k):
        q = lax.div(k, PAIR)
        h = lax.rem(k, PAIR)
        slot = lax.rem(q, PAIR)
        @pl.when(h == 0)
        def _():
            mat[...] = tmat[slot, q, :BW, :BW]
        factor_block(mat, linv, lambda t: task(h * SUBL + t, q))
        @pl.when(h == 0)
        def _():
            inv0 = linv[...]
            inv0s = split3(inv0)
            l10 = dot6(split3(tmat[slot, q, BW:, :BW]), inv0s, NT)
            l10s = split3(l10)
            mat[...] = tmat[slot, q, BW:, BW:] - dot6(l10s, l10s, NT)
            inv_all[q, :BW, :BW] = inv0
            inv_all[q, :BW, BW:] = jnp.zeros((BW, BW), F32)
            inv_all[q, BW:, :BW] = dot6(l10s, inv0s, NN)
        @pl.when((h == 1) & (q < npan - 1))
        def _():
            each(MB, (npan - 1 - q) * (q + 1), lambda s: task(s, q))
        @pl.when(h == 1)
        def _():
            inv1 = linv[...]
            inv_all[q, BW:, BW:] = inv1
            inv_all[q, BW:, :BW] = -dot6(split3(inv1), split3(inv_all[q, BW:, :BW]), NN)
            invs = split3(inv_all[q])
            def below(s):
                for u in HALVES:
                    i = q + 1 + PAIR * s + u
                    ok = (i < npan).astype(jnp.int32)
                    for z, v in enumerate(split3(stack_dot(split3(tmat[slot, ok * i + (1 - ok) * np_out]), invs, NT))):
                        lsp[z, ok * ltile(i, q) + (1 - ok) * lsp_spare] = v
            upto(lax.div(npan - q, PAIR), below)
        @pl.when((h == 1) & (q < npan - 1))
        def _():
            @pl.when(q == 0)
            def _():
                load(1)
            update(q + 1, q, q + 1, 1)
            @pl.when(q < npan - 2)
            def _():
                load(q + 2)
    upto(PAIR * npan, panel)
    @pl.when(p == 1)
    def _():
        for z, part, par in every:
            last(par, part, z, 0).wait_recv()
            last(par, part, z, 1).start()

    zcopy = remote(zin.at[0], zin.at[1], psem.at[0, 1], psem.at[1, 1], partner())
    @pl.when(p == 1)
    def _():
        row = lax.broadcasted_iota(jnp.int32, (MB, PW), 0)
        lane = lax.broadcasted_iota(jnp.int32, (MB, PW), 1)
        par = lax.div(row, SUBL)
        idx = lax.rem(row, SUBL)
        col = d * n_own + idx
        for q in range(np_in):
            hit = (idx < n_own) & (lax.div(col, BW) == q) & (lane == par * BW + lax.rem(col, BW))
            xw[q] = jnp.where(hit, 1.0, 0.0)
    @pl.when(p == 0)
    def _():
        zcopy.wait_recv()
        def cp(q):
            xw[q] = zin[1, q]
        upto(np_out, cp)

    def spread(x, lo, hi, tile, dims):
        xs = split3(x)
        def some(i):
            for u in range(RING):
                j = lo + RING * i + u
                ok = (j < hi).astype(jnp.int32)
                at = ok * j + (1 - ok) * np_out
                xw[at] = xw[at] - stack_dot(xs, pieces(lsp, ok * tile(j)), dims)
        upto(lax.div(hi - lo + RING - 1, RING), some)
    def fwd(q):
        y = stack_dot(split3(xw[q]), split3(inv_all[q]), NT)
        xw[q] = y
        spread(y, q + 1, npan, lambda j: ltile(j, q), NT)
    upto(npan, fwd)
    def back(s):
        q = npan - 1 - s
        x = stack_dot(split3(xw[q]), split3(inv_all[q]), NN)
        xw[q] = x
        spread(x, 0, q, lambda j: ltile(q, j), NN)
    upto(npan, back)

    xcopy = remote(pack.at[1], pack.at[0], psem.at[0, 2], psem.at[1, 2], partner())
    @pl.when(p == 1)
    def _():
        for z, part, par in every:
            last(par, part, z, 1).wait_recv()
        def zq(q):
            for par in HALVES:
                acc = jnp.zeros((MB, BW), F32)
                for i in range(n_in):
                    acc = acc + stack_dot(split3(xw[i // PAIR, :, (i % PAIR) * BW:(i % PAIR + 1) * BW]), split3(block(par, base_g + q * n_in + i)), NN)
                zin[0, q, :, par * BW:(par + 1) * BW] = acc
        upto(np_out, zq)
        zcopy.start()
        xcopy.wait_recv()
        zcopy.wait_send()
    @pl.when(p == 0)
    def _():
        for par in reversed(HALVES):
            pack[par, np_out * n_own:] = jnp.zeros((pack.shape[1] - np_out * n_own, PW), F32)
            for q in range(np_out):
                pack[par, q * n_own:(q + 1) * n_own] = xw[q, par * SUBL:par * SUBL + n_own]
            if par == 1:
                xcopy.start()
    n_t = fin.shape[4]
    for t in range(PAIR * (pack.shape[1] // SUBL)):
        part, z = divmod(t, n_t)
        half = t % PAIR
        fin[(part, *(along(part, ph) for ph in PARTS), z)] = pack[0, t // PAIR * SUBL:(t // PAIR + 1) * SUBL, half * BW:(half + 1) * BW]
    def fcopy(part, j):
        c1, e, f = (along(part, ph) for ph in PARTS)
        if j < 6:
            phase, step = 2 - j // 3, j % 3 + 1
            ref = fin.at[part, c1, e, f] if phase == 2 else fin.at[part, c1, e]
        else:
            z = j % PAIR
            phase, step = 0, UPDOWN[z]
            ref = fin.at[part, c1] if j < 8 else fin.at[part, turn(c1, 3 - PAIR * z), pl.ds(PAIR * z, 2)]
        s = part * 10 + j
        return remote(ref, ref, ssem.at[s], rsem.at[s], chip(part, phase, step))
    def fstep(came, js):
        def part_fn(part):
            for j in came:
                fcopy(part, j).wait_recv()
            for j in js:
                fcopy(part, j).start()
        for part in PARTS:
            part_fn(part)
    fstep((), (0, 1, 2))
    fstep((0, 1, 2), (3, 4, 5))
    fstep((3, 4, 5), (6, 7))
    def frelay(part):
        for z in HALVES:
            fcopy(part, 6 + z).wait_recv()
            fcopy(part, 8 + z).start()
    for part in PARTS:
        frelay(part)
    fstep((8, 9), ())
    for part in PARTS:
        for j in range(10):
            fcopy(part, j).wait_send()
    @pl.when(p == 1)
    def _():
        for z, part, par in every:
            last(par, part, z, 0).wait_send()
            last(par, part, z, 1).wait_send()
    @pl.when(p == 0)
    def _():
        xcopy.wait_send()

def solve(early, quarter, np_in, np_out, n_dp, damp, cuts):
    n_own = np_in * BW // n_dp
    n_row = -(-np_out * n_own // SUBL)
    n_t = -(-PAIR * n_row // 3)
    n_tile = np_out * (np_out - 1) // PAIR + 1
    V = lambda *s: pltpu.VMEM(s, F32)
    D = lambda *s: pltpu.SemaphoreType.DMA(s)
    hb = pl.BlockSpec(memory_space=pl.ANY)
    vb = pl.BlockSpec(memory_space=pltpu.VMEM)
    f32 = lambda *s: jax.ShapeDtypeStruct(s, F32)
    return pl.pallas_call(functools.partial(solve_kernel, np_in, np_out, n_dp, damp, cuts),
        out_shape=f32(3, RING, RING, RING, n_t, SUBL, BW), in_specs=[hb, vb], out_specs=vb,
        scratch_shapes=[V(2, cuts[-1], 3, RING, BW, BW), V(2, np_out + 1, PW, PW), V(BW, BW), V(BW, BW), V(np_out, PW, PW), pltpu.VMEM((3, n_tile, PW, PW), BF), V(np_out + 1, MB, PW),
            V(2, np_out, MB, PW), V(2, n_row * SUBL, PW), D(54), D(54), D(2, 3), D(2)],
        compiler_params=pltpu.CompilerParams(collective_id=1, has_side_effects=True, vmem_limit_bytes=67043328), name="solve")(early, quarter)

def finish_kernel(np_in, np_out, n_own, w_hbm, blocks, fin, w_out, a_out, s_out, wbuf, gath, cols_s, cols_a, up_s, up_a, isem, lsem, usem, wsem, csem):
    p = lax.axis_index('mp')
    wload = pltpu.make_async_copy(w_hbm, wbuf, isem)
    wload.start()
    sets = [(s_out, cols_s, up_s, np_out, 1), (a_out, cols_a, up_a, np_in, 0)]
    jobs, n = [], 0
    for out, cols, up, n_pan, of_s in sets:
        for q in range(n_pan):
            base = block_at(q, np_in, np_out, of_s) // PAIR
            low = pltpu.make_async_copy(blocks.at[p, pl.ds(base, n_pan - q)], cols.at[q, pl.ds(q, n_pan - q)], lsem.at[n])
            ups = [pltpu.make_async_copy(blocks.at[par, pl.ds(base + 1, n_pan - 1 - q), p], up.at[par, q, pl.ds(q + 1, n_pan - 1 - q)], usem.at[par, n]) for par in HALVES] if q < n_pan - 1 else []
            send = pltpu.make_async_copy(cols.at[q], out.at[q], csem.at[n])
            jobs.append((low, ups, send, cols, up, q))
            n += 1
    for low, ups, *_ in jobs:
        for c in (*ups, low):
            c.start()
    n_t = fin.shape[4]
    def tile(t, c):
        part, z = divmod(t, n_t)
        return fin[(part, *(c + c)[part:part + 3], z)]
    wload.wait()
    def weights(q):
        lo, hi = q * n_own // SUBL, ((q + 1) * n_own - 1) // SUBL
        for half in HALVES:
            def fill(z):
              for y in range(RING):
                vals = []
                for x in range(RING):
                    c = (x, y, z)
                    v = jnp.concatenate([tile(PAIR * r + half, c) for r in range(lo, hi + 1)], 0)
                    at = q * n_own - lo * SUBL
                    vals.append(v[at:at + n_own])
                gath[rows_at((z * RING + y) * RING * n_own, RING * n_own)] = jnp.concatenate(vals, 0)
            upto(RING, fill)
            for b in range(np_in):
                r = slice((PAIR * q + half) * BW, (PAIR * q + half + 1) * BW)
                wbuf[b, r] = wbuf[b, r] - LEARN_RATE * gath[b * BW:(b + 1) * BW].T
    for q in range(np_out // PAIR):
        weights(q)
    for low, ups, send, cols, up, q in jobs:
        low.wait()
        for c in ups:
            c.wait()
    for low, ups, send, cols, up, q in jobs:
        for q2 in range(q):
            for par in HALVES:
                cols[q, q2, par] = up[par, q2, q].T
        send.start()
    for q in range(np_out // PAIR, np_out):
        weights(q)
    wsend = pltpu.make_async_copy(wbuf, w_out, wsem)
    wsend.start()
    for low, ups, send, *_ in jobs:
        send.wait()
    wsend.wait()

def finish(w3, blocks, fin, np_in, np_out, n_dp):
    V = pltpu.VMEM
    D = pltpu.SemaphoreType.DMA
    hb = pl.BlockSpec(memory_space=pl.ANY)
    vb = pl.BlockSpec(memory_space=V)
    n_job = np_in + np_out
    square = lambda n: (n, n, 2, BW, BW)
    w_new, a_new, s_new = pl.pallas_call(functools.partial(finish_kernel, np_in, np_out, np_in * BW // n_dp),
        out_shape=(jax.ShapeDtypeStruct(w3.shape, F32), jax.ShapeDtypeStruct(square(np_in), F32), jax.ShapeDtypeStruct(square(np_out), F32)),
        in_specs=[hb, hb, vb], out_specs=(hb, hb, hb),
        scratch_shapes=[V(w3.shape, F32), V((np_in * BW, BW), F32), V(square(np_out), F32), V(square(np_in), F32), V((2, np_out, np_out, BW, BW), F32), V((2, np_in, np_in, BW, BW), F32),
            D, D((n_job,)), D((2, n_job)), D, D((n_job,))],
        compiler_params=pltpu.CompilerParams(vmem_limit_bytes=63 * 2**20), name="outputs")(w3, blocks.reshape(2, -1, 2, BW, BW), fin)
    return w_new, a_new.reshape(np_in, -1, BW), s_new.reshape(np_out, -1, BW)


def solution(mesh):
    n_dp = mesh.shape['dp']

    def local_step(a_loc, g_loc, w_loc, a_old_loc, s_old_loc):
        np_in = a_loc.shape[1] // PW
        np_out = g_loc.shape[1] // PW
        n_in, n_out = PAIR * np_in, PAIR * np_out
        early = np_in * (np_in + 1) + np_out * (np_out + 1)
        cuts = (0, 2, -(-early // GROUP), (early + n_in * np_out) // GROUP)
        panels = lambda x: x.transpose(1, 0, 2)
        blocks, quarter = front(a_loc, g_loc, panels(a_old_loc), panels(s_old_loc), n_dp, cuts)
        fin = solve(blocks, quarter, np_in, np_out, n_dp, DAMP_SHIFT, cuts)
        return tuple(panels(x) for x in finish(panels(w_loc), blocks, fin, np_in, np_out, n_dp))

    spec_rows = P('dp', None)
    spec_cyc = P(None, 'mp', None)
    return jax.shard_map(local_step, mesh=mesh, in_specs=(spec_rows, spec_rows, spec_cyc, spec_cyc, spec_cyc), out_specs=(spec_cyc, spec_cyc, spec_cyc), check_vma=False)
```

time: 3270 us -> 262 us (0.08)
  waiting for transfers between devices: 1420 us -> 0 us
  other arithmetic: 1040 us -> 0 us
  matrix products: 412 us -> 0 us
  local copies, waits for them, and re-layouts: 340 us -> 0 us
  Pallas kernels: 0 us -> 261 us
    psum x67 -> x0, waiting for transfers between devices: 1420 us -> none  [the longest x42 711 us: solve_cyclic(): solved = lax.psum(jnp.where(is_owner, solved, 0.0), 'mp')]
    another operation x143 -> x0, other arithmetic: 803 us -> none  [the longest x72 301 us: factor_cyclic(): diag_fac = jnp.linalg.cholesky(column[:blk_width])]
    dot_general x73 -> x0, matrix products: 308 us -> none  [the longest x22 104 us: factor_cyclic(): jnp.einsum('in,tjn->itj', panel_vals[blk_width:], coupling, precision=PRE...]
    pallas_call x0 -> x3, Pallas kernels: none -> 261 us  [the longest x1 130 us: solve(): pl.pallas_call(functools.partial(solve_kernel, np_in, np_out, n_dp, damp,...]
    unnamed x545 -> x0, local copies, waits for them, and re-layouts: 158 us -> none
    another operation x70 -> x0, matrix products: 104 us -> none  [the longest x48 75.4 us: solve_cyclic(): lax.linalg.triangular_solve(diag_fac, current[:, col_start:col_start + bl...]
    slice x131 -> x0, local copies, waits for them, and re-layouts: 78.3 us -> none  [the longest x24 26.4 us: solve_cyclic(): trail_cols[:, blk_width:]]
    dynamic_update_slice x38 -> x0, other arithmetic: 61.1 us -> none  [the longest x16 27.3 us: solve_cyclic(): current = lax.dynamic_update_slice(current, head_cols, (0, 0))]
  transfers between devices with their start and end apart: 67 -> 0, of which waited for: 62 -> 0; matrix products, arithmetic and copies ran while one was open for 17% -> 0% of each run, Pallas kernels for 0% -> 0%
where the time goes in v4:
time: 262 us
  Pallas kernels  261 us (100%)
    pallas_call x1, Pallas kernels, solve(): pl.pallas_call(functools.partial(solve_kernel, np_in, np_out, n_dp, damp,...  130 us
    pallas_call x1, Pallas kernels, front(): pl.pallas_call(functools.partial(front_kernel, np_in, np_out, n_dp, cuts,...  116 us
    pallas_call x1, Pallas kernels, finish(): pl.pallas_call(functools.partial(finish_kernel, np_in, np_out, np_in * BW...  14.9 us

profile of v4, /device:TPU:0, one launch (start us, length us, event | category | flops | bytes accessed | tf_op | source)
XLA Modules:
  0.0 261.6 jit_solution(11626103728935377093)
XLA Ops:
  0.6 115.8 %front.1 = (f32[2,9,3,4,128,128]{5,4,3,2,1,0:T(8,128)}, f32[2,4,3,128,128]{4,3,2,1,0:T(8,128)}) custom-call(bf16[2048,768]{1,0:T(8,128)(2,1)} %a_hbm.1, bf16[2048,2304]{1,0:T(8,128)(2,1)} %g_hbm.1, f32[162,128,128]{2,1,0:T(8,128)} %bitcast.16, f32[18,128,128]{2,1,0:T(8,128)} %bitcast.18), custom_call_target="tpu_custom_call" | custom-call | tf_op jit(solution)/shard_map/front/pallas_call | solution.py:405
  116.5 130.1 %solve.1.fin = f32[3,4,4,4,5,8,128]{6,5,4,3,2,1,0:T(8,128)} custom-call(f32[2,9,3,4,128,128]{5,4,3,2,1,0:T(8,128)} %get-tuple-element.8.early, f32[2,4,3,128,128]{4,3,2,1,0:T(8,128)} %get-tuple-element.9.quarter), custom_call_target="tpu_custom_call" | custom-call | tf_op jit(solution)/shard_map/solve/pallas_call | solution.py:645
  246.6 14.9 %outputs.1 = (f32[3,2304,128]{2,1,0:T(8,128)}, f32[3,3,2,128,128]{4,3,2,1,0:T(8,128)}, f32[9,9,2,128,128]{4,3,2,1,0:T(8,128)}) custom-call(f32[3,2304,128]{2,1,0:T(8,128)} %bitcast.17, f32[2,54,2,128,128]{4,3,2,1,0:T(8,128)} %bitcast.15, f32[3,4,4,4,5,8,128]{6,5,4,3,2,1,0:T(8,128)} %solve.1.fin), custom_call_target="tpu_custom_call" | custom-call | tf_op jit(solution)/shard_map/outputs/pallas_call | solution.py:715

commit v5 on v4

--- a/solution.py
+++ b/solution.py
@@ -148,6 +148,9 @@
 def along(part, phase):
     return place(part, phase)[0]
 
+def both_ends(sems, *at):
+    return sems.at[(0, *at)], sems.at[(1, *at)]
+
 def chip(part, phase, step):
     c, stride = place(part, phase)
     return {'dp': lax.axis_index('dp') + (turn(c, step) - c) * stride}
@@ -202,7 +205,7 @@
         return (i // PAIR, i % PAIR) if i < np_in else ((np_in + 1) // PAIR + (i - np_in) // PAIR, (i - np_in) % PAIR)
     def mine_at(i):
         z, h = pair_of(i)
-        return own.at[z, :, h * BW:(h + 1) * BW]
+        return own.at[z, :, h * BW:h * BW + BW]
     mine = [pltpu.make_async_copy(column(i, p), mine_at(i), lsem.at[i]) for i in range(n_col)]
     theirs = [pltpu.make_async_copy(column(i, 1 - p), flip.at[i % n_slot], lsem.at[n_col + i]) for i in range(n_col)]
     of_a = range(block_at(0, np_in, np_out, 0), block_at(np_in, np_in, np_out, 0))
@@ -219,7 +222,7 @@
     entry_barrier()
     def transpose(src, i, par):
         for kc in range(ns // PW):
-            agt[i * (ns // PW) + kc, pl.ds(pl.multiple_of(par * BW, BW), BW), :] = src[kc * PW:(kc + 1) * PW, :].T
+            agt[i * (ns // PW) + kc, pl.ds(pl.multiple_of(par * BW, BW), BW), :] = src[kc * PW:kc * PW + PW, :].T
     for i in range(n_col):
         theirs[i].wait()
         transpose(flip.at[i % n_slot], i, 1 - p)
@@ -240,7 +243,7 @@
             for c in reversed(range(n)):
                 for h in HALVES:
                     b = starts[c] + PAIR * (i - lo) + h
-                    acc[lax.div(b, GROUP), lax.div(lax.rem(b, GROUP), RING), lax.rem(b, RING)] = prod[h * BW:(h + 1) * BW, c * BW:(c + 1) * BW]
+                    acc[lax.div(b, GROUP), lax.div(lax.rem(b, GROUP), RING), lax.rem(b, RING)] = prod[h * BW:h * BW + BW, c * BW:c * BW + BW]
         each(lo, hi, some)
     share_of_new = (1.0 - FACTOR_DECAY) / (ns * n_dp)
     n_pair = (np_in + 1) // PAIR
@@ -267,14 +270,14 @@
         return buf.at[ms, part, along(part, 0), rows_at(coord * ROWS + half * MB, MB)]
     firsts = ((ra, rb), (ra2, rb2))
     seconds = ((rc, rd), (rc2, rd2))
-    n_copy = 21
+    n_copy = 23
     def round_steps(k):
         m0, m1 = cuts[k], cuts[k + 1]
         ms = pl.ds(m0, m1 - m0)
         late = k == len(cuts) - 2
         def copy(part, kind, phase, i):
             c = along(part, phase)
-            step = i + 1 if kind == 2 or kind == 3 and phase else UPDOWN[i]
+            step = i + 1 if kind == 2 or kind == 3 and phase == 2 else UPDOWN[i]
             if kind == 0:
                 src, dst = cut(acc, ms, part, phase, turn(c, 2), i), firsts[phase][i].at[ms, part]
             elif kind == 1:
@@ -282,9 +285,9 @@
             elif kind == 2:
                 src, dst = share(acc, ms, part, phase, turn(c, step)), r3.at[i, ms, part]
             else:
-                src = share(full, ms, part, phase, c) if kind == 3 else cut(full, ms, part, 0, turn(c, 4 - step), i)
+                src = share(full, ms, part, phase, c) if kind == 3 else cut(full, ms, part, phase, turn(c, 4 - step), i)
                 dst = src
-            s = (k * 3 + part) * n_copy + (0, 4, 8, 11, 19)[kind] + (PAIR * phase + i if kind < 2 else 3 * (2 - phase) + i if kind == 3 else i)
+            s = (k * 3 + part) * n_copy + (0, 4, 8, 11, 19)[kind] + (PAIR * phase + i if kind < 2 or kind == 4 else 3 * (2 - phase) + i if kind == 3 else i)
             return remote(src, dst, ssem.at[s], rsem.at[s], chip(part, phase, step))
         every, near = PARTS, HALVES
         def go(part, kind, phase, which):
@@ -334,10 +337,15 @@
         def widen():
             for part in PARTS:
                 come(part, 3, 2, every)
-                go(part, 3, 1, every)
+                go(part, 3, 1, near)
+        def relay_wide():
+            for z in near:
+                for part in PARTS:
+                    come(part, 3, 1, (z,))
+                    go(part, 4, 1, (z,))
         def near_go():
             for part in PARTS:
-                come(part, 3, 1, every)
+                come(part, 4, 1, near)
                 go(part, 3, 0, near)
         def relay():
             for z in near:
@@ -350,22 +358,22 @@
                 swap(part).start()
                 keep(part).start()
         def swap(part):
-            return remote(full.at[ms, part], blocks.at[p, ms, part], psem.at[0, k, part], psem.at[1, k, part], partner())
+            return remote(full.at[ms, part], blocks.at[p, ms, part], *both_ends(psem, k, part), partner())
         def keep(part):
             return pltpu.make_async_copy(full.at[ms, part], blocks.at[p, ms, part], psem.at[2, k, part])
         def wide():
             for part in PARTS:
-                come(part, 3, 1, every)
+                come(part, 4, 1, near)
                 swap_quarter(part).start()
                 def some(m):
                     quarter[p, m - m0, part] = full[m, part, along(part, 0)]
                 each(m0, m1, some)
         def swap_quarter(part):
-            return remote(full.at[ms, part, along(part, 0)], quarter.at[p, :, part], psem.at[0, k, part], psem.at[1, k, part], partner())
+            return remote(full.at[ms, part, along(part, 0)], quarter.at[p, :, part], *both_ends(psem, k, part), partner())
         def start():
             for part in PARTS:
                 go(part, 0, 0, near)
-        kinds = [(0, 0, near), (1, 0, near), (0, 1, near), (1, 1, near), (2, 2, every), (3, 2, every), (3, 1, every), (3, 0, near), (4, 0, near)]
+        kinds = [(0, 0, near), (1, 0, near), (0, 1, near), (1, 1, near), (2, 2, every), (3, 2, every), (3, 1, near), (4, 1, near), (3, 0, near), (4, 0, near)]
         def settle():
             for part in PARTS:
                 for kind, phase, which in kinds[:len(kinds) - PAIR * late]:
@@ -376,10 +384,10 @@
                 c.wait_send()
                 if not late:
                     keep(part).wait()
-        return [start, lambda: fold(0), lambda: gain(0), lambda: fold(1), lambda: gain(1), done, widen] + ([wide] if late else [near_go, relay, whole]), settle
+        return [start, lambda: fold(0), lambda: gain(0), lambda: fold(1), lambda: gain(1), done, widen, relay_wide] + ([wide] if late else [near_go, relay, whole]), settle
     rounds = [round_steps(k) for k in range(len(cuts) - 1)]
-    chunks = [lambda: grams(1, (0,)), lambda: (grams(1, (2,)), grams(0, range(0, np_in, PAIR))), lambda: (grams(1, range(EARLY, np_out, PAIR)), grads((0,))), lambda: grads(range(2, np_out, PAIR)),
-        lambda: [c.wait() for c in olds]]
+    chunks = [lambda: grams(1, (0,)), lambda: (grams(1, (2,)), grams(0, range(0, np_in, PAIR))), lambda: (grams(1, range(EARLY, np_out, PAIR)), grads((0,))),
+        lambda: (grads(range(2, np_out, PAIR)), [c.wait() for c in olds])]
     for k, z in order:
         todo = chunks if k < 0 else rounds[k][0]
         if 0 <= z < len(todo):
@@ -396,7 +404,7 @@
     hb = pl.BlockSpec(memory_space=pl.ANY)
     vb = pl.BlockSpec(memory_space=pltpu.VMEM)
     nm = cuts[-1]
-    order = [(k, x - lag) for x in range(13) for k, lag in ((-1, 0), (0, 0), (1, 3), (2, 3))]
+    order = [(k, x - lag) for x in range(15) for k, lag in ((-1, 0), (0, 0), (1, 2), (2, 3))]
     slab = lambda n: [V(nm, 3, n, BW)] * 2
     n_col = np_in + np_out
     s_blk, a_blk = s_old3.reshape(-1, BW, BW), a_old3.reshape(-1, BW, BW)
@@ -406,7 +414,7 @@
         out_shape=(f32(2, cuts[-2], 3, RING, BW, BW), f32(2, nm - cuts[-2], 3, BW, BW)),
         in_specs=[hb] * 4, out_specs=(hb, vb),
         scratch_shapes=[*[V(nm, 3, RING, BW, BW)] * 2, B(n_col * ns // PW, PW, PW), B((np_in + 1) // PAIR + (np_out + 1) // PAIR, ns, PW), B(4, ns, BW), V(cuts[-2], 3, SUBL, BW),
-            *slab(HALF), *slab(BW), *slab(MB), *slab(ROWS), V(3, nm, 3, SUBL, BW), D(PAIR * n_col + n_old), *[D(63 * (len(cuts) - 1))] * 2, D(3, len(cuts) - 1, 3)],
+            *slab(HALF), *slab(BW), *slab(MB), *slab(ROWS), V(3, nm, 3, SUBL, BW), D(PAIR * n_col + n_old), *[D(69 * (len(cuts) - 1))] * 2, D(3, len(cuts) - 1, 3)],
         compiler_params=pltpu.CompilerParams(collective_id=0, has_side_effects=True, vmem_limit_bytes=67043328), name="front")(a_loc, g_loc, s_blk, a_blk)
 
 def solve_kernel(np_in, np_out, n_dp, damp, cuts, early, quarter, fin, full, tmat, mat, linv, inv_all, lsp, xw, zin, pack, ssem, rsem, psem, osem):
@@ -414,8 +422,8 @@
     d = lax.axis_index('dp')
     n_own = np_in * BW // n_dp
     n_in, n_out = PAIR * np_in, PAIR * np_out
-    first = [pltpu.make_async_copy(early.at[par], full.at[par, pl.ds(0, cuts[-2])], osem.at[par]) for par in HALVES]
-    for c in first:
+    first, then = [[pltpu.make_async_copy(early.at[par, pl.ds(cuts[z], cuts[z + 1] - cuts[z])], full.at[par, pl.ds(cuts[z], cuts[z + 1] - cuts[z])], osem.at[z, par]) for par in HALVES] for z in HALVES]
+    for c in first + then:
         c.start()
     entry_barrier()
     ms = pl.ds(cuts[-2], cuts[-1] - cuts[-2])
@@ -434,8 +442,13 @@
                 each(cuts[-2], cuts[-1], put)
         for z, part, par in every:
             last(par, part, z, 0).start()
-    for c in first:
-        c.wait()
+    def wait_for(copies):
+        for c in copies:
+            c.wait()
+    wait_for(first)
+    @pl.when(p == 1)
+    def _():
+        wait_for(then)
 
     def block(par, b):
         return full[par, lax.div(b, GROUP), lax.div(lax.rem(b, GROUP), RING), lax.rem(b, RING)]
@@ -451,7 +464,7 @@
             cols = pl.ds(par * BW, BW)
             def rows(i):
                 for h in HALVES:
-                    tmat[slot, i, h * BW:(h + 1) * BW, cols] = block(par, base + PAIR * (i - q) + h)
+                    tmat[slot, i, h * BW:h * BW + BW, cols] = block(par, base + PAIR * (i - q) + h)
             each(q, npan, rows)
             tmat[slot, q, cols, cols] = tmat[slot, q, cols, cols] + eye
 
@@ -502,11 +515,12 @@
             inv_all[q, BW:, :BW] = -dot6(split3(inv1), split3(inv_all[q, BW:, :BW]), NN)
             invs = split3(inv_all[q])
             def below(s):
-                for u in HALVES:
-                    i = q + 1 + PAIR * s + u
-                    ok = (i < npan).astype(jnp.int32)
-                    for z, v in enumerate(split3(stack_dot(split3(tmat[slot, ok * i + (1 - ok) * np_out]), invs, NT))):
-                        lsp[z, ok * ltile(i, q) + (1 - ok) * lsp_spare] = v
+                i = q + 1 + PAIR * s
+                ok = (i + 1 < npan).astype(jnp.int32)
+                both = jnp.concatenate([tmat[slot, i], tmat[slot, ok * (i + 1) + (1 - ok) * np_out]], 0)
+                for z, v in enumerate(split3(stack_dot(split3(both), invs, NT))):
+                    lsp[z, ltile(i, q)] = v[:PW]
+                    lsp[z, ok * ltile(i + 1, q) + (1 - ok) * lsp_spare] = v[PW:]
             upto(lax.div(npan - q, PAIR), below)
         @pl.when((h == 1) & (q < npan - 1))
         def _():
@@ -517,14 +531,18 @@
             @pl.when(q < npan - 2)
             def _():
                 load(q + 2)
-    upto(PAIR * npan, panel)
+    upto(1, panel)
+    @pl.when(p == 0)
+    def _():
+        wait_for(then)
+    each(1, PAIR * npan, panel)
     @pl.when(p == 1)
     def _():
         for z, part, par in every:
             last(par, part, z, 0).wait_recv()
             last(par, part, z, 1).start()
 
-    zcopy = remote(zin.at[0], zin.at[1], psem.at[0, 1], psem.at[1, 1], partner())
+    zcopy = remote(zin.at[0], zin.at[1], *both_ends(psem, 1), partner())
     @pl.when(p == 1)
     def _():
         row = lax.broadcasted_iota(jnp.int32, (MB, PW), 0)
@@ -563,7 +581,7 @@
         spread(x, 0, q, lambda j: ltile(q, j), NN)
     upto(npan, back)
 
-    xcopy = remote(pack.at[1], pack.at[0], psem.at[0, 2], psem.at[1, 2], partner())
+    xcopy = remote(pack.at[1], pack.at[0], *both_ends(psem, 2), partner())
     @pl.when(p == 1)
     def _():
         for z, part, par in every:
@@ -573,7 +591,7 @@
                 acc = jnp.zeros((MB, BW), F32)
                 for i in range(n_in):
                     acc = acc + stack_dot(split3(xw[i // PAIR, :, (i % PAIR) * BW:(i % PAIR + 1) * BW]), split3(block(par, base_g + q * n_in + i)), NN)
-                zin[0, q, :, par * BW:(par + 1) * BW] = acc
+                zin[0, q, :, par * BW:par * BW + BW] = acc
         upto(np_out, zq)
         zcopy.start()
         xcopy.wait_recv()
@@ -590,7 +608,7 @@
     for t in range(PAIR * (pack.shape[1] // SUBL)):
         part, z = divmod(t, n_t)
         half = t % PAIR
-        fin[(part, *(along(part, ph) for ph in PARTS), z)] = pack[0, t // PAIR * SUBL:(t // PAIR + 1) * SUBL, half * BW:(half + 1) * BW]
+        fin[(part, *(along(part, ph) for ph in PARTS), z)] = pack[0, t // PAIR * SUBL:t // PAIR * SUBL + SUBL, half * BW:half * BW + BW]
     def fcopy(part, j):
         c1, e, f = (along(part, ph) for ph in PARTS)
         if j < 6:
@@ -645,7 +663,7 @@
     return pl.pallas_call(functools.partial(solve_kernel, np_in, np_out, n_dp, damp, cuts),
         out_shape=f32(3, RING, RING, RING, n_t, SUBL, BW), in_specs=[hb, vb], out_specs=vb,
         scratch_shapes=[V(2, cuts[-1], 3, RING, BW, BW), V(2, np_out + 1, PW, PW), V(BW, BW), V(BW, BW), V(np_out, PW, PW), pltpu.VMEM((3, n_tile, PW, PW), BF), V(np_out + 1, MB, PW),
-            V(2, np_out, MB, PW), V(2, n_row * SUBL, PW), D(54), D(54), D(2, 3), D(2)],
+            V(2, np_out, MB, PW), V(2, n_row * SUBL, PW), D(54), D(54), D(2, 3), D(2, 2)],
         compiler_params=pltpu.CompilerParams(collective_id=1, has_side_effects=True, vmem_limit_bytes=67043328), name="solve")(early, quarter)
 
 def finish_kernel(np_in, np_out, n_own, w_hbm, blocks, fin, w_out, a_out, s_out, wbuf, gath, cols_s, cols_a, up_s, up_a, isem, lsem, usem, wsem, csem):
@@ -685,7 +703,7 @@
             upto(RING, fill)
             for b in range(np_in):
                 r = slice((PAIR * q + half) * BW, (PAIR * q + half + 1) * BW)
-                wbuf[b, r] = wbuf[b, r] - LEARN_RATE * gath[b * BW:(b + 1) * BW].T
+                wbuf[b, r] = wbuf[b, r] - LEARN_RATE * gath[b * BW:b * BW + BW].T
     for q in range(np_out // PAIR):
         weights(q)
     for low, ups, send, cols, up, q in jobs:

time: 262 us -> 251 us (0.958)
  Pallas kernels: 261 us -> 250 us
    pallas_call x1, Pallas kernels: 116 us -> 110 us  [front(): pl.pallas_call(functools.partial(front_kernel, np_in, np_out, n_dp, cuts,...]
    pallas_call x1, Pallas kernels: 130 us -> 125 us  [solve(): pl.pallas_call(functools.partial(solve_kernel, np_in, np_out, n_dp, damp,...]
where the time goes in v5:
time: 251 us
  Pallas kernels  250 us (100%)
    pallas_call x1, Pallas kernels, solve(): pl.pallas_call(functools.partial(solve_kernel, np_in, np_out, n_dp, damp,...  125 us
    pallas_call x1, Pallas kernels, front(): pl.pallas_call(functools.partial(front_kernel, np_in, np_out, n_dp, cuts,...  110 us
    pallas_call x1, Pallas kernels, finish(): pl.pallas_call(functools.partial(finish_kernel, np_in, np_out, np_in * BW...  14.9 us

profile of v5, /device:TPU:0, one launch (start us, length us, event | category | flops | bytes accessed | tf_op | source)
XLA Modules:
  0.0 251.1 jit_solution(15367090788255034797)
XLA Ops:
  0.6 110.1 %front.1 = (f32[2,9,3,4,128,128]{5,4,3,2,1,0:T(8,128)}, f32[2,4,3,128,128]{4,3,2,1,0:T(8,128)}) custom-call(bf16[2048,768]{1,0:T(8,128)(2,1)} %a_hbm.1, bf16[2048,2304]{1,0:T(8,128)(2,1)} %g_hbm.1, f32[162,128,128]{2,1,0:T(8,128)} %bitcast.16, f32[18,128,128]{2,1,0:T(8,128)} %bitcast.18), custom_call_target="tpu_custom_call" | custom-call | tf_op jit(solution)/shard_map/front/pallas_call | solution.py:413
  110.7 125.4 %solve.1.fin = f32[3,4,4,4,5,8,128]{6,5,4,3,2,1,0:T(8,128)} custom-call(f32[2,9,3,4,128,128]{5,4,3,2,1,0:T(8,128)} %get-tuple-element.8.early, f32[2,4,3,128,128]{4,3,2,1,0:T(8,128)} %get-tuple-element.9.quarter), custom_call_target="tpu_custom_call" | custom-call | tf_op jit(solution)/shard_map/solve/pallas_call | solution.py:663
  236.1 14.9 %outputs.1 = (f32[3,2304,128]{2,1,0:T(8,128)}, f32[3,3,2,128,128]{4,3,2,1,0:T(8,128)}, f32[9,9,2,128,128]{4,3,2,1,0:T(8,128)}) custom-call(f32[3,2304,128]{2,1,0:T(8,128)} %bitcast.17, f32[2,54,2,128,128]{4,3,2,1,0:T(8,128)} %bitcast.15, f32[3,4,4,4,5,8,128]{6,5,4,3,2,1,0:T(8,128)} %solve.1.fin), custom_call_target="tpu_custom_call" | custom-call | tf_op jit(solution)/shard_map/outputs/pallas_call | solution.py:733

commit v6 on v5

--- a/solution.py
+++ b/solution.py
@@ -207,7 +207,8 @@
         z, h = pair_of(i)
         return own.at[z, :, h * BW:h * BW + BW]
     mine = [pltpu.make_async_copy(column(i, p), mine_at(i), lsem.at[i]) for i in range(n_col)]
-    theirs = [pltpu.make_async_copy(column(i, 1 - p), flip.at[i % n_slot], lsem.at[n_col + i]) for i in range(n_col)]
+    turns = [*range(np_in, n_col), *range(np_in)]
+    theirs = [pltpu.make_async_copy(column(i, 1 - p), flip.at[z % n_slot], lsem.at[n_col + i]) for z, i in enumerate(turns)]
     of_a = range(block_at(0, np_in, np_out, 0), block_at(np_in, np_in, np_out, 0))
     n_old = block_at(np_out, np_in, np_out, 1)
     mine_rows = [rows_at(along(part, 1) * ROWS + along(part, 2) * SUBL, SUBL) for part in PARTS]
@@ -217,22 +218,25 @@
         at, _ = decode(j * RING + along(part, 0), np_in, np_out)
         src = ao_hbm if j * RING in of_a else s_hbm
         olds.append(pltpu.make_async_copy(src.at[at, mine_rows[part]], old.at[m, part], lsem.at[PAIR * n_col + j]))
-    for c in theirs[:n_slot] + mine:
+    for c in theirs[:n_slot] + mine[np_in:] + mine[:np_in]:
         c.start()
     entry_barrier()
     def transpose(src, i, par):
         for kc in range(ns // PW):
             agt[i * (ns // PW) + kc, pl.ds(pl.multiple_of(par * BW, BW), BW), :] = src[kc * PW:kc * PW + PW, :].T
-    for i in range(n_col):
-        theirs[i].wait()
-        transpose(flip.at[i % n_slot], i, 1 - p)
-        if i + n_slot < n_col:
-            theirs[i + n_slot].start()
+    def ready(zs):
+        for z in zs:
+            i = turns[z]
+            theirs[z].wait()
+            transpose(flip.at[z % n_slot], i, 1 - p)
+            if z + n_slot < n_col:
+                theirs[z + n_slot].start()
+        for z in zs:
+            mine[turns[z]].wait()
+            transpose(mine_at(turns[z]), turns[z], p)
+    ready(range(np_out))
     for c in olds:
         c.start()
-    for i in range(n_col):
-        mine[i].wait()
-        transpose(mine_at(i), i, p)
 
     def gram(z, row0, lo, hi, starts, scale):
         n = len(starts)
@@ -386,7 +390,7 @@
                     keep(part).wait()
         return [start, lambda: fold(0), lambda: gain(0), lambda: fold(1), lambda: gain(1), done, widen, relay_wide] + ([wide] if late else [near_go, relay, whole]), settle
     rounds = [round_steps(k) for k in range(len(cuts) - 1)]
-    chunks = [lambda: grams(1, (0,)), lambda: (grams(1, (2,)), grams(0, range(0, np_in, PAIR))), lambda: (grams(1, range(EARLY, np_out, PAIR)), grads((0,))),
+    chunks = [lambda: grams(1, (0,)), lambda: (grams(1, (2,)), ready(range(np_out, n_col)), grams(0, range(0, np_in, PAIR))), lambda: (grams(1, range(EARLY, np_out, PAIR)), grads((0,))),
         lambda: (grads(range(2, np_out, PAIR)), [c.wait() for c in olds])]
     for k, z in order:
         todo = chunks if k < 0 else rounds[k][0]
@@ -417,7 +421,7 @@
             *slab(HALF), *slab(BW), *slab(MB), *slab(ROWS), V(3, nm, 3, SUBL, BW), D(PAIR * n_col + n_old), *[D(69 * (len(cuts) - 1))] * 2, D(3, len(cuts) - 1, 3)],
         compiler_params=pltpu.CompilerParams(collective_id=0, has_side_effects=True, vmem_limit_bytes=67043328), name="front")(a_loc, g_loc, s_blk, a_blk)
 
-def solve_kernel(np_in, np_out, n_dp, damp, cuts, early, quarter, fin, full, tmat, mat, linv, inv_all, lsp, xw, zin, pack, ssem, rsem, psem, osem):
+def solve_kernel(np_in, np_out, n_dp, damp, cuts, early, quarter, fin, full, tmat, mat, linv, inv_all, lsp, lspt, xw, zin, pack, ssem, rsem, psem, osem):
     p = lax.axis_index('mp')
     d = lax.axis_index('dp')
     n_own = np_in * BW // n_dp
@@ -475,7 +479,7 @@
     def update(i, k, q, ok):
         slot = lax.rem(q, PAIR)
         at = ok * i + (1 - ok) * np_out
-        prod = stack_dot(pieces(lsp, ok * ltile(i, k)), pieces(lsp, ok * ltile(q, k)), NT)
+        prod = stack_dot(pieces(lsp, ok * ltile(i, k)), pieces(lspt, ok * ltile(q, k)), NN)
         tmat[slot, at] = tmat[slot, at] - prod
 
     def task(s, q):
@@ -513,14 +517,18 @@
             inv1 = linv[...]
             inv_all[q, BW:, BW:] = inv1
             inv_all[q, BW:, :BW] = -dot6(split3(inv1), split3(inv_all[q, BW:, :BW]), NN)
-            invs = split3(inv_all[q])
+            invs = split3(inv_all[q].T)
             def below(s):
                 i = q + 1 + PAIR * s
                 ok = (i + 1 < npan).astype(jnp.int32)
                 both = jnp.concatenate([tmat[slot, i], tmat[slot, ok * (i + 1) + (1 - ok) * np_out]], 0)
-                for z, v in enumerate(split3(stack_dot(split3(both), invs, NT))):
-                    lsp[z, ltile(i, q)] = v[:PW]
-                    lsp[z, ok * ltile(i + 1, q) + (1 - ok) * lsp_spare] = v[PW:]
+                low = stack_dot(split3(both), invs, NN)
+                at = ltile(i, q), ok * ltile(i + 1, q) + (1 - ok) * lsp_spare
+                for u in HALVES:
+                    one = low[u * PW:(u + 1) * PW]
+                    for ref, v in ((lsp, one), (lspt, one.T)):
+                        for z, piece in enumerate(split3(v)):
+                            ref[z, at[u]] = piece
             upto(lax.div(npan - q, PAIR), below)
         @pl.when((h == 1) & (q < npan - 1))
         def _():
@@ -560,25 +568,25 @@
             xw[q] = zin[1, q]
         upto(np_out, cp)
 
-    def spread(x, lo, hi, tile, dims):
+    def spread(x, lo, hi, tile, ref):
         xs = split3(x)
         def some(i):
             for u in range(RING):
                 j = lo + RING * i + u
                 ok = (j < hi).astype(jnp.int32)
                 at = ok * j + (1 - ok) * np_out
-                xw[at] = xw[at] - stack_dot(xs, pieces(lsp, ok * tile(j)), dims)
+                xw[at] = xw[at] - stack_dot(xs, pieces(ref, ok * tile(j)), NN)
         upto(lax.div(hi - lo + RING - 1, RING), some)
     def fwd(q):
         y = stack_dot(split3(xw[q]), split3(inv_all[q]), NT)
         xw[q] = y
-        spread(y, q + 1, npan, lambda j: ltile(j, q), NT)
+        spread(y, q + 1, npan, lambda j: ltile(j, q), lspt)
     upto(npan, fwd)
     def back(s):
         q = npan - 1 - s
         x = stack_dot(split3(xw[q]), split3(inv_all[q]), NN)
         xw[q] = x
-        spread(x, 0, q, lambda j: ltile(q, j), NN)
+        spread(x, 0, q, lambda j: ltile(q, j), lsp)
     upto(npan, back)
 
     xcopy = remote(pack.at[1], pack.at[0], *both_ends(psem, 2), partner())
@@ -662,7 +670,7 @@
     f32 = lambda *s: jax.ShapeDtypeStruct(s, F32)
     return pl.pallas_call(functools.partial(solve_kernel, np_in, np_out, n_dp, damp, cuts),
         out_shape=f32(3, RING, RING, RING, n_t, SUBL, BW), in_specs=[hb, vb], out_specs=vb,
-        scratch_shapes=[V(2, cuts[-1], 3, RING, BW, BW), V(2, np_out + 1, PW, PW), V(BW, BW), V(BW, BW), V(np_out, PW, PW), pltpu.VMEM((3, n_tile, PW, PW), BF), V(np_out + 1, MB, PW),
+        scratch_shapes=[V(2, cuts[-1], 3, RING, BW, BW), V(2, np_out + 1, PW, PW), V(BW, BW), V(BW, BW), V(np_out, PW, PW), *[pltpu.VMEM((3, n_tile, PW, PW), BF)] * 2, V(np_out + 1, MB, PW),
             V(2, np_out, MB, PW), V(2, n_row * SUBL, PW), D(54), D(54), D(2, 3), D(2, 2)],
         compiler_params=pltpu.CompilerParams(collective_id=1, has_side_effects=True, vmem_limit_bytes=67043328), name="solve")(early, quarter)
 

time: 251 us -> 249 us (level)
  no operation moved by 1% of the time
where the time goes in v6:
time: 249 us
  Pallas kernels  248 us (100%)
    pallas_call x1, Pallas kernels, solve(): pl.pallas_call(functools.partial(solve_kernel, np_in, np_out, n_dp, damp,...  123 us
    pallas_call x1, Pallas kernels, front(): pl.pallas_call(functools.partial(front_kernel, np_in, np_out, n_dp, cuts,...  110 us
    pallas_call x1, Pallas kernels, finish(): pl.pallas_call(functools.partial(finish_kernel, np_in, np_out, np_in * BW...  14.9 us

profile of v6, /device:TPU:0, one launch (start us, length us, event | category | flops | bytes accessed | tf_op | source)
XLA Modules:
  0.0 249.0 jit_solution(9564562018577396095)
XLA Ops:
  0.6 110.0 %front.1 = (f32[2,9,3,4,128,128]{5,4,3,2,1,0:T(8,128)}, f32[2,4,3,128,128]{4,3,2,1,0:T(8,128)}) custom-call(bf16[2048,768]{1,0:T(8,128)(2,1)} %a_hbm.1, bf16[2048,2304]{1,0:T(8,128)(2,1)} %g_hbm.1, f32[162,128,128]{2,1,0:T(8,128)} %bitcast.16, f32[18,128,128]{2,1,0:T(8,128)} %bitcast.18), custom_call_target="tpu_custom_call" | custom-call | tf_op jit(solution)/shard_map/front/pallas_call | solution.py:417
  110.7 123.3 %solve.1.fin = f32[3,4,4,4,5,8,128]{6,5,4,3,2,1,0:T(8,128)} custom-call(f32[2,9,3,4,128,128]{5,4,3,2,1,0:T(8,128)} %get-tuple-element.8.early, f32[2,4,3,128,128]{4,3,2,1,0:T(8,128)} %get-tuple-element.9.quarter), custom_call_target="tpu_custom_call" | custom-call | tf_op jit(solution)/shard_map/solve/pallas_call | solution.py:671
  233.9 14.9 %outputs.1 = (f32[3,2304,128]{2,1,0:T(8,128)}, f32[3,3,2,128,128]{4,3,2,1,0:T(8,128)}, f32[9,9,2,128,128]{4,3,2,1,0:T(8,128)}) custom-call(f32[3,2304,128]{2,1,0:T(8,128)} %bitcast.17, f32[2,54,2,128,128]{4,3,2,1,0:T(8,128)} %bitcast.15, f32[3,4,4,4,5,8,128]{6,5,4,3,2,1,0:T(8,128)} %solve.1.fin), custom_call_target="tpu_custom_call" | custom-call | tf_op jit(solution)/shard_map/outputs/pallas_call | solution.py:741

commit v7 on v6

--- a/solution.py
+++ b/solution.py
@@ -44,6 +44,12 @@
     sub = lax.broadcasted_iota(jnp.int32, (MB, BW), 0)
     odd = lax.rem(sub, PAIR)
     zero = lane.astype(F32) * 0.0
+    ri = lax.broadcasted_iota(jnp.int32, (BW, BW), 0)
+    ci = lax.broadcasted_iota(jnp.int32, (BW, BW), 1)
+    whole = mat[...]
+    diag = jnp.where(ci == ri, whole, 0.0)
+    down, along_row = lax.rsqrt(jnp.sum(diag, axis=1, keepdims=True)), lax.rsqrt(jnp.sum(diag, axis=0, keepdims=True))
+    mat[...] = whole * down * along_row
     rows = mat[:MB]
     for t in range(BW // MB):
         k = t * MB
@@ -97,11 +103,9 @@
         if more:
             terms = [mult[j] * bc(w[j:j + 1]) for j in range(MB)]
             while len(terms) > 1:
-                terms = [x + y for x, y in zip(terms[::2], terms[1::2])]
+                terms = [x + y for x, y in zip(terms[::PAIR], terms[1::PAIR])]
             rows = jnp.where(inside, 0.0, near) - terms[0]
-    ri = lax.broadcasted_iota(jnp.int32, (BW, BW), 0)
-    ci = lax.broadcasted_iota(jnp.int32, (BW, BW), 1)
-    linv[...] = jnp.where(ci <= ri, linv[...], 0.0)
+    linv[...] = jnp.where(ci <= ri, linv[...], 0.0) * along_row
 
 
 def dot6(a, b, dims):

time: 249 us -> 253 us (1.016)
  Pallas kernels: 248 us -> 252 us
    pallas_call x1, Pallas kernels: 123 us -> 127 us  [solve(): pl.pallas_call(functools.partial(solve_kernel, np_in, np_out, n_dp, damp,...]
where the time goes in v7:
time: 253 us; the launch traced here: 252 us
  Pallas kernels  252 us (100%)
    pallas_call x1, Pallas kernels, solve(): pl.pallas_call(functools.partial(solve_kernel, np_in, np_out, n_dp, damp,...  127 us
    pallas_call x1, Pallas kernels, front(): pl.pallas_call(functools.partial(front_kernel, np_in, np_out, n_dp, cuts,...  110 us
    pallas_call x1, Pallas kernels, finish(): pl.pallas_call(functools.partial(finish_kernel, np_in, np_out, np_in * BW...  14.9 us

profile of v7, /device:TPU:0, one launch (start us, length us, event | category | flops | bytes accessed | tf_op | source)
XLA Modules:
  0.0 252.4 jit_solution(2746762977027191277)
XLA Ops:
  0.6 110.0 %front.1 = (f32[2,9,3,4,128,128]{5,4,3,2,1,0:T(8,128)}, f32[2,4,3,128,128]{4,3,2,1,0:T(8,128)}) custom-call(bf16[2048,768]{1,0:T(8,128)(2,1)} %a_hbm.1, bf16[2048,2304]{1,0:T(8,128)(2,1)} %g_hbm.1, f32[162,128,128]{2,1,0:T(8,128)} %bitcast.16, f32[18,128,128]{2,1,0:T(8,128)} %bitcast.18), custom_call_target="tpu_custom_call" | custom-call | tf_op jit(solution)/shard_map/front/pallas_call | solution.py:421
  110.7 126.6 %solve.1.fin = f32[3,4,4,4,5,8,128]{6,5,4,3,2,1,0:T(8,128)} custom-call(f32[2,9,3,4,128,128]{5,4,3,2,1,0:T(8,128)} %get-tuple-element.8.early, f32[2,4,3,128,128]{4,3,2,1,0:T(8,128)} %get-tuple-element.9.quarter), custom_call_target="tpu_custom_call" | custom-call | tf_op jit(solution)/shard_map/solve/pallas_call | solution.py:675
  237.3 14.9 %outputs.1 = (f32[3,2304,128]{2,1,0:T(8,128)}, f32[3,3,2,128,128]{4,3,2,1,0:T(8,128)}, f32[9,9,2,128,128]{4,3,2,1,0:T(8,128)}) custom-call(f32[3,2304,128]{2,1,0:T(8,128)} %bitcast.17, f32[2,54,2,128,128]{4,3,2,1,0:T(8,128)} %bitcast.15, f32[3,4,4,4,5,8,128]{6,5,4,3,2,1,0:T(8,128)} %solve.1.fin), custom_call_target="tpu_custom_call" | custom-call | tf_op jit(solution)/shard_map/outputs/pallas_call | solution.py:745

commit v8 on v7

--- a/solution.py
+++ b/solution.py
@@ -495,14 +495,14 @@
 
     load(0)
 
-    def panel(k):
+    def panel(k, *work):
         q = lax.div(k, PAIR)
         h = lax.rem(k, PAIR)
         slot = lax.rem(q, PAIR)
         @pl.when(h == 0)
         def _():
             mat[...] = tmat[slot, q, :BW, :BW]
-        factor_block(mat, linv, lambda t: task(h * SUBL + t, q))
+        factor_block(mat, linv, lambda t: [fn(h * SUBL + t, q) for fn in work])
         @pl.when(h == 0)
         def _():
             inv0 = linv[...]
@@ -547,7 +547,7 @@
     @pl.when(p == 0)
     def _():
         wait_for(then)
-    each(1, PAIR * npan, panel)
+    each(1, PAIR * npan, lambda k: panel(k, task))
     @pl.when(p == 1)
     def _():
         for z, part, par in every:

time: 253 us -> 252 us (level)
  no operation moved by 1% of the time
where the time goes in v8:
time: 252 us
  Pallas kernels  251 us (100%)
    pallas_call x1, Pallas kernels, solve(): pl.pallas_call(functools.partial(solve_kernel, np_in, np_out, n_dp, damp,...  126 us
    pallas_call x1, Pallas kernels, front(): pl.pallas_call(functools.partial(front_kernel, np_in, np_out, n_dp, cuts,...  110 us
    pallas_call x1, Pallas kernels, finish(): pl.pallas_call(functools.partial(finish_kernel, np_in, np_out, np_in * BW...  14.9 us

profile of v8, /device:TPU:0, one launch (start us, length us, event | category | flops | bytes accessed | tf_op | source)
XLA Modules:
  0.0 252.2 jit_solution(8427275430300481169)
XLA Ops:
  0.6 110.0 %front.1 = (f32[2,9,3,4,128,128]{5,4,3,2,1,0:T(8,128)}, f32[2,4,3,128,128]{4,3,2,1,0:T(8,128)}) custom-call(bf16[2048,768]{1,0:T(8,128)(2,1)} %a_hbm.1, bf16[2048,2304]{1,0:T(8,128)(2,1)} %g_hbm.1, f32[162,128,128]{2,1,0:T(8,128)} %bitcast.16, f32[18,128,128]{2,1,0:T(8,128)} %bitcast.18), custom_call_target="tpu_custom_call" | custom-call | tf_op jit(solution)/shard_map/front/pallas_call | solution.py:421
  110.7 126.5 %solve.1.fin = f32[3,4,4,4,5,8,128]{6,5,4,3,2,1,0:T(8,128)} custom-call(f32[2,9,3,4,128,128]{5,4,3,2,1,0:T(8,128)} %get-tuple-element.8.early, f32[2,4,3,128,128]{4,3,2,1,0:T(8,128)} %get-tuple-element.9.quarter), custom_call_target="tpu_custom_call" | custom-call | tf_op jit(solution)/shard_map/solve/pallas_call | solution.py:675
  237.2 14.9 %outputs.1 = (f32[3,2304,128]{2,1,0:T(8,128)}, f32[3,3,2,128,128]{4,3,2,1,0:T(8,128)}, f32[9,9,2,128,128]{4,3,2,1,0:T(8,128)}) custom-call(f32[3,2304,128]{2,1,0:T(8,128)} %bitcast.17, f32[2,54,2,128,128]{4,3,2,1,0:T(8,128)} %bitcast.15, f32[3,4,4,4,5,8,128]{6,5,4,3,2,1,0:T(8,128)} %solve.1.fin), custom_call_target="tpu_custom_call" | custom-call | tf_op jit(solution)/shard_map/outputs/pallas_call | solution.py:745
